TPU v7x, 256 devices: a whole 4x4x8 slice. The times are simulated.
256 devices in a mesh: samp: 32 (over y, z_hi, x), tile: 8 (over z_lo, core).
Axes of the slice: x: 4, y: 4, z: 8 (z_hi: 2, z_lo: 4; z = z_hi * 4 + z_lo), core: 2. Of those that a mesh axis runs over, the one named last changes fastest.
Arguments:
- traits: bfloat16 [32768, 1024], P('samp'), may hold values from -300 to 300
- covariates: bfloat16 [32768, 32], P('samp'), may hold values from -6 to 6
- genotypes: int32 [32768, 2048], P('samp', 'tile'), may hold values from 0 to 2
- shuffles: int32 [6, 32768], P(None, 'samp'), may hold values from 0 to 32767, as said below
Outputs:
- observed: float32 [1024, 2048], P('samp', 'tile')
- perm_max: float32 [6, 1024], P(None, 'samp')
Inputs may be any that keep to these rules, and one draw needn't show every extreme that they name: Row p of shuffles maps each aligned block of 1024 samples one to one onto the same block's samples.
All inputs are finite; a program needn't handle non-finite values.
Results may differ from a plain program's by a relative error of at most 0.0045.
Values sent between devices are 32-bit elements; how exact they have to be, the bound alone decides.
No kernel may reach another device: no remote copies, remote signals or barrier semaphores. Data moves between devices by JAX's collectives and lax.ppermute only.
A program may use at most 64 MiB of HBM per device.

v0:
```python
import math

import jax
import jax.numpy as jnp
from jax import lax
from jax.experimental import pallas as pl
from jax.experimental.pallas import tpu as pltpu
from jax.sharding import Mesh, PartitionSpec as P


C = 32
EPSILON = 1e-05

ROWS = 1024
E = 1024
V = 256
PERMS = 6
HALF = E // 2
COLS = V + HALF + 128
BLOCKS = (V + HALF) // 128
SPLIT = (3, 2, 1)
SQUARES = 16
CHUNK = (PERMS + 1) * V // 2
LANES = CHUNK // 128
F32 = jnp.float32
BF16 = jnp.bfloat16


def dot(a, b):
    return jnp.dot(a, b, preferred_element_type=F32)


def call(kernel, outs, *args, grid_spec=None, in_specs=None, flops=0, room=4):
    shapes = [jax.ShapeDtypeStruct(s, d) for s, d in outs]
    single = len(shapes) == 1
    extra = {} if grid_spec is None else {"grid_spec": grid_spec}
    if in_specs is not None:
        extra["in_specs"] = in_specs
    nbytes = sum(math.prod(s) * jnp.dtype(d).itemsize for s, d in outs)
    out = pl.pallas_call(
        kernel,
        out_shape=shapes[0] if single else shapes,
        cost_estimate=pl.CostEstimate(flops=flops, bytes_accessed=nbytes, transcendentals=0),
        compiler_params=pltpu.CompilerParams(vmem_limit_bytes=room << 20),
        **extra,
    )(*args)
    return out if single else list(out)


def shifts(axis, k):
    n = lax.axis_size(axis)
    return [(i, (i + k) % n) for i in range(n)]


def shift(value, axis, k):
    return lax.ppermute(value, axis, shifts(axis, k))


def front_kernel(core_ref, traits_ref, cov_ref, geno_ref, pay_ref, xt_ref, dx_ref):
    del core_ref
    row = lax.broadcasted_iota(jnp.int32, (128 - C, ROWS), 0)
    tail = jnp.where(row == 0, 1.0, 0.0).astype(F32)
    design_t = jnp.concatenate([cov_ref[...].astype(F32), tail], axis=0)
    dosage = geno_ref[...].astype(F32).astype(BF16)
    design_b = jnp.transpose(design_t).astype(BF16)
    dx_ref[:, :V] = dosage
    dx_ref[:, V:] = design_b
    xt = design_t[:48].astype(BF16)
    xt_ref[...] = xt
    pay_ref[BLOCKS * C :, :] = dot(xt, design_b)[:40]
    for at, part in ((0, dot(xt, dosage)), (V // 128, dot(xt, traits_ref[...]))):
        for j in range(part.shape[1] // 128):
            block = part[:, j * 128 : (j + 1) * 128]
            pay_ref[(at + j) * C : (at + j + 1) * C, :] = block[:C]
            ones = BLOCKS * C + C + 1 + at + j
            pay_ref[ones : ones + 1, :] = block[C : C + 1]


def turn_kernel(traits_ref, out_ref):
    out_ref[...] = jnp.transpose(traits_ref[...])


def perm_kernel(base_ref, order_ref, dx_ref, after_ref, out_ref, token_ref):
    del after_ref
    order = order_ref[0] - base_ref[0]
    for at in range(0, ROWS, 256):
        row = lax.broadcasted_iota(jnp.int32, (256, ROWS), 0) + at
        pick = jnp.where(row == order, 1.0, 0.0).astype(BF16)
        out_ref[0, at : at + 256, :] = dot(pick, dx_ref[...]).astype(BF16)
    token_ref[...] = jnp.zeros(token_ref.shape, F32)


def sum_kernel(a, b, c, d, token, out):
    del token
    out[...] = (a[...] + c[...]) + (b[...] + d[...])


def solve_kernel(own_ref, far_ref, out_ref):
    total = own_ref[...] + far_ref[...]
    gram = total[BLOCKS * C :]
    blocks = [total[j * C : (j + 1) * C] for j in range(BLOCKS)]
    ones = [gram[C + 1 + j : C + 2 + j] for j in range(BLOCKS)]
    row_id = lax.broadcasted_iota(jnp.int32, (40, COLS), 0)
    top = jnp.concatenate([*blocks, gram[:C]], axis=1)
    low = jnp.concatenate([*ones, gram[C : C + 1]], axis=1)
    m = jnp.concatenate([top, jnp.broadcast_to(low, (8, COLS))], axis=0)
    for k in range(C + 1):
        at = V + HALF + k
        col = m[:, at : at + 1]
        row = m[k : k + 1, :] / m[k : k + 1, at : at + 1]
        m = jnp.where(row_id == k, row, m - col * row)
    out_ref[...] = jnp.where(row_id[:, : V + HALF] <= C, m[:, : V + HALF], 0.0)


def resid_kernel(core_ref, own_ref, far_ref, yt_ref, xt_ref, dx_ref, dxp1_ref, dxp2_ref, dxp3_ref, rt_ref, g1_ref, g2_ref, ss_ref):
    core = core_ref[0]
    xt = xt_ref[...]
    zeros = jnp.zeros((8, E), F32)
    mine = own_ref[:, V:]
    other = far_ref[...]
    first = jnp.where(core == 0, mine, other)
    second = jnp.where(core == 0, other, mine)
    coef = jnp.concatenate([jnp.concatenate([first, second], axis=1), zeros], axis=0)
    coef_t = jnp.transpose(coef).astype(BF16)
    ss_parts = []
    for at in range(0, E, 128):
        res = yt_ref[at : at + 128, :].astype(F32) - dot(coef_t[at : at + 128], xt)
        rt_ref[at : at + 128, :] = res.astype(BF16)
        sq = res * res
        lanes = sq[:, :128]
        for b in range(128, ROWS, 128):
            lanes = lanes + sq[:, b : b + 128]
        ss_parts.append(jnp.sum(jnp.transpose(lanes), axis=0, keepdims=True))
    gamma = jnp.concatenate([own_ref[:, :V], jnp.zeros((88, V), F32)], axis=0).astype(BF16)
    res_g = dx_ref[:, :V].astype(F32) - dot(dx_ref[:, V:], gamma)
    g1_ref[:, :V] = res_g.astype(BF16)
    ss_v = jnp.sum(res_g * res_g, axis=0, keepdims=True)
    places = [(ref, q) for ref in (dxp1_ref, dxp2_ref, dxp3_ref) for q in range(ref.shape[0])]
    for p, (src, q) in enumerate(places):
        g = (src[q, :, :V].astype(F32) - dot(src[q, :, V:], gamma)).astype(BF16)
        at = (p + 1) * V
        if at + V <= CHUNK:
            g1_ref[:, at : at + V] = g
        elif at >= CHUNK:
            g2_ref[:, at - CHUNK : at - CHUNK + V] = g
        else:
            g1_ref[:, at:] = g[:, : CHUNK - at]
            g2_ref[:, : at + V - CHUNK] = g[:, CHUNK - at :]
    ss_ref[...] = jnp.concatenate(
        [*ss_parts, ss_v[:, :128], ss_v[:, 128:], jnp.zeros((SQUARES - 10, 128), F32)], axis=0
    )


def lanes_to_rows(out_ref, value):
    rows = value.shape[0]
    for j in range(LANES):
        out_ref[j * rows : (j + 1) * rows, :] = value[:, j * 128 : (j + 1) * 128]


def cross1_kernel(to_ref, rt_ref, g_ref, ss_ref, after_ref, low_ref, high_ref):
    del to_ref, after_ref
    lanes_to_rows(low_ref, dot(rt_ref[:, 0, 0].reshape(128, ROWS), g_ref[...]))
    low_ref[LANES * 128 :, :] = ss_ref[...]
    lanes_to_rows(high_ref, dot(rt_ref[:, 1, 0].reshape(128, ROWS), g_ref[...]))


def cross2_kernel(to_ref, rt_ref, g_ref, after_ref, low_ref, high_ref):
    del to_ref, after_ref
    lanes_to_rows(low_ref, dot(rt_ref[:128], g_ref[...]))
    lanes_to_rows(high_ref, dot(rt_ref[128:], g_ref[...]))


def relay_kernel(a, b, after, out):
    del after
    out[...] = a[...] + b[...]


def mid_kernel(at_ref, low, low_near, low_far, high, high_near, high_far, *outs):
    me = at_ref[0]
    for k in range(4):
        for j in range(LANES):
            rows = pl.ds(pl.multiple_of(j * 128 + ((me + k) % 4) * 32, 32), 32)
            outs[k][j * 64 : j * 64 + 32, :] = low[rows, :] + (low_near[rows, :] + low_far[rows, :])
            outs[k][j * 64 + 32 : j * 64 + 64, :] = high[rows, :] + (high_near[rows, :] + high_far[rows, :])
        if outs[k].shape[0] > LANES * 64:
            rows = pl.ds(LANES * 128, SQUARES)
            outs[k][LANES * 64 :, :] = low[rows, :] + (low_near[rows, :] + low_far[rows, :])


def last_kernel(at_ref, a, b, c, d, keep, send):
    z = at_ref[0]
    for out, half in ((keep, z), (send, 1 - z)):
        for j in range(LANES):
            rows = pl.ds(pl.multiple_of(j * 64 + half * 32, 32), 32)
            out[j * 32 : (j + 1) * 32, :] = (a[rows, :] + c[rows, :]) + (b[rows, :] + d[rows, :])
        if out.shape[0] > LANES * 32:
            rows = pl.ds(LANES * 64, SQUARES)
            out[LANES * 32 :, :] = (a[rows, :] + c[rows, :]) + (b[rows, :] + d[rows, :])


def score_kernel(at_ref, keep1, got1, keep2, got2, obs_ref, peak_ref):
    samples = 32 * ROWS
    factor = math.sqrt(samples - C - 2) / samples
    first = keep1[...] + got1[...]
    second = keep2[...] + got2[...]
    sums = first[LANES * 32 :]
    scales = lax.rsqrt(sums / samples + EPSILON)
    place = lax.broadcasted_iota(jnp.int32, (SQUARES, 128), 0)
    lane = lax.broadcasted_iota(jnp.int32, (32, 128), 1)
    row = lax.broadcasted_iota(jnp.int32, (32, 128), 0)
    scale_e = jnp.sum(jnp.where(place == at_ref[0] // 4, scales, 0.0), axis=0, keepdims=True)
    own = jnp.where(lane == row + (at_ref[0] % 4) * 32, scale_e, 0.0)
    own_scale = jnp.sum(own, axis=1, keepdims=True)
    scale_v = jnp.concatenate([scales[8:9], scales[9:10]], axis=1)
    blocks = [part[j * 32 : (j + 1) * 32] for part in (first, second) for j in range(LANES)]

    def scores(p):
        cross = jnp.concatenate([blocks[2 * p], blocks[2 * p + 1]], axis=1)
        return cross * own_scale * scale_v * factor

    obs_ref[...] = scores(0)
    peaks = jnp.zeros((32, 128), F32)
    for p in range(PERMS):
        peaks = jnp.where(lane == p, jnp.max(jnp.abs(scores(p + 1)), axis=1, keepdims=True), peaks)
    peak_ref[...] = peaks


def peak_kernel(a, b, c, d, out_ref):
    best = jnp.maximum(jnp.maximum(a[...], b[...]), jnp.maximum(c[...], d[...]))
    full = jnp.concatenate([best, jnp.zeros((96, 128), F32)], axis=0)
    out_ref[...] = jnp.transpose(full)[:PERMS, :32]


def scalar_spec(n_in, n_out, grid=(1,)):
    whole = pl.BlockSpec(memory_space=pltpu.VMEM)
    return pltpu.PrefetchScalarGridSpec(
        num_scalar_prefetch=1,
        grid=grid,
        in_specs=[whole] * n_in,
        out_specs=[whole] * n_out,
    )


def in_hbm(value):
    return pltpu.with_memory_space_constraint(value, pltpu.HBM)


def index(axis):
    return jnp.reshape(lax.axis_index(axis), (1,)).astype(jnp.int32)


def program(traits, covariates, genotypes, shuffles):
    core, x, y, zh = index("core"), index("x"), index("y"), index("zh")
    samp = (y * 2 + zh) * 4 + x
    anywhere = pl.BlockSpec(memory_space=pl.ANY)

    pay, xt, dx = call(
        front_kernel,
        [((BLOCKS * C + 40, 128), F32), ((48, ROWS), BF16), ((ROWS, V + 128), BF16)],
        core, in_hbm(traits), in_hbm(covariates.T), in_hbm(genotypes),
        grid_spec=pltpu.PrefetchScalarGridSpec(
            num_scalar_prefetch=1,
            grid=(1,),
            in_specs=[
                pl.BlockSpec((ROWS, HALF), lambda i, c: (0, c[0])),
                pl.BlockSpec((C, ROWS), lambda i, c: (0, 0)),
                pl.BlockSpec((ROWS, V), lambda i, c: (0, 0)),
            ],
            out_specs=[
                pl.BlockSpec((BLOCKS * C + 40, 128), lambda i, c: (0, 0)),
                pl.BlockSpec((48, ROWS), lambda i, c: (0, 0)),
                pl.BlockSpec((ROWS, V + 128), lambda i, c: (0, 0)),
            ],
        ),
        flops=2 * 128 * ROWS * COLS,
        room=14,
    )

    orders = shuffles.reshape(PERMS, 1, ROWS)

    def permuted(first, count, after):
        return call(
            perm_kernel, [((count, ROWS, V + 128), BF16), ((8, 128), F32)],
            samp * ROWS, orders, dx, after,
            grid_spec=pltpu.PrefetchScalarGridSpec(
                num_scalar_prefetch=1,
                grid=(count,),
                in_specs=[
                    pl.BlockSpec((1, 1, ROWS), lambda i, b: (i + first, 0, 0)),
                    pl.BlockSpec((ROWS, V + 128), lambda i, b: (0, 0)),
                    anywhere,
                ],
                out_specs=[
                    pl.BlockSpec((1, ROWS, V + 128), lambda i, b: (i, 0, 0)),
                    pl.BlockSpec((8, 128), lambda i, b: (0, 0)),
                ],
            ),
            flops=2 * count * ROWS * ROWS * (V + 128),
            room=8,
        )

    def summed(value, axis, token):
        parts = [value] + [shift(value, axis, k) for k in (1, 2, 3)]
        return call(sum_kernel, [(value.shape, F32)], *parts, token, room=2)

    turned, at = [], 0
    for axis, count in (("x", SPLIT[0]), ("y", SPLIT[1])):
        rows, token = permuted(at, count, pay)
        pay = summed(pay, axis, token)
        turned.append(rows)
        at += count
    turned.append(permuted(at, SPLIT[2], pay)[0])
    yt = call(
        turn_kernel, [((E, ROWS), BF16)], traits,
        grid_spec=pl.GridSpec(
            grid=(4,),
            in_specs=[pl.BlockSpec((ROWS, 256), lambda i: (0, i))],
            out_specs=pl.BlockSpec((256, ROWS), lambda i: (i, 0)),
        ),
        flops=10**9,
        room=6,
    )
    coef = call(solve_kernel, [((40, V + HALF), F32)], pay, shift(pay, "zh", 1), room=4, flops=10**8)
    far = shift(coef[:, V:], "core", 1)
    rt, g1, g2, ss = call(
        resid_kernel,
        [((E, ROWS), BF16), ((ROWS, CHUNK), BF16), ((ROWS, CHUNK), BF16), ((SQUARES, 128), F32)],
        core, coef, far, yt, xt, dx, *turned,
        grid_spec=scalar_spec(8, 4),
        flops=2 * 2 * ROWS * E * 128,
        room=24,
    )

    rt5 = rt.reshape(4, 2, 4, 32, ROWS)
    g_spec = pl.BlockSpec((ROWS, CHUNK), lambda i, t: (0, 0))
    ss_spec = pl.BlockSpec((SQUARES, 128), lambda i, t: (0, 0))

    def cross(axis, k, after):
        onx = axis == "x"
        low = LANES * 128 + (SQUARES if onx else 0)
        return call(
            cross1_kernel if onx else cross2_kernel,
            [((low, 128), F32), ((LANES * 128, 128), F32)],
            ((x if onx else y) + k) % 4,
            *((rt5, g1, ss) if onx else (rt, g2)),
            after,
            grid_spec=pltpu.PrefetchScalarGridSpec(
                num_scalar_prefetch=1,
                grid=(1,),
                in_specs=[
                    *(
                        (pl.BlockSpec((4, 2, 1, 32, ROWS), lambda i, t: (0, 0, t[0], 0, 0)), g_spec, ss_spec)
                        if onx
                        else (pl.BlockSpec((256, ROWS), lambda i, t: (t[0], 0)), g_spec)
                    ),
                    anywhere,
                ],
                out_specs=[
                    pl.BlockSpec((low, 128), lambda i, t: (0, 0)),
                    pl.BlockSpec((LANES * 128, 128), lambda i, t: (0, 0)),
                ],
            ),
            flops=2 * 256 * ROWS * CHUNK,
            room=10,
        )

    part, got = {}, {}
    after = ss
    for k in (2, 1, 3, 0):
        for axis in ("x", "y"):
            part[axis, k] = cross(axis, k, after)
            after = part[axis, k][1]
            low, high = part[axis, k]
            if k == 2:
                got[axis, "low2"] = shift(low, axis, 1)
                got[axis, "high2"] = shift(high, axis, 3)
            elif k == 1:
                got[axis, "high"] = shift(high, axis, 1)
            elif k == 3:
                got[axis, "low"] = shift(low, axis, 3)
    parts = {}
    whole = pl.BlockSpec(memory_space=pltpu.VMEM)
    for axis in ("x", "y"):
        relayed = []
        for k, half, name in ((1, 0, "low2"), (3, 1, "high2")):
            mine = part[axis, k][half]
            relayed.append(
                call(
                    relay_kernel, [(mine.shape, F32)], mine, got[axis, name], after,
                    in_specs=[whole, whole, anywhere], room=2,
                )
            )
        got[axis, "lows"], got[axis, "highs"] = shift(relayed[0], axis, 1), shift(relayed[1], axis, 3)
    keeps = []
    for axis, other, at in (("x", "y", y), ("y", "x", x)):
        rows = LANES * 64 + (SQUARES if axis == "x" else 0)
        low, high = part[axis, 0]
        parts[axis] = call(
            mid_kernel, [((rows, 128), F32)] * 4, at,
            low, got[axis, "low"], got[axis, "lows"], high, got[axis, "high"], got[axis, "highs"],
            grid_spec=scalar_spec(6, 4), flops=10**7, room=4,
        )
        for k in (1, 2, 3):
            parts[axis][k] = shift(parts[axis][k], other, k)
    for axis in ("x", "y"):
        rows = LANES * 32 + (SQUARES if axis == "x" else 0)
        keep, send = call(
            last_kernel, [((rows, 128), F32)] * 2, zh, *parts[axis],
            grid_spec=scalar_spec(4, 2), flops=10**6, room=2,
        )
        keeps += [keep, shift(send, "zh", 1)]
    observed, peaks = call(
        score_kernel, [((32, V), F32), ((32, 128), F32)], samp, *keeps,
        grid_spec=scalar_spec(4, 2), flops=10**6, room=4,
    )
    peaks = jnp.maximum(peaks, shift(peaks, "core", 1))
    perm_max = call(
        peak_kernel, [((PERMS, 32), F32)], peaks, *(shift(peaks, "zl", k) for k in (1, 2, 3)),
        room=2,
    )
    return observed, perm_max


def solution(mesh):
    fine = Mesh(mesh.devices.reshape(4, 2, 4, 4, 2), ("y", "zh", "x", "zl", "core"))
    samp, tile = ("y", "zh", "x"), ("zl", "core")
    return jax.shard_map(
        program,
        mesh=fine,
        in_specs=(P(samp, None), P(samp, None), P(samp, tile), P(None, samp)),
        out_specs=(P(samp, tile), P(None, samp)),
        check_vma=False,
    )
```

profile of v0, /device:TPU:1, one launch (start us, length us, event | category | flops | bytes accessed | tf_op | source)
XLA Modules:
  0.0 128.3 jit_solution(12504179444256932521)
XLA Ops:
  0.6 2.2 %shard_map.59 = (f32[232,128]{1,0:T(8,128)S(1)}, bf16[48,1024]{1,0:T(8,128)(2,1)S(1)}, bf16[1024,384]{1,0:T(8,128)(2,1)S(1)}) custom-call(s32[1]{0:T(128)} %bitcast.3.core_ref, bf16[1024,1024]{1,0:T(8,128)(2,1)} %traits_ref.3, bf16[32,1024]{1,0:T(8,128)(2,1)} %bitcast.10, s32[1024,256]{1,0:T(8,128)} %geno_ref.1), custom_call_target="tpu_custom_call" | custom-call | flops 234881024 | bytes 1003520 | tf_op jit(solution)/shard_map/pallas_call | solution.py:40
  2.8 2.1 %collective-permute-start = (f32[232,128]{1,0:T(8,128)S(1)}, f32[232,128]{1,0:T(8,128)S(1)}, u32[]{:S(2)}, u32[]{:S(2)}) collective-permute-start(f32[232,128]{1,0:T(8,128)S(1)} %get-tuple-element.44.after_ref.a), channel_id=1, source_target_pairs={{0,8},{8,16},{16,24},{24,0},{1,9},{9,17},{17,25},{25,1},{2,10},{10... | collective-permute-start | bytes 356360 | tf_op jit(solution)/shard_map/ppermute | solution.py:56
  4.9 2.5 %collective-permute-start.1 = (f32[232,128]{1,0:T(8,128)S(1)}, f32[232,128]{1,0:T(8,128)S(1)}, u32[]{:S(2)}, u32[]{:S(2)}) collective-permute-start(f32[232,128]{1,0:T(8,128)S(1)} %get-tuple-element.44.after_ref.a), channel_id=1, source_target_pairs={{0,16},{8,24},{16,0},{24,8},{1,17},{9,25},{17,1},{25,9},{2,18},{10... | collective-permute-start | bytes 356360 | tf_op jit(solution)/shard_map/ppermute | solution.py:56
  7.4 1.2 collective-permute-start.2
  8.6 3.8 %shard_map.60 = (bf16[3,1024,384]{2,1,0:T(8,128)(2,1)S(1)}, f32[8,128]{1,0:T(8,128)S(1)}) custom-call(s32[1]{0:T(128)S(6)} %mul.13.base_ref, s32[6,1,1024]{2,1,0:T(1,128)S(1)} %reshape.42.order_ref, bf16[1024,384]{1,0:T(8,128)(2,1)S(1)} %get-tuple-element.45.dx_ref, f32[232,128]{1,0:T(8,128)S(1)} %get-tuple-element.44.after_ref.a), custom_call_target="tpu_custom_call" | custom-call | flops 2415919104 | bytes 2363392 | tf_op jit(solution)/shard_map/pallas_call | solution.py:40
  12.4 0.2 collective-permute-done.1.c
  12.6 1.4 %collective-permute-start.3 = (f32[232,128]{1,0:T(8,128)S(1)}, f32[232,128]{1,0:T(8,128)S(1)}, u32[]{:S(2)}, u32[]{:S(2)}) collective-permute-start(f32[232,128]{1,0:T(8,128)S(1)} %shard_map.61.after_ref.a), channel_id=1, source_target_pairs={{0,64},{64,128},{128,192},{192,0},{1,65},{65,129},{129,193},{193,1... | collective-permute-start | bytes 356360 | tf_op jit(solution)/shard_map/ppermute | solution.py:56
  14.0 2.6 %collective-permute-start.4 = (f32[232,128]{1,0:T(8,128)S(1)}, f32[232,128]{1,0:T(8,128)S(1)}, u32[]{:S(2)}, u32[]{:S(2)}) collective-permute-start(f32[232,128]{1,0:T(8,128)S(1)} %shard_map.61.after_ref.a), channel_id=1, source_target_pairs={{0,128},{64,192},{128,0},{192,64},{1,129},{65,193},{129,1},{193,65... | collective-permute-start | bytes 356360 | tf_op jit(solution)/shard_map/ppermute | solution.py:56
  16.6 1.1 collective-permute-start.5
  17.7 2.5 %shard_map.62 = (bf16[2,1024,384]{2,1,0:T(8,128)(2,1)S(1)}, f32[8,128]{1,0:T(8,128)S(1)}) custom-call(s32[1]{0:T(128)S(6)} %mul.13.base_ref, s32[6,1,1024]{2,1,0:T(1,128)S(1)} %reshape.42.order_ref, bf16[1024,384]{1,0:T(8,128)(2,1)S(1)} %get-tuple-element.45.dx_ref, f32[232,128]{1,0:T(8,128)S(1)} %shard_map.61.after_ref.a), custom_call_target="tpu_custom_call" | custom-call | flops 1610612736 | bytes 1576960 | tf_op jit(solution)/shard_map/pallas_call | solution.py:40
  20.2 0.4 collective-permute-done.4.c
  20.6 0.7 collective-permute-done.5.d
  21.4 7.4 %collective-permute-start.6 = (f32[232,128]{1,0:T(8,128)S(1)}, f32[232,128]{1,0:T(8,128)S(1)}, u32[]{:S(2)}, u32[]{:S(2)}) collective-permute-start(f32[232,128]{1,0:T(8,128)S(1)} %shard_map.63.own_ref.after_ref), channel_id=1, source_target_pairs={{0,32},{32,0},{1,33},{33,1},{2,34},{34,2},{3,35},{35,3},{4,36},{36... | collective-permute-start | bytes 356360 | tf_op jit(solution)/shard_map/ppermute | solution.py:56
  28.7 2.3 %collective-permute-done.6.far_ref = f32[232,128]{1,0:T(8,128)S(1)} collective-permute-done((f32[232,128]{1,0:T(8,128)S(1)}, f32[232,128]{1,0:T(8,128)S(1)}, u32[]{:S(2)}, u32[]{:S(2)}) %collective-permute-start.6) | collective-permute-done | bytes 118816 | tf_op jit(solution)/shard_map/ppermute | solution.py:56
  31.1 2.8 %shard_map.64.own_ref = f32[40,768]{1,0:T(8,128)S(1)} custom-call(f32[232,128]{1,0:T(8,128)S(1)} %shard_map.63.own_ref.after_ref, f32[232,128]{1,0:T(8,128)S(1)} %collective-permute-done.6.far_ref), custom_call_target="tpu_custom_call" | custom-call | flops 100000000 | bytes 122880 | tf_op jit(solution)/shard_map/pallas_call | solution.py:40
  33.9 3.5 %collective-permute-start.7 = (f32[40,512]{1,0:T(8,128)S(1)}, f32[40,512]{1,0:T(8,128)S(1)}, u32[]{:S(2)}, u32[]{:S(2)}) collective-permute-start(f32[40,512]{1,0:T(8,128)S(1)} %slice.4), channel_id=1, source_target_pairs={{0,1},{1,0},{2,3},{3,2},{4,5},{5,4},{6,7},{7,6},{8,9},{9,8},{10,11... | collective-permute-start | bytes 245768 | tf_op jit(solution)/shard_map/ppermute | solution.py:56
  37.4 1.1 shard_map.65.yt_ref
  38.5 1.8 %shard_map.66 = (bf16[1,1024,384]{2,1,0:T(8,128)(2,1)S(1)}, f32[8,128]{1,0:T(8,128)}) custom-call(s32[1]{0:T(128)S(6)} %mul.13.base_ref, s32[6,1,1024]{2,1,0:T(1,128)S(1)} %reshape.42.order_ref, bf16[1024,384]{1,0:T(8,128)(2,1)S(1)} %get-tuple-element.45.dx_ref, f32[232,128]{1,0:T(8,128)S(1)} %shard_map.63.own_ref.after_ref), custom_call_target="tpu_custom_call" | custom-call | flops 805306368 | bytes 790528 | tf_op jit(solution)/shard_map/pallas_call | solution.py:40
  40.3 1.8 %shard_map.67 = (bf16[1024,1024]{1,0:T(8,128)(2,1)S(1)}, bf16[1024,896]{1,0:T(8,128)(2,1)S(1)}, bf16[1024,896]{1,0:T(8,128)(2,1)S(1)}, f32[16,128]{1,0:T(8,128)S(1)}) custom-call(s32[1]{0:T(128)} %bitcast.3.core_ref, f32[40,768]{1,0:T(8,128)S(1)} %shard_map.64.own_ref, f32[40,512]{1,0:T(8,128)S(1)} %collective-permute-done.7.far_ref, ...), custom_call_target="tpu_custom_call" | custom-call | flops 536870912 | bytes 5775360 | tf_op jit(solution)/shard_map/pallas_call | solution.py:40
  42.1 0.7 shard_map.68
  42.8 2.7 %collective-permute-start.12 = (f32[896,128]{1,0:T(8,128)S(1)}, f32[896,128]{1,0:T(8,128)S(1)}, u32[]{:S(2)}, u32[]{:S(2)}) collective-permute-start(f32[896,128]{1,0:T(8,128)S(1)} %get-tuple-element.56.after_ref), channel_id=1, source_target_pairs={{0,24},{8,0},{16,8},{24,16},{1,25},{9,1},{17,9},{25,17},{2,26},{10... | collective-permute-start | bytes 1376264 | tf_op jit(solution)/shard_map/ppermute | solution.py:56
  45.6 0.7 shard_map.69
  46.3 2.5 %collective-permute-start.22 = (f32[896,128]{1,0:T(8,128)S(1)}, f32[896,128]{1,0:T(8,128)S(1)}, u32[]{:S(2)}, u32[]{:S(2)}) collective-permute-start(f32[896,128]{1,0:T(8,128)S(1)} %get-tuple-element.57.after_ref), channel_id=1, source_target_pairs={{0,192},{64,0},{128,64},{192,128},{1,193},{65,1},{129,65},{193,129... | collective-permute-start | bytes 1376264 | tf_op jit(solution)/shard_map/ppermute | solution.py:56
  48.8 0.7 shard_map.70
  49.6 0.1 collective-permute-start.11
  49.6 0.7 shard_map.71
  50.4 0.7 shard_map.72
  51.1 0.7 shard_map.73
  51.8 0.7 shard_map.74
  52.5 2.9 %collective-permute-done.12.b = f32[896,128]{1,0:T(8,128)S(1)} collective-permute-done((f32[896,128]{1,0:T(8,128)S(1)}, f32[896,128]{1,0:T(8,128)S(1)}, u32[]{:S(2)}, u32[]{:S(2)}) %collective-permute-start.12) | collective-permute-done | bytes 458784 | tf_op jit(solution)/shard_map/ppermute | solution.py:56
  55.4 3.4 %collective-permute-start.8 = (f32[912,128]{1,0:T(8,128)S(1)}, f32[912,128]{1,0:T(8,128)S(1)}, u32[]{:S(2)}, u32[]{:S(2)}) collective-permute-start(f32[912,128]{1,0:T(8,128)S(1)} %get-tuple-element.63), channel_id=1, source_target_pairs={{0,24},{8,0},{16,8},{24,16},{1,25},{9,1},{17,9},{25,17},{2,26},{10... | collective-permute-start | bytes 1400840 | tf_op jit(solution)/shard_map/ppermute | solution.py:56
  58.8 0.7 shard_map.75
  59.6 0.1 collective-permute-start.13
  59.8 1.5 %collective-permute-start.10 = (f32[912,128]{1,0:T(8,128)S(1)}, f32[912,128]{1,0:T(8,128)S(1)}, u32[]{:S(2)}, u32[]{:S(2)}) collective-permute-start(f32[912,128]{1,0:T(8,128)S(1)} %shard_map.76), channel_id=1, source_target_pairs={{0,8},{8,16},{16,24},{24,0},{1,9},{9,17},{17,25},{25,1},{2,10},{10... | collective-permute-start | bytes 1400840 | tf_op jit(solution)/shard_map/ppermute | solution.py:56
  61.3 0.2 collective-permute-done.19.b
  61.5 2.3 %collective-permute-start.18 = (f32[896,128]{1,0:T(8,128)S(1)}, f32[896,128]{1,0:T(8,128)S(1)}, u32[]{:S(2)}, u32[]{:S(2)}) collective-permute-start(f32[896,128]{1,0:T(8,128)S(1)} %get-tuple-element.75), channel_id=1, source_target_pairs={{0,192},{64,0},{128,64},{192,128},{1,193},{65,1},{129,65},{193,129... | collective-permute-start | bytes 1376264 | tf_op jit(solution)/shard_map/ppermute | solution.py:56
  63.8 4.8 %collective-permute-done.11.high_near = f32[896,128]{1,0:T(8,128)S(1)} collective-permute-done((f32[896,128]{1,0:T(8,128)S(1)}, f32[896,128]{1,0:T(8,128)S(1)}, u32[]{:S(2)}, u32[]{:S(2)}) %collective-permute-start.11) | collective-permute-done | bytes 458784 | tf_op jit(solution)/shard_map/ppermute | solution.py:56
  68.6 0.3 collective-permute-start.21
  68.9 2.5 %collective-permute-start.23 = (f32[896,128]{1,0:T(8,128)S(1)}, f32[896,128]{1,0:T(8,128)S(1)}, u32[]{:S(2)}, u32[]{:S(2)}) collective-permute-start(f32[896,128]{1,0:T(8,128)S(1)} %shard_map.81), channel_id=1, source_target_pairs={{0,192},{64,0},{128,64},{192,128},{1,193},{65,1},{129,65},{193,129... | collective-permute-start | bytes 1376264 | tf_op jit(solution)/shard_map/ppermute | solution.py:56
  71.4 6.4 %collective-permute-done.13.high_far = f32[896,128]{1,0:T(8,128)S(1)} collective-permute-done((f32[896,128]{1,0:T(8,128)S(1)}, f32[896,128]{1,0:T(8,128)S(1)}, u32[]{:S(2)}, u32[]{:S(2)}) %collective-permute-start.13) | collective-permute-done | bytes 458784 | tf_op jit(solution)/shard_map/ppermute | solution.py:56
  77.8 0.3 collective-permute-start.20
  78.1 0.5 collective-permute-done.10.low_far
  78.6 0.2 shard_map.78
  78.7 0.6 collective-permute-start.14
  79.4 3.1 %collective-permute-start.15 = (f32[464,128]{1,0:T(8,128)S(1)}, f32[464,128]{1,0:T(8,128)S(1)}, u32[]{:S(2)}, u32[]{:S(2)}) collective-permute-start(f32[464,128]{1,0:T(8,128)S(1)} %get-tuple-element.70), channel_id=1, source_target_pairs={{0,128},{64,192},{128,0},{192,64},{1,129},{65,193},{129,1},{193,65... | collective-permute-start | bytes 712712 | tf_op jit(solution)/shard_map/ppermute | solution.py:56
  82.5 1.3 %collective-permute-start.16 = (f32[464,128]{1,0:T(8,128)S(1)}, f32[464,128]{1,0:T(8,128)S(1)}, u32[]{:S(2)}, u32[]{:S(2)}) collective-permute-start(f32[464,128]{1,0:T(8,128)S(1)} %get-tuple-element.71), channel_id=1, source_target_pairs={{0,192},{64,0},{128,64},{192,128},{1,193},{65,1},{129,65},{193,129... | collective-permute-start | bytes 712712 | tf_op jit(solution)/shard_map/ppermute | solution.py:56
  83.8 6.7 %collective-permute-done.20.low_far = f32[896,128]{1,0:T(8,128)S(1)} collective-permute-done((f32[896,128]{1,0:T(8,128)S(1)}, f32[896,128]{1,0:T(8,128)S(1)}, u32[]{:S(2)}, u32[]{:S(2)}) %collective-permute-start.20) | collective-permute-done | bytes 458784 | tf_op jit(solution)/shard_map/ppermute | solution.py:56
  90.5 0.2 shard_map.82
  90.7 0.1 collective-permute-start.24
  90.8 3.5 %collective-permute-start.25 = (f32[448,128]{1,0:T(8,128)S(1)}, f32[448,128]{1,0:T(8,128)S(1)}, u32[]{:S(2)}, u32[]{:S(2)}) collective-permute-start(f32[448,128]{1,0:T(8,128)S(1)} %get-tuple-element.80), channel_id=1, source_target_pairs={{0,16},{8,24},{16,0},{24,8},{1,17},{9,25},{17,1},{25,9},{2,18},{10... | collective-permute-start | bytes 688136 | tf_op jit(solution)/shard_map/ppermute | solution.py:56
  94.3 1.3 %collective-permute-done.14.b = f32[464,128]{1,0:T(8,128)S(1)} collective-permute-done((f32[464,128]{1,0:T(8,128)S(1)}, f32[464,128]{1,0:T(8,128)S(1)}, u32[]{:S(2)}, u32[]{:S(2)}) %collective-permute-start.14) | collective-permute-done | bytes 237600 | tf_op jit(solution)/shard_map/ppermute | solution.py:56
  95.6 2.3 %collective-permute-start.26 = (f32[448,128]{1,0:T(8,128)S(1)}, f32[448,128]{1,0:T(8,128)S(1)}, u32[]{:S(2)}, u32[]{:S(2)}) collective-permute-start(f32[448,128]{1,0:T(8,128)S(1)} %get-tuple-element.81), channel_id=1, source_target_pairs={{0,24},{8,0},{16,8},{24,16},{1,25},{9,1},{17,9},{25,17},{2,26},{10... | collective-permute-start | bytes 688136 | tf_op jit(solution)/shard_map/ppermute | solution.py:56
  97.9 3.8 %collective-permute-done.15.c = f32[464,128]{1,0:T(8,128)S(1)} collective-permute-done((f32[464,128]{1,0:T(8,128)S(1)}, f32[464,128]{1,0:T(8,128)S(1)}, u32[]{:S(2)}, u32[]{:S(2)}) %collective-permute-start.15) | collective-permute-done | bytes 237600 | tf_op jit(solution)/shard_map/ppermute | solution.py:56
  101.7 6.2 %collective-permute-start.17 = (f32[240,128]{1,0:T(8,128)S(1)}, f32[240,128]{1,0:T(8,128)S(1)}, u32[]{:S(2)}, u32[]{:S(2)}) collective-permute-start(f32[240,128]{1,0:T(8,128)S(1)} %get-tuple-element.73), channel_id=1, source_target_pairs={{0,32},{32,0},{1,33},{33,1},{2,34},{34,2},{3,35},{35,3},{4,36},{36... | collective-permute-start | bytes 368648 | tf_op jit(solution)/shard_map/ppermute | solution.py:56
  108.0 2.2 %collective-permute-start.27 = (f32[224,128]{1,0:T(8,128)S(1)}, f32[224,128]{1,0:T(8,128)S(1)}, u32[]{:S(2)}, u32[]{:S(2)}) collective-permute-start(f32[224,128]{1,0:T(8,128)S(1)} %get-tuple-element.83), channel_id=1, source_target_pairs={{0,32},{32,0},{1,33},{33,1},{2,34},{34,2},{3,35},{35,3},{4,36},{36... | collective-permute-start | bytes 344072 | tf_op jit(solution)/shard_map/ppermute | solution.py:56
  110.2 6.5 %collective-permute-done.27.got2 = f32[224,128]{1,0:T(8,128)S(1)} collective-permute-done((f32[224,128]{1,0:T(8,128)S(1)}, f32[224,128]{1,0:T(8,128)S(1)}, u32[]{:S(2)}, u32[]{:S(2)}) %collective-permute-start.27) | collective-permute-done | bytes 114720 | tf_op jit(solution)/shard_map/ppermute | solution.py:56
  116.7 0.7 shard_map.84
  117.4 4.4 %collective-permute-start.28 = (f32[32,128]{1,0:T(8,128)S(1)}, f32[32,128]{1,0:T(8,128)S(1)}, u32[]{:S(2)}, u32[]{:S(2)}) collective-permute-start(f32[32,128]{1,0:T(8,128)S(1)} %get-tuple-element.85), channel_id=1, source_target_pairs={{0,1},{1,0},{2,3},{3,2},{4,5},{5,4},{6,7},{7,6},{8,9},{9,8},{10,11... | collective-permute-start | bytes 49160 | tf_op jit(solution)/shard_map/ppermute | solution.py:56
  121.9 0.8 collective-permute-done.28
  122.7 0.5 collective-permute-start.29
  123.2 2.8 %collective-permute-start.31 = (f32[32,128]{1,0:T(8,128)S(1)}, f32[32,128]{1,0:T(8,128)S(1)}, u32[]{:S(2)}, u32[]{:S(2)}) collective-permute-start(f32[32,128]{1,0:T(8,128)S(1)} %max.3.a), channel_id=1, source_target_pairs={{0,6},{2,0},{4,2},{6,4},{1,7},{3,1},{5,3},{7,5},{8,14},{10,8},{12,... | collective-permute-start | bytes 49160 | tf_op jit(solution)/shard_map/ppermute | solution.py:56
  126.0 1.1 collective-permute-done.29.b
  127.1 0.6 collective-permute-done.31.d
  127.7 0.7 shard_map.85
  (34 shorter events, 0.5 us)
Async XLA Ops:
  0.6 7.9 %copy-start.1 = (s32[6,1024]{1,0:T(8,128)S(1)}, s32[6,1024]{1,0:T(8,128)}, u32[]{:S(2)}) copy-start(s32[6,1024]{1,0:T(8,128)} %param.7) | copy-start | bytes 73732
  2.8 9.5 %collective-permute-start = (f32[232,128]{1,0:T(8,128)S(1)}, f32[232,128]{1,0:T(8,128)S(1)}, u32[]{:S(2)}, u32[]{:S(2)}) collective-permute-start(f32[232,128]{1,0:T(8,128)S(1)} %get-tuple-element.44.after_ref.a), channel_id=1, source_target_pairs={{0,8},{8,16},{16,24},{24,0},{1,9},{9,17},{17,25},{25,1},{2,10},{10... | collective-permute-start | bytes 356360 | tf_op jit(solution)/shard_map/ppermute | solution.py:56
  4.9 7.6 %collective-permute-start.1 = (f32[232,128]{1,0:T(8,128)S(1)}, f32[232,128]{1,0:T(8,128)S(1)}, u32[]{:S(2)}, u32[]{:S(2)}) collective-permute-start(f32[232,128]{1,0:T(8,128)S(1)} %get-tuple-element.44.after_ref.a), channel_id=1, source_target_pairs={{0,16},{8,24},{16,0},{24,8},{1,17},{9,25},{17,1},{25,9},{2,18},{10... | collective-permute-start | bytes 356360 | tf_op jit(solution)/shard_map/ppermute | solution.py:56
  7.4 5.2 %collective-permute-start.2 = (f32[232,128]{1,0:T(8,128)S(1)}, f32[232,128]{1,0:T(8,128)S(1)}, u32[]{:S(2)}, u32[]{:S(2)}) collective-permute-start(f32[232,128]{1,0:T(8,128)S(1)} %get-tuple-element.44.after_ref.a), channel_id=1, source_target_pairs={{0,24},{8,0},{16,8},{24,16},{1,25},{9,1},{17,9},{25,17},{2,26},{10... | collective-permute-start | bytes 356360 | tf_op jit(solution)/shard_map/ppermute | solution.py:56
  12.6 24.8 %copy-start = (bf16[1024,1024]{1,0:T(8,128)(2,1)S(1)}, bf16[1024,1024]{1,0:T(8,128)(2,1)}, u32[]{:S(2)}) copy-start(bf16[1024,1024]{1,0:T(8,128)(2,1)} %traits_ref.3) | copy-start | bytes 6291460
  12.6 7.6 %collective-permute-start.3 = (f32[232,128]{1,0:T(8,128)S(1)}, f32[232,128]{1,0:T(8,128)S(1)}, u32[]{:S(2)}, u32[]{:S(2)}) collective-permute-start(f32[232,128]{1,0:T(8,128)S(1)} %shard_map.61.after_ref.a), channel_id=1, source_target_pairs={{0,64},{64,128},{128,192},{192,0},{1,65},{65,129},{129,193},{193,1... | collective-permute-start | bytes 356360 | tf_op jit(solution)/shard_map/ppermute | solution.py:56
  14.0 6.7 %collective-permute-start.4 = (f32[232,128]{1,0:T(8,128)S(1)}, f32[232,128]{1,0:T(8,128)S(1)}, u32[]{:S(2)}, u32[]{:S(2)}) collective-permute-start(f32[232,128]{1,0:T(8,128)S(1)} %shard_map.61.after_ref.a), channel_id=1, source_target_pairs={{0,128},{64,192},{128,0},{192,64},{1,129},{65,193},{129,1},{193,65... | collective-permute-start | bytes 356360 | tf_op jit(solution)/shard_map/ppermute | solution.py:56
  16.6 4.7 %collective-permute-start.5 = (f32[232,128]{1,0:T(8,128)S(1)}, f32[232,128]{1,0:T(8,128)S(1)}, u32[]{:S(2)}, u32[]{:S(2)}) collective-permute-start(f32[232,128]{1,0:T(8,128)S(1)} %shard_map.61.after_ref.a), channel_id=1, source_target_pairs={{0,192},{64,0},{128,64},{192,128},{1,193},{65,1},{129,65},{193,129... | collective-permute-start | bytes 356360 | tf_op jit(solution)/shard_map/ppermute | solution.py:56
  21.4 9.7 %collective-permute-start.6 = (f32[232,128]{1,0:T(8,128)S(1)}, f32[232,128]{1,0:T(8,128)S(1)}, u32[]{:S(2)}, u32[]{:S(2)}) collective-permute-start(f32[232,128]{1,0:T(8,128)S(1)} %shard_map.63.own_ref.after_ref), channel_id=1, source_target_pairs={{0,32},{32,0},{1,33},{33,1},{2,34},{34,2},{3,35},{35,3},{4,36},{36... | collective-permute-start | bytes 356360 | tf_op jit(solution)/shard_map/ppermute | solution.py:56
  33.9 6.4 %collective-permute-start.7 = (f32[40,512]{1,0:T(8,128)S(1)}, f32[40,512]{1,0:T(8,128)S(1)}, u32[]{:S(2)}, u32[]{:S(2)}) collective-permute-start(f32[40,512]{1,0:T(8,128)S(1)} %slice.4), channel_id=1, source_target_pairs={{0,1},{1,0},{2,3},{3,2},{4,5},{5,4},{6,7},{7,6},{8,9},{9,8},{10,11... | collective-permute-start | bytes 245768 | tf_op jit(solution)/shard_map/ppermute | solution.py:56
  42.8 12.6 %collective-permute-start.12 = (f32[896,128]{1,0:T(8,128)S(1)}, f32[896,128]{1,0:T(8,128)S(1)}, u32[]{:S(2)}, u32[]{:S(2)}) collective-permute-start(f32[896,128]{1,0:T(8,128)S(1)} %get-tuple-element.56.after_ref), channel_id=1, source_target_pairs={{0,24},{8,0},{16,8},{24,16},{1,25},{9,1},{17,9},{25,17},{2,26},{10... | collective-permute-start | bytes 1376264 | tf_op jit(solution)/shard_map/ppermute | solution.py:56
  45.6 14.1 %collective-permute-start.9 = (f32[912,128]{1,0:T(8,128)S(1)}, f32[912,128]{1,0:T(8,128)S(1)}, u32[]{:S(2)}, u32[]{:S(2)}) collective-permute-start(f32[912,128]{1,0:T(8,128)S(1)} %get-tuple-element.65), channel_id=1, source_target_pairs={{0,8},{8,16},{16,24},{24,0},{1,9},{9,17},{17,25},{25,1},{2,10},{10... | collective-permute-start | bytes 1400840 | tf_op jit(solution)/shard_map/ppermute | solution.py:56
  46.3 13.5 %collective-permute-start.22 = (f32[896,128]{1,0:T(8,128)S(1)}, f32[896,128]{1,0:T(8,128)S(1)}, u32[]{:S(2)}, u32[]{:S(2)}) collective-permute-start(f32[896,128]{1,0:T(8,128)S(1)} %get-tuple-element.57.after_ref), channel_id=1, source_target_pairs={{0,192},{64,0},{128,64},{192,128},{1,193},{65,1},{129,65},{193,129... | collective-permute-start | bytes 1376264 | tf_op jit(solution)/shard_map/ppermute | solution.py:56
  48.8 12.7 %collective-permute-start.19 = (f32[896,128]{1,0:T(8,128)S(1)}, f32[896,128]{1,0:T(8,128)S(1)}, u32[]{:S(2)}, u32[]{:S(2)}) collective-permute-start(f32[896,128]{1,0:T(8,128)S(1)} %get-tuple-element.77), channel_id=1, source_target_pairs={{0,64},{64,128},{128,192},{192,0},{1,65},{65,129},{129,193},{193,1... | collective-permute-start | bytes 1376264 | tf_op jit(solution)/shard_map/ppermute | solution.py:56
  49.6 19.0 %collective-permute-start.11 = (f32[896,128]{1,0:T(8,128)S(1)}, f32[896,128]{1,0:T(8,128)S(1)}, u32[]{:S(2)}, u32[]{:S(2)}) collective-permute-start(f32[896,128]{1,0:T(8,128)S(1)} %get-tuple-element.58.after_ref), channel_id=1, source_target_pairs={{0,8},{8,16},{16,24},{24,0},{1,9},{9,17},{17,25},{25,1},{2,10},{10... | collective-permute-start | bytes 1376264 | tf_op jit(solution)/shard_map/ppermute | solution.py:56
  55.4 13.5 %collective-permute-start.8 = (f32[912,128]{1,0:T(8,128)S(1)}, f32[912,128]{1,0:T(8,128)S(1)}, u32[]{:S(2)}, u32[]{:S(2)}) collective-permute-start(f32[912,128]{1,0:T(8,128)S(1)} %get-tuple-element.63), channel_id=1, source_target_pairs={{0,24},{8,0},{16,8},{24,16},{1,25},{9,1},{17,9},{25,17},{2,26},{10... | collective-permute-start | bytes 1400840 | tf_op jit(solution)/shard_map/ppermute | solution.py:56
  59.6 18.2 %collective-permute-start.13 = (f32[896,128]{1,0:T(8,128)S(1)}, f32[896,128]{1,0:T(8,128)S(1)}, u32[]{:S(2)}, u32[]{:S(2)}) collective-permute-start(f32[896,128]{1,0:T(8,128)S(1)} %shard_map.77), channel_id=1, source_target_pairs={{0,24},{8,0},{16,8},{24,16},{1,25},{9,1},{17,9},{25,17},{2,26},{10... | collective-permute-start | bytes 1376264 | tf_op jit(solution)/shard_map/ppermute | solution.py:56
  59.8 18.8 %collective-permute-start.10 = (f32[912,128]{1,0:T(8,128)S(1)}, f32[912,128]{1,0:T(8,128)S(1)}, u32[]{:S(2)}, u32[]{:S(2)}) collective-permute-start(f32[912,128]{1,0:T(8,128)S(1)} %shard_map.76), channel_id=1, source_target_pairs={{0,8},{8,16},{16,24},{24,0},{1,9},{9,17},{17,25},{25,1},{2,10},{10... | collective-permute-start | bytes 1400840 | tf_op jit(solution)/shard_map/ppermute | solution.py:56
  61.5 17.8 %collective-permute-start.18 = (f32[896,128]{1,0:T(8,128)S(1)}, f32[896,128]{1,0:T(8,128)S(1)}, u32[]{:S(2)}, u32[]{:S(2)}) collective-permute-start(f32[896,128]{1,0:T(8,128)S(1)} %get-tuple-element.75), channel_id=1, source_target_pairs={{0,192},{64,0},{128,64},{192,128},{1,193},{65,1},{129,65},{193,129... | collective-permute-start | bytes 1376264 | tf_op jit(solution)/shard_map/ppermute | solution.py:56
  68.6 13.9 %collective-permute-start.21 = (f32[896,128]{1,0:T(8,128)S(1)}, f32[896,128]{1,0:T(8,128)S(1)}, u32[]{:S(2)}, u32[]{:S(2)}) collective-permute-start(f32[896,128]{1,0:T(8,128)S(1)} %get-tuple-element.59.after_ref), channel_id=1, source_target_pairs={{0,64},{64,128},{128,192},{192,0},{1,65},{65,129},{129,193},{193,1... | collective-permute-start | bytes 1376264 | tf_op jit(solution)/shard_map/ppermute | solution.py:56
  68.9 14.9 %collective-permute-start.23 = (f32[896,128]{1,0:T(8,128)S(1)}, f32[896,128]{1,0:T(8,128)S(1)}, u32[]{:S(2)}, u32[]{:S(2)}) collective-permute-start(f32[896,128]{1,0:T(8,128)S(1)} %shard_map.81), channel_id=1, source_target_pairs={{0,192},{64,0},{128,64},{192,128},{1,193},{65,1},{129,65},{193,129... | collective-permute-start | bytes 1376264 | tf_op jit(solution)/shard_map/ppermute | solution.py:56
  77.8 12.7 %collective-permute-start.20 = (f32[896,128]{1,0:T(8,128)S(1)}, f32[896,128]{1,0:T(8,128)S(1)}, u32[]{:S(2)}, u32[]{:S(2)}) collective-permute-start(f32[896,128]{1,0:T(8,128)S(1)} %shard_map.80), channel_id=1, source_target_pairs={{0,64},{64,128},{128,192},{192,0},{1,65},{65,129},{129,193},{193,1... | collective-permute-start | bytes 1376264 | tf_op jit(solution)/shard_map/ppermute | solution.py:56
  78.7 16.8 %collective-permute-start.14 = (f32[464,128]{1,0:T(8,128)S(1)}, f32[464,128]{1,0:T(8,128)S(1)}, u32[]{:S(2)}, u32[]{:S(2)}) collective-permute-start(f32[464,128]{1,0:T(8,128)S(1)} %get-tuple-element.69), channel_id=1, source_target_pairs={{0,64},{64,128},{128,192},{192,0},{1,65},{65,129},{129,193},{193,1... | collective-permute-start | bytes 712712 | tf_op jit(solution)/shard_map/ppermute | solution.py:56
  79.4 22.3 %collective-permute-start.15 = (f32[464,128]{1,0:T(8,128)S(1)}, f32[464,128]{1,0:T(8,128)S(1)}, u32[]{:S(2)}, u32[]{:S(2)}) collective-permute-start(f32[464,128]{1,0:T(8,128)S(1)} %get-tuple-element.70), channel_id=1, source_target_pairs={{0,128},{64,192},{128,0},{192,64},{1,129},{65,193},{129,1},{193,65... | collective-permute-start | bytes 712712 | tf_op jit(solution)/shard_map/ppermute | solution.py:56
  82.5 19.2 %collective-permute-start.16 = (f32[464,128]{1,0:T(8,128)S(1)}, f32[464,128]{1,0:T(8,128)S(1)}, u32[]{:S(2)}, u32[]{:S(2)}) collective-permute-start(f32[464,128]{1,0:T(8,128)S(1)} %get-tuple-element.71), channel_id=1, source_target_pairs={{0,192},{64,0},{128,64},{192,128},{1,193},{65,1},{129,65},{193,129... | collective-permute-start | bytes 712712 | tf_op jit(solution)/shard_map/ppermute | solution.py:56
  90.7 17.2 %collective-permute-start.24 = (f32[448,128]{1,0:T(8,128)S(1)}, f32[448,128]{1,0:T(8,128)S(1)}, u32[]{:S(2)}, u32[]{:S(2)}) collective-permute-start(f32[448,128]{1,0:T(8,128)S(1)} %get-tuple-element.79), channel_id=1, source_target_pairs={{0,8},{8,16},{16,24},{24,0},{1,9},{9,17},{17,25},{25,1},{2,10},{10... | collective-permute-start | bytes 688136 | tf_op jit(solution)/shard_map/ppermute | solution.py:56
  90.8 17.1 %collective-permute-start.25 = (f32[448,128]{1,0:T(8,128)S(1)}, f32[448,128]{1,0:T(8,128)S(1)}, u32[]{:S(2)}, u32[]{:S(2)}) collective-permute-start(f32[448,128]{1,0:T(8,128)S(1)} %get-tuple-element.80), channel_id=1, source_target_pairs={{0,16},{8,24},{16,0},{24,8},{1,17},{9,25},{17,1},{25,9},{2,18},{10... | collective-permute-start | bytes 688136 | tf_op jit(solution)/shard_map/ppermute | solution.py:56
  95.6 12.3 %collective-permute-start.26 = (f32[448,128]{1,0:T(8,128)S(1)}, f32[448,128]{1,0:T(8,128)S(1)}, u32[]{:S(2)}, u32[]{:S(2)}) collective-permute-start(f32[448,128]{1,0:T(8,128)S(1)} %get-tuple-element.81), channel_id=1, source_target_pairs={{0,24},{8,0},{16,8},{24,16},{1,25},{9,1},{17,9},{25,17},{2,26},{10... | collective-permute-start | bytes 688136 | tf_op jit(solution)/shard_map/ppermute | solution.py:56
  101.7 15.0 %collective-permute-start.17 = (f32[240,128]{1,0:T(8,128)S(1)}, f32[240,128]{1,0:T(8,128)S(1)}, u32[]{:S(2)}, u32[]{:S(2)}) collective-permute-start(f32[240,128]{1,0:T(8,128)S(1)} %get-tuple-element.73), channel_id=1, source_target_pairs={{0,32},{32,0},{1,33},{33,1},{2,34},{34,2},{3,35},{35,3},{4,36},{36... | collective-permute-start | bytes 368648 | tf_op jit(solution)/shard_map/ppermute | solution.py:56
  108.0 8.7 %collective-permute-start.27 = (f32[224,128]{1,0:T(8,128)S(1)}, f32[224,128]{1,0:T(8,128)S(1)}, u32[]{:S(2)}, u32[]{:S(2)}) collective-permute-start(f32[224,128]{1,0:T(8,128)S(1)} %get-tuple-element.83), channel_id=1, source_target_pairs={{0,32},{32,0},{1,33},{33,1},{2,34},{34,2},{3,35},{35,3},{4,36},{36... | collective-permute-start | bytes 344072 | tf_op jit(solution)/shard_map/ppermute | solution.py:56
  117.4 5.3 %collective-permute-start.28 = (f32[32,128]{1,0:T(8,128)S(1)}, f32[32,128]{1,0:T(8,128)S(1)}, u32[]{:S(2)}, u32[]{:S(2)}) collective-permute-start(f32[32,128]{1,0:T(8,128)S(1)} %get-tuple-element.85), channel_id=1, source_target_pairs={{0,1},{1,0},{2,3},{3,2},{4,5},{5,4},{6,7},{7,6},{8,9},{9,8},{10,11... | collective-permute-start | bytes 49160 | tf_op jit(solution)/shard_map/ppermute | solution.py:56
  122.7 4.4 %collective-permute-start.29 = (f32[32,128]{1,0:T(8,128)S(1)}, f32[32,128]{1,0:T(8,128)S(1)}, u32[]{:S(2)}, u32[]{:S(2)}) collective-permute-start(f32[32,128]{1,0:T(8,128)S(1)} %max.3.a), channel_id=1, source_target_pairs={{0,2},{2,4},{4,6},{6,0},{1,3},{3,5},{5,7},{7,1},{8,10},{10,12},{12... | collective-permute-start | bytes 49160 | tf_op jit(solution)/shard_map/ppermute | solution.py:56
  123.2 3.9 %collective-permute-start.30 = (f32[32,128]{1,0:T(8,128)S(1)}, f32[32,128]{1,0:T(8,128)S(1)}, u32[]{:S(2)}, u32[]{:S(2)}) collective-permute-start(f32[32,128]{1,0:T(8,128)S(1)} %max.3.a), channel_id=1, source_target_pairs={{0,4},{2,6},{4,0},{6,2},{1,5},{3,7},{5,1},{7,3},{8,12},{10,14},{12... | collective-permute-start | bytes 49160 | tf_op jit(solution)/shard_map/ppermute | solution.py:56
  123.2 4.5 %collective-permute-start.31 = (f32[32,128]{1,0:T(8,128)S(1)}, f32[32,128]{1,0:T(8,128)S(1)}, u32[]{:S(2)}, u32[]{:S(2)}) collective-permute-start(f32[32,128]{1,0:T(8,128)S(1)} %max.3.a), channel_id=1, source_target_pairs={{0,6},{2,0},{4,2},{6,4},{1,7},{3,1},{5,3},{7,5},{8,14},{10,8},{12,... | collective-permute-start | bytes 49160 | tf_op jit(solution)/shard_map/ppermute | solution.py:56
where the time goes:
time: 129 us; the launch traced here: 128 us
  starting transfers between devices  64.3 us (50%)
  waiting for transfers between devices  39.2 us (30%)
  Pallas kernels  23.9 us (19%)
    ppermute x32, starting transfers between devices, shift(): return lax.ppermute(value, axis, shifts(axis, k))  64.3 us
    ppermute x32, waiting for transfers between devices, shift(): return lax.ppermute(value, axis, shifts(axis, k))  39.2 us
    pallas_call x27, Pallas kernels, call(): pl.pallas_call(kernel, out_shape=shapes[0] if single else shapes, cost_es...  23.9 us
  transfers between devices with their start and end apart: 32, of which 16 were waited for; matrix products, arithmetic and copies ran while one was open for 0% of the time, Pallas kernels for 12%

commit v1 on v0

--- a/solution.py
+++ b/solution.py
@@ -97,44 +97,54 @@
 
 def solve_kernel(own_ref, far_ref, out_ref):
     total = own_ref[...] + far_ref[...]
-    gram = total[BLOCKS * C :]
-    blocks = [total[j * C : (j + 1) * C] for j in range(BLOCKS)]
-    ones = [gram[C + 1 + j : C + 2 + j] for j in range(BLOCKS)]
-    row_id = lax.broadcasted_iota(jnp.int32, (40, COLS), 0)
-    top = jnp.concatenate([*blocks, gram[:C]], axis=1)
-    low = jnp.concatenate([*ones, gram[C : C + 1]], axis=1)
-    m = jnp.concatenate([top, jnp.broadcast_to(low, (8, COLS))], axis=0)
-    for k in range(C + 1):
-        at = V + HALF + k
-        col = m[:, at : at + 1]
-        row = m[k : k + 1, :] / m[k : k + 1, at : at + 1]
-        m = jnp.where(row_id == k, row, m - col * row)
-    out_ref[...] = jnp.where(row_id[:, : V + HALF] <= C, m[:, : V + HALF], 0.0)
-
-
-def resid_kernel(core_ref, own_ref, far_ref, yt_ref, xt_ref, dx_ref, dxp1_ref, dxp2_ref, dxp3_ref, rt_ref, g1_ref, g2_ref, ss_ref):
-    core = core_ref[0]
-    xt = xt_ref[...]
-    zeros = jnp.zeros((8, E), F32)
-    mine = own_ref[:, V:]
-    other = far_ref[...]
-    first = jnp.where(core == 0, mine, other)
-    second = jnp.where(core == 0, other, mine)
-    coef = jnp.concatenate([jnp.concatenate([first, second], axis=1), zeros], axis=0)
-    coef_t = jnp.transpose(coef).astype(BF16)
-    ss_parts = []
-    for at in range(0, E, 128):
-        res = yt_ref[at : at + 128, :].astype(F32) - dot(coef_t[at : at + 128], xt)
-        rt_ref[at : at + 128, :] = res.astype(BF16)
-        sq = res * res
-        lanes = sq[:, :128]
-        for b in range(128, ROWS, 128):
-            lanes = lanes + sq[:, b : b + 128]
-        ss_parts.append(jnp.sum(jnp.transpose(lanes), axis=0, keepdims=True))
+    base = BLOCKS * C
+    m = [
+        [total[j * C + g * 8 : j * C + g * 8 + 8] for j in range(BLOCKS)] + [total[base + g * 8 : base + g * 8 + 8]]
+        for g in range(C // 8)
+    ]
+    wide = (8, 128)
+    zero = jnp.broadcast_to(total[base + 39 : base + 40], wide)
+    ones = [total[base + C + 1 + j : base + C + 2 + j] for j in range(BLOCKS)] + [total[base + C : base + C + 1]]
+    m.append([jnp.broadcast_to(part, wide) for part in ones])
+    row_id = lax.broadcasted_iota(jnp.int32, wide, 0)
+
+    def line_of(part, line):
+        return jnp.broadcast_to(part[line : line + 1], wide)
+
+    for k in range(0, C, 2):
+        here, line = k // 8, k % 8
+        left = [jnp.broadcast_to(part[BLOCKS][:, k : k + 1], wide) + zero for part in m]
+        right = [jnp.broadcast_to(part[BLOCKS][:, k + 1 : k + 2], wide) + zero for part in m]
+        p, q = line_of(left[here], line), line_of(right[here], line)
+        r, s = line_of(left[here], line + 1), line_of(right[here], line + 1)
+        inverse = 1.0 / (p * s - q * r)
+        p, q, r, s = p * inverse, q * inverse, r * inverse, s * inverse
+        for j in range(BLOCKS + 1):
+            top, low = line_of(m[here][j], line), line_of(m[here][j], line + 1)
+            top, low = s * top - q * low, p * low - r * top
+            for g in range(len(m)):
+                rest = m[g][j] - left[g] * top - right[g] * low
+                if g == here:
+                    rest = jnp.where(row_id == line, top, jnp.where(row_id == line + 1, low, rest))
+                m[g][j] = rest
+    last = [jnp.broadcast_to(part[BLOCKS][:, C : C + 1], wide) + zero for part in m]
+    inverse = 1.0 / line_of(last[-1], 0)
+    for j in range(BLOCKS):
+        row = line_of(m[-1][j], 0) * inverse
+        for g in range(len(m)):
+            m[g][j] = m[g][j] - last[g] * row if g < C // 8 else row
+    for g in range(len(m)):
+        for j in range(BLOCKS):
+            done = m[g][j] if g < C // 8 else jnp.where(row_id == 0, m[g][j], 0.0)
+            out_ref[g * 8 : g * 8 + 8, j * 128 : (j + 1) * 128] = done
+
+
+def geno_kernel(own_ref, dx_ref, dxp1_ref, dxp2_ref, dxp3_ref, g1_ref, g2_ref, ss_ref):
     gamma = jnp.concatenate([own_ref[:, :V], jnp.zeros((88, V), F32)], axis=0).astype(BF16)
     res_g = dx_ref[:, :V].astype(F32) - dot(dx_ref[:, V:], gamma)
     g1_ref[:, :V] = res_g.astype(BF16)
     ss_v = jnp.sum(res_g * res_g, axis=0, keepdims=True)
+    ss_ref[...] = jnp.concatenate([ss_v[:, :128], ss_v[:, 128:], jnp.zeros((6, 128), F32)], axis=0)
     places = [(ref, q) for ref in (dxp1_ref, dxp2_ref, dxp3_ref) for q in range(ref.shape[0])]
     for p, (src, q) in enumerate(places):
         g = (src[q, :, :V].astype(F32) - dot(src[q, :, V:], gamma)).astype(BF16)
@@ -146,9 +156,27 @@
         else:
             g1_ref[:, at:] = g[:, : CHUNK - at]
             g2_ref[:, : at + V - CHUNK] = g[:, CHUNK - at :]
-    ss_ref[...] = jnp.concatenate(
-        [*ss_parts, ss_v[:, :128], ss_v[:, 128:], jnp.zeros((SQUARES - 10, 128), F32)], axis=0
-    )
+
+
+def resid_kernel(core_ref, own_ref, far_ref, yt_ref, xt_ref, ss_v_ref, rt_ref, ss_ref):
+    core = core_ref[0]
+    xt = xt_ref[...]
+    mine = own_ref[:, V:]
+    other = far_ref[...]
+    first = jnp.where(core == 0, mine, other)
+    second = jnp.where(core == 0, other, mine)
+    coef = jnp.concatenate([jnp.concatenate([first, second], axis=1), jnp.zeros((8, E), F32)], axis=0)
+    coef_t = jnp.transpose(coef).astype(BF16)
+    for j in range(E // 128):
+        at = j * 128
+        res = yt_ref[at : at + 128, :].astype(F32) - dot(coef_t[at : at + 128], xt)
+        rt_ref[at : at + 128, :] = res.astype(BF16)
+        sq = res * res
+        lanes = sq[:, :128]
+        for b in range(128, ROWS, 128):
+            lanes = lanes + sq[:, b : b + 128]
+        ss_ref[j : j + 1, :] = jnp.sum(jnp.transpose(lanes), axis=0, keepdims=True)
+    ss_ref[8:, :] = ss_v_ref[...]
 
 
 def lanes_to_rows(out_ref, value):
@@ -198,31 +226,51 @@
             out[LANES * 32 :, :] = (a[rows, :] + c[rows, :]) + (b[rows, :] + d[rows, :])
 
 
-def score_kernel(at_ref, keep1, got1, keep2, got2, obs_ref, peak_ref):
-    samples = 32 * ROWS
-    factor = math.sqrt(samples - C - 2) / samples
-    first = keep1[...] + got1[...]
-    second = keep2[...] + got2[...]
-    sums = first[LANES * 32 :]
-    scales = lax.rsqrt(sums / samples + EPSILON)
+FACTOR = math.sqrt(32 * ROWS - C - 2) / (32 * ROWS)
+
+
+def score1_kernel(at_ref, keep, got, obs_ref, peak_ref, scale_ref):
+    total = keep[...] + got[...]
+    scales = lax.rsqrt(total[LANES * 32 :] / (32 * ROWS) + EPSILON)
     place = lax.broadcasted_iota(jnp.int32, (SQUARES, 128), 0)
     lane = lax.broadcasted_iota(jnp.int32, (32, 128), 1)
     row = lax.broadcasted_iota(jnp.int32, (32, 128), 0)
     scale_e = jnp.sum(jnp.where(place == at_ref[0] // 4, scales, 0.0), axis=0, keepdims=True)
     own = jnp.where(lane == row + (at_ref[0] % 4) * 32, scale_e, 0.0)
-    own_scale = jnp.sum(own, axis=1, keepdims=True)
-    scale_v = jnp.concatenate([scales[8:9], scales[9:10]], axis=1)
-    blocks = [part[j * 32 : (j + 1) * 32] for part in (first, second) for j in range(LANES)]
-
-    def scores(p):
-        cross = jnp.concatenate([blocks[2 * p], blocks[2 * p + 1]], axis=1)
-        return cross * own_scale * scale_v * factor
-
-    obs_ref[...] = scores(0)
-    peaks = jnp.zeros((32, 128), F32)
-    for p in range(PERMS):
-        peaks = jnp.where(lane == p, jnp.max(jnp.abs(scores(p + 1)), axis=1, keepdims=True), peaks)
-    peak_ref[...] = peaks
+    own_scale = jnp.broadcast_to(jnp.sum(own, axis=1, keepdims=True), (32, 128))
+    scale_ref[:32, :] = own_scale
+    scale_ref[32:, :] = scales[8:16]
+    scale_v = [scales[8:9], scales[9:10]]
+    peaks = [None] * 3
+    for j in range(LANES):
+        score = total[j * 32 : (j + 1) * 32] * own_scale * scale_v[j % 2] * FACTOR
+        if j < 2:
+            obs_ref[:, j * 128 : (j + 1) * 128] = score
+        else:
+            p = j // 2 - 1
+            peaks[p] = jnp.abs(score) if peaks[p] is None else jnp.maximum(peaks[p], jnp.abs(score))
+    out = jnp.zeros((32, 128), F32)
+    for p, part in enumerate(peaks):
+        out = jnp.where(lane == p, jnp.max(part, axis=1, keepdims=True), out)
+    peak_ref[...] = out
+
+
+def score2_kernel(keep, got, peak1_ref, scale_ref, peak_ref):
+    total = keep[...] + got[...]
+    own_scale = scale_ref[:32]
+    scale_v = [scale_ref[32:33], scale_ref[33:34]]
+    lane = lax.broadcasted_iota(jnp.int32, (32, 128), 1)
+    peaks = [None] * PERMS
+    for j in range(LANES):
+        score = jnp.abs(total[j * 32 : (j + 1) * 32] * own_scale * scale_v[(j + LANES) % 2] * FACTOR)
+        p = (j + LANES) // 2 - 1
+        peaks[p] = score if peaks[p] is None else jnp.maximum(peaks[p], score)
+    out = peak1_ref[...]
+    for p, part in enumerate(peaks):
+        if part is not None:
+            best = jnp.max(part, axis=1, keepdims=True)
+            out = jnp.where(lane == p, jnp.maximum(out, best), out)
+    peak_ref[...] = out
 
 
 def peak_kernel(a, b, c, d, out_ref):
@@ -322,13 +370,20 @@
     )
     coef = call(solve_kernel, [((40, V + HALF), F32)], pay, shift(pay, "zh", 1), room=4, flops=10**8)
     far = shift(coef[:, V:], "core", 1)
-    rt, g1, g2, ss = call(
+    g1, g2, ss_v = call(
+        geno_kernel,
+        [((ROWS, CHUNK), BF16), ((ROWS, CHUNK), BF16), ((8, 128), F32)],
+        coef, dx, *turned,
+        flops=2 * 128 * ROWS * 2 * CHUNK,
+        room=16,
+    )
+    rt, ss = call(
         resid_kernel,
-        [((E, ROWS), BF16), ((ROWS, CHUNK), BF16), ((ROWS, CHUNK), BF16), ((SQUARES, 128), F32)],
-        core, coef, far, yt, xt, dx, *turned,
-        grid_spec=scalar_spec(8, 4),
-        flops=2 * 2 * ROWS * E * 128,
-        room=24,
+        [((E, ROWS), BF16), ((SQUARES, 128), F32)],
+        core, coef, far, yt, xt, ss_v,
+        grid_spec=scalar_spec(5, 2),
+        flops=2 * 128 * ROWS * E,
+        room=12,
     )
 
     rt5 = rt.reshape(4, 2, 4, 32, ROWS)
@@ -390,7 +445,8 @@
                     in_specs=[whole, whole, anywhere], room=2,
                 )
             )
-        got[axis, "lows"], got[axis, "highs"] = shift(relayed[0], axis, 1), shift(relayed[1], axis, 3)
+        got[axis, "lows"] = shift(relayed[0], axis, 1)
+        got[axis, "highs"] = shift(relayed[1], axis, 3)
     keeps = []
     for axis, other, at in (("x", "y", y), ("y", "x", x)):
         rows = LANES * 64 + (SQUARES if axis == "x" else 0)
@@ -408,11 +464,12 @@
             last_kernel, [((rows, 128), F32)] * 2, zh, *parts[axis],
             grid_spec=scalar_spec(4, 2), flops=10**6, room=2,
         )
-        keeps += [keep, shift(send, "zh", 1)]
-    observed, peaks = call(
-        score_kernel, [((32, V), F32), ((32, 128), F32)], samp, *keeps,
-        grid_spec=scalar_spec(4, 2), flops=10**6, room=4,
-    )
+        keeps.append((keep, shift(send, "zh", 1)))
+    observed, peaks, scales = call(
+        score1_kernel, [((32, V), F32), ((32, 128), F32), ((40, 128), F32)], samp, *keeps[0],
+        grid_spec=scalar_spec(2, 3), flops=10**6, room=4,
+    )
+    peaks = call(score2_kernel, [((32, 128), F32)], *keeps[1], peaks, scales, flops=10**6, room=4)
     peaks = jnp.maximum(peaks, shift(peaks, "core", 1))
     perm_max = call(
         peak_kernel, [((PERMS, 32), F32)], peaks, *(shift(peaks, "zl", k) for k in (1, 2, 3)),

time: 129 us -> 126 us (0.977)
  waiting for transfers between devices: 39.2 us -> 37.4 us
    ppermute x32, waiting for transfers between devices: 39.2 us -> 37.4 us  [shift(): return lax.ppermute(value, axis, shifts(axis, k))]
    pallas_call x27 -> x29, Pallas kernels: 23.9 us -> 23.1 us  [call(): pl.pallas_call(kernel, out_shape=shapes[0] if single else shapes, cost_es...]
  transfers between devices with their start and end apart: 32 -> 32, of which waited for: 16 -> 17; matrix products, arithmetic and copies ran while one was open for 0% -> 0% of each run, Pallas kernels for 12% -> 13%
where the time goes in v1:
time: 126 us
  starting transfers between devices  64.4 us (51%)
  waiting for transfers between devices  37.4 us (30%)
  Pallas kernels  23.1 us (18%)
    ppermute x32, starting transfers between devices, shift(): return lax.ppermute(value, axis, shifts(axis, k))  64.4 us
    ppermute x32, waiting for transfers between devices, shift(): return lax.ppermute(value, axis, shifts(axis, k))  37.4 us
    pallas_call x29, Pallas kernels, call(): pl.pallas_call(kernel, out_shape=shapes[0] if single else shapes, cost_es...  23.1 us
  transfers between devices with their start and end apart: 32, of which 17 were waited for; matrix products, arithmetic and copies ran while one was open for 0% of the time, Pallas kernels for 13%

profile of v1, /device:TPU:1, one launch (start us, length us, event | category | flops | bytes accessed | tf_op | source)
XLA Modules:
  0.0 125.8 jit_solution(10612296649412014896)
XLA Ops:
  0.6 2.2 %shard_map.59 = (f32[232,128]{1,0:T(8,128)S(1)}, bf16[48,1024]{1,0:T(8,128)(2,1)S(1)}, bf16[1024,384]{1,0:T(8,128)(2,1)S(1)}) custom-call(s32[1]{0:T(128)} %bitcast.3.core_ref, bf16[1024,1024]{1,0:T(8,128)(2,1)} %traits_ref.3, bf16[32,1024]{1,0:T(8,128)(2,1)} %bitcast.10, s32[1024,256]{1,0:T(8,128)} %geno_ref.1), custom_call_target="tpu_custom_call" | custom-call | flops 234881024 | bytes 1003520 | tf_op jit(solution)/shard_map/pallas_call | solution.py:40
  2.8 2.1 %collective-permute-start = (f32[232,128]{1,0:T(8,128)S(1)}, f32[232,128]{1,0:T(8,128)S(1)}, u32[]{:S(2)}, u32[]{:S(2)}) collective-permute-start(f32[232,128]{1,0:T(8,128)S(1)} %get-tuple-element.46.after_ref.a), channel_id=1, source_target_pairs={{0,8},{8,16},{16,24},{24,0},{1,9},{9,17},{17,25},{25,1},{2,10},{10... | collective-permute-start | bytes 356360 | tf_op jit(solution)/shard_map/ppermute | solution.py:56
  4.9 2.5 %collective-permute-start.1 = (f32[232,128]{1,0:T(8,128)S(1)}, f32[232,128]{1,0:T(8,128)S(1)}, u32[]{:S(2)}, u32[]{:S(2)}) collective-permute-start(f32[232,128]{1,0:T(8,128)S(1)} %get-tuple-element.46.after_ref.a), channel_id=1, source_target_pairs={{0,16},{8,24},{16,0},{24,8},{1,17},{9,25},{17,1},{25,9},{2,18},{10... | collective-permute-start | bytes 356360 | tf_op jit(solution)/shard_map/ppermute | solution.py:56
  7.4 1.2 collective-permute-start.2
  8.6 3.8 %shard_map.60 = (bf16[3,1024,384]{2,1,0:T(8,128)(2,1)S(1)}, f32[8,128]{1,0:T(8,128)S(1)}) custom-call(s32[1]{0:T(128)S(6)} %mul.13.base_ref, s32[6,1,1024]{2,1,0:T(1,128)S(1)} %reshape.42.order_ref, bf16[1024,384]{1,0:T(8,128)(2,1)S(1)} %get-tuple-element.47.dx_ref, f32[232,128]{1,0:T(8,128)S(1)} %get-tuple-element.46.after_ref.a), custom_call_target="tpu_custom_call" | custom-call | flops 2415919104 | bytes 2363392 | tf_op jit(solution)/shard_map/pallas_call | solution.py:40
  12.4 0.2 collective-permute-done.1.c
  12.6 1.4 %collective-permute-start.3 = (f32[232,128]{1,0:T(8,128)S(1)}, f32[232,128]{1,0:T(8,128)S(1)}, u32[]{:S(2)}, u32[]{:S(2)}) collective-permute-start(f32[232,128]{1,0:T(8,128)S(1)} %shard_map.61.after_ref.a), channel_id=1, source_target_pairs={{0,64},{64,128},{128,192},{192,0},{1,65},{65,129},{129,193},{193,1... | collective-permute-start | bytes 356360 | tf_op jit(solution)/shard_map/ppermute | solution.py:56
  14.0 2.6 %collective-permute-start.4 = (f32[232,128]{1,0:T(8,128)S(1)}, f32[232,128]{1,0:T(8,128)S(1)}, u32[]{:S(2)}, u32[]{:S(2)}) collective-permute-start(f32[232,128]{1,0:T(8,128)S(1)} %shard_map.61.after_ref.a), channel_id=1, source_target_pairs={{0,128},{64,192},{128,0},{192,64},{1,129},{65,193},{129,1},{193,65... | collective-permute-start | bytes 356360 | tf_op jit(solution)/shard_map/ppermute | solution.py:56
  16.6 1.1 collective-permute-start.5
  17.7 2.5 %shard_map.62 = (bf16[2,1024,384]{2,1,0:T(8,128)(2,1)S(1)}, f32[8,128]{1,0:T(8,128)S(1)}) custom-call(s32[1]{0:T(128)S(6)} %mul.13.base_ref, s32[6,1,1024]{2,1,0:T(1,128)S(1)} %reshape.42.order_ref, bf16[1024,384]{1,0:T(8,128)(2,1)S(1)} %get-tuple-element.47.dx_ref, f32[232,128]{1,0:T(8,128)S(1)} %shard_map.61.after_ref.a), custom_call_target="tpu_custom_call" | custom-call | flops 1610612736 | bytes 1576960 | tf_op jit(solution)/shard_map/pallas_call | solution.py:40
  20.2 0.4 collective-permute-done.4.c
  20.6 0.7 collective-permute-done.5.d
  21.4 7.4 %collective-permute-start.6 = (f32[232,128]{1,0:T(8,128)S(1)}, f32[232,128]{1,0:T(8,128)S(1)}, u32[]{:S(2)}, u32[]{:S(2)}) collective-permute-start(f32[232,128]{1,0:T(8,128)S(1)} %shard_map.63.own_ref.after_ref), channel_id=1, source_target_pairs={{0,32},{32,0},{1,33},{33,1},{2,34},{34,2},{3,35},{35,3},{4,36},{36... | collective-permute-start | bytes 356360 | tf_op jit(solution)/shard_map/ppermute | solution.py:56
  28.7 1.1 shard_map.65.yt_ref
  29.9 1.2 collective-permute-done.6.far_ref
  31.1 1.7 %shard_map.64.own_ref = f32[40,768]{1,0:T(8,128)S(1)} custom-call(f32[232,128]{1,0:T(8,128)S(1)} %shard_map.63.own_ref.after_ref, f32[232,128]{1,0:T(8,128)S(1)} %collective-permute-done.6.far_ref), custom_call_target="tpu_custom_call" | custom-call | flops 100000000 | bytes 122880 | tf_op jit(solution)/shard_map/pallas_call | solution.py:40
  32.8 3.5 %collective-permute-start.7 = (f32[40,512]{1,0:T(8,128)S(1)}, f32[40,512]{1,0:T(8,128)S(1)}, u32[]{:S(2)}, u32[]{:S(2)}) collective-permute-start(f32[40,512]{1,0:T(8,128)S(1)} %slice.4), channel_id=1, source_target_pairs={{0,1},{1,0},{2,3},{3,2},{4,5},{5,4},{6,7},{7,6},{8,9},{9,8},{10,11... | collective-permute-start | bytes 245768 | tf_op jit(solution)/shard_map/ppermute | solution.py:56
  36.3 1.8 %shard_map.66 = (bf16[1,1024,384]{2,1,0:T(8,128)(2,1)S(1)}, f32[8,128]{1,0:T(8,128)}) custom-call(s32[1]{0:T(128)S(6)} %mul.13.base_ref, s32[6,1,1024]{2,1,0:T(1,128)S(1)} %reshape.42.order_ref, bf16[1024,384]{1,0:T(8,128)(2,1)S(1)} %get-tuple-element.47.dx_ref, f32[232,128]{1,0:T(8,128)S(1)} %shard_map.63.own_ref.after_ref), custom_call_target="tpu_custom_call" | custom-call | flops 805306368 | bytes 790528 | tf_op jit(solution)/shard_map/pallas_call | solution.py:40
  38.1 1.1 shard_map.67
  39.2 1.0 shard_map.68
  40.1 0.7 shard_map.69
  40.9 2.7 %collective-permute-start.12 = (f32[896,128]{1,0:T(8,128)S(1)}, f32[896,128]{1,0:T(8,128)S(1)}, u32[]{:S(2)}, u32[]{:S(2)}) collective-permute-start(f32[896,128]{1,0:T(8,128)S(1)} %get-tuple-element.59.after_ref), channel_id=1, source_target_pairs={{0,24},{8,0},{16,8},{24,16},{1,25},{9,1},{17,9},{25,17},{2,26},{10... | collective-permute-start | bytes 1376264 | tf_op jit(solution)/shard_map/ppermute | solution.py:56
  43.6 0.7 shard_map.70
  44.3 2.5 %collective-permute-start.22 = (f32[896,128]{1,0:T(8,128)S(1)}, f32[896,128]{1,0:T(8,128)S(1)}, u32[]{:S(2)}, u32[]{:S(2)}) collective-permute-start(f32[896,128]{1,0:T(8,128)S(1)} %get-tuple-element.60.after_ref), channel_id=1, source_target_pairs={{0,192},{64,0},{128,64},{192,128},{1,193},{65,1},{129,65},{193,129... | collective-permute-start | bytes 1376264 | tf_op jit(solution)/shard_map/ppermute | solution.py:56
  46.9 0.7 shard_map.71
  47.6 0.1 collective-permute-start.11
  47.7 0.7 shard_map.72
  48.4 0.7 shard_map.73
  49.1 0.7 shard_map.74
  49.8 0.7 shard_map.75
  50.6 2.9 %collective-permute-done.12.b = f32[896,128]{1,0:T(8,128)S(1)} collective-permute-done((f32[896,128]{1,0:T(8,128)S(1)}, f32[896,128]{1,0:T(8,128)S(1)}, u32[]{:S(2)}, u32[]{:S(2)}) %collective-permute-start.12) | collective-permute-done | bytes 458784 | tf_op jit(solution)/shard_map/ppermute | solution.py:56
  53.4 3.4 %collective-permute-start.8 = (f32[912,128]{1,0:T(8,128)S(1)}, f32[912,128]{1,0:T(8,128)S(1)}, u32[]{:S(2)}, u32[]{:S(2)}) collective-permute-start(f32[912,128]{1,0:T(8,128)S(1)} %get-tuple-element.66), channel_id=1, source_target_pairs={{0,24},{8,0},{16,8},{24,16},{1,25},{9,1},{17,9},{25,17},{2,26},{10... | collective-permute-start | bytes 1400840 | tf_op jit(solution)/shard_map/ppermute | solution.py:56
  56.9 0.7 shard_map.76
  57.8 1.5 %collective-permute-start.10 = (f32[912,128]{1,0:T(8,128)S(1)}, f32[912,128]{1,0:T(8,128)S(1)}, u32[]{:S(2)}, u32[]{:S(2)}) collective-permute-start(f32[912,128]{1,0:T(8,128)S(1)} %shard_map.77), channel_id=1, source_target_pairs={{0,8},{8,16},{16,24},{24,0},{1,9},{9,17},{17,25},{25,1},{2,10},{10... | collective-permute-start | bytes 1400840 | tf_op jit(solution)/shard_map/ppermute | solution.py:56
  59.3 0.2 collective-permute-done.19.b
  59.6 2.2 %collective-permute-start.18 = (f32[896,128]{1,0:T(8,128)S(1)}, f32[896,128]{1,0:T(8,128)S(1)}, u32[]{:S(2)}, u32[]{:S(2)}) collective-permute-start(f32[896,128]{1,0:T(8,128)S(1)} %get-tuple-element.79), channel_id=1, source_target_pairs={{0,192},{64,0},{128,64},{192,128},{1,193},{65,1},{129,65},{193,129... | collective-permute-start | bytes 1376264 | tf_op jit(solution)/shard_map/ppermute | solution.py:56
  61.8 4.8 %collective-permute-done.11.high_near = f32[896,128]{1,0:T(8,128)S(1)} collective-permute-done((f32[896,128]{1,0:T(8,128)S(1)}, f32[896,128]{1,0:T(8,128)S(1)}, u32[]{:S(2)}, u32[]{:S(2)}) %collective-permute-start.11) | collective-permute-done | bytes 458784 | tf_op jit(solution)/shard_map/ppermute | solution.py:56
  66.6 0.3 collective-permute-start.21
  67.0 2.5 %collective-permute-start.23 = (f32[896,128]{1,0:T(8,128)S(1)}, f32[896,128]{1,0:T(8,128)S(1)}, u32[]{:S(2)}, u32[]{:S(2)}) collective-permute-start(f32[896,128]{1,0:T(8,128)S(1)} %shard_map.83), channel_id=1, source_target_pairs={{0,192},{64,0},{128,64},{192,128},{1,193},{65,1},{129,65},{193,129... | collective-permute-start | bytes 1376264 | tf_op jit(solution)/shard_map/ppermute | solution.py:56
  69.5 6.4 %collective-permute-done.13.high_far = f32[896,128]{1,0:T(8,128)S(1)} collective-permute-done((f32[896,128]{1,0:T(8,128)S(1)}, f32[896,128]{1,0:T(8,128)S(1)}, u32[]{:S(2)}, u32[]{:S(2)}) %collective-permute-start.13) | collective-permute-done | bytes 458784 | tf_op jit(solution)/shard_map/ppermute | solution.py:56
  75.9 0.3 collective-permute-start.20
  76.1 0.5 collective-permute-done.10.low_far
  76.6 0.2 shard_map.79
  76.8 0.6 collective-permute-start.14
  77.4 3.1 %collective-permute-start.15 = (f32[464,128]{1,0:T(8,128)S(1)}, f32[464,128]{1,0:T(8,128)S(1)}, u32[]{:S(2)}, u32[]{:S(2)}) collective-permute-start(f32[464,128]{1,0:T(8,128)S(1)} %get-tuple-element.73), channel_id=1, source_target_pairs={{0,128},{64,192},{128,0},{192,64},{1,129},{65,193},{129,1},{193,65... | collective-permute-start | bytes 712712 | tf_op jit(solution)/shard_map/ppermute | solution.py:56
  80.5 1.4 %collective-permute-start.16 = (f32[464,128]{1,0:T(8,128)S(1)}, f32[464,128]{1,0:T(8,128)S(1)}, u32[]{:S(2)}, u32[]{:S(2)}) collective-permute-start(f32[464,128]{1,0:T(8,128)S(1)} %get-tuple-element.74), channel_id=1, source_target_pairs={{0,192},{64,0},{128,64},{192,128},{1,193},{65,1},{129,65},{193,129... | collective-permute-start | bytes 712712 | tf_op jit(solution)/shard_map/ppermute | solution.py:56
  81.9 6.6 %collective-permute-done.20.low_far = f32[896,128]{1,0:T(8,128)S(1)} collective-permute-done((f32[896,128]{1,0:T(8,128)S(1)}, f32[896,128]{1,0:T(8,128)S(1)}, u32[]{:S(2)}, u32[]{:S(2)}) %collective-permute-start.20) | collective-permute-done | bytes 458784 | tf_op jit(solution)/shard_map/ppermute | solution.py:56
  88.5 0.2 shard_map.84
  88.8 3.5 %collective-permute-start.25 = (f32[448,128]{1,0:T(8,128)S(1)}, f32[448,128]{1,0:T(8,128)S(1)}, u32[]{:S(2)}, u32[]{:S(2)}) collective-permute-start(f32[448,128]{1,0:T(8,128)S(1)} %get-tuple-element.84), channel_id=1, source_target_pairs={{0,16},{8,24},{16,0},{24,8},{1,17},{9,25},{17,1},{25,9},{2,18},{10... | collective-permute-start | bytes 688136 | tf_op jit(solution)/shard_map/ppermute | solution.py:56
  92.3 1.3 %collective-permute-done.14.b = f32[464,128]{1,0:T(8,128)S(1)} collective-permute-done((f32[464,128]{1,0:T(8,128)S(1)}, f32[464,128]{1,0:T(8,128)S(1)}, u32[]{:S(2)}, u32[]{:S(2)}) %collective-permute-start.14) | collective-permute-done | bytes 237600 | tf_op jit(solution)/shard_map/ppermute | solution.py:56
  93.6 2.3 %collective-permute-start.26 = (f32[448,128]{1,0:T(8,128)S(1)}, f32[448,128]{1,0:T(8,128)S(1)}, u32[]{:S(2)}, u32[]{:S(2)}) collective-permute-start(f32[448,128]{1,0:T(8,128)S(1)} %get-tuple-element.85), channel_id=1, source_target_pairs={{0,24},{8,0},{16,8},{24,16},{1,25},{9,1},{17,9},{25,17},{2,26},{10... | collective-permute-start | bytes 688136 | tf_op jit(solution)/shard_map/ppermute | solution.py:56
  95.9 3.7 %collective-permute-done.15.c = f32[464,128]{1,0:T(8,128)S(1)} collective-permute-done((f32[464,128]{1,0:T(8,128)S(1)}, f32[464,128]{1,0:T(8,128)S(1)}, u32[]{:S(2)}, u32[]{:S(2)}) %collective-permute-start.15) | collective-permute-done | bytes 237600 | tf_op jit(solution)/shard_map/ppermute | solution.py:56
  99.8 6.1 %collective-permute-start.17 = (f32[240,128]{1,0:T(8,128)S(1)}, f32[240,128]{1,0:T(8,128)S(1)}, u32[]{:S(2)}, u32[]{:S(2)}) collective-permute-start(f32[240,128]{1,0:T(8,128)S(1)} %get-tuple-element.76), channel_id=1, source_target_pairs={{0,32},{32,0},{1,33},{33,1},{2,34},{34,2},{3,35},{35,3},{4,36},{36... | collective-permute-start | bytes 368648 | tf_op jit(solution)/shard_map/ppermute | solution.py:56
  106.0 2.2 %collective-permute-start.27 = (f32[224,128]{1,0:T(8,128)S(1)}, f32[224,128]{1,0:T(8,128)S(1)}, u32[]{:S(2)}, u32[]{:S(2)}) collective-permute-start(f32[224,128]{1,0:T(8,128)S(1)} %get-tuple-element.87), channel_id=1, source_target_pairs={{0,32},{32,0},{1,33},{33,1},{2,34},{34,2},{3,35},{35,3},{4,36},{36... | collective-permute-start | bytes 344072 | tf_op jit(solution)/shard_map/ppermute | solution.py:56
  108.3 0.7 shard_map.81
  109.0 5.7 %collective-permute-done.27.got = f32[224,128]{1,0:T(8,128)S(1)} collective-permute-done((f32[224,128]{1,0:T(8,128)S(1)}, f32[224,128]{1,0:T(8,128)S(1)}, u32[]{:S(2)}, u32[]{:S(2)}) %collective-permute-start.27) | collective-permute-done | bytes 114720 | tf_op jit(solution)/shard_map/ppermute | solution.py:56
  114.7 0.1 shard_map.86
  114.8 4.5 %collective-permute-start.28 = (f32[32,128]{1,0:T(8,128)S(1)}, f32[32,128]{1,0:T(8,128)S(1)}, u32[]{:S(2)}, u32[]{:S(2)}) collective-permute-start(f32[32,128]{1,0:T(8,128)S(1)} %shard_map.86), channel_id=1, source_target_pairs={{0,1},{1,0},{2,3},{3,2},{4,5},{5,4},{6,7},{7,6},{8,9},{9,8},{10,11... | collective-permute-start | bytes 49160 | tf_op jit(solution)/shard_map/ppermute | solution.py:56
  119.3 0.8 collective-permute-done.28
  120.2 0.5 collective-permute-start.29
  120.7 2.8 %collective-permute-start.31 = (f32[32,128]{1,0:T(8,128)S(1)}, f32[32,128]{1,0:T(8,128)S(1)}, u32[]{:S(2)}, u32[]{:S(2)}) collective-permute-start(f32[32,128]{1,0:T(8,128)S(1)} %max.3.a), channel_id=1, source_target_pairs={{0,6},{2,0},{4,2},{6,4},{1,7},{3,1},{5,3},{7,5},{8,14},{10,8},{12,... | collective-permute-start | bytes 49160 | tf_op jit(solution)/shard_map/ppermute | solution.py:56
  123.4 1.1 collective-permute-done.29.b
  124.6 0.6 collective-permute-done.31.d
  125.1 0.7 shard_map.87
  (36 shorter events, 0.7 us)
Async XLA Ops:
  0.6 7.9 %copy-start.1 = (s32[6,1024]{1,0:T(8,128)S(1)}, s32[6,1024]{1,0:T(8,128)}, u32[]{:S(2)}) copy-start(s32[6,1024]{1,0:T(8,128)} %param.7) | copy-start | bytes 73732
  2.8 9.5 %collective-permute-start = (f32[232,128]{1,0:T(8,128)S(1)}, f32[232,128]{1,0:T(8,128)S(1)}, u32[]{:S(2)}, u32[]{:S(2)}) collective-permute-start(f32[232,128]{1,0:T(8,128)S(1)} %get-tuple-element.46.after_ref.a), channel_id=1, source_target_pairs={{0,8},{8,16},{16,24},{24,0},{1,9},{9,17},{17,25},{25,1},{2,10},{10... | collective-permute-start | bytes 356360 | tf_op jit(solution)/shard_map/ppermute | solution.py:56
  4.9 7.6 %collective-permute-start.1 = (f32[232,128]{1,0:T(8,128)S(1)}, f32[232,128]{1,0:T(8,128)S(1)}, u32[]{:S(2)}, u32[]{:S(2)}) collective-permute-start(f32[232,128]{1,0:T(8,128)S(1)} %get-tuple-element.46.after_ref.a), channel_id=1, source_target_pairs={{0,16},{8,24},{16,0},{24,8},{1,17},{9,25},{17,1},{25,9},{2,18},{10... | collective-permute-start | bytes 356360 | tf_op jit(solution)/shard_map/ppermute | solution.py:56
  7.4 5.2 %collective-permute-start.2 = (f32[232,128]{1,0:T(8,128)S(1)}, f32[232,128]{1,0:T(8,128)S(1)}, u32[]{:S(2)}, u32[]{:S(2)}) collective-permute-start(f32[232,128]{1,0:T(8,128)S(1)} %get-tuple-element.46.after_ref.a), channel_id=1, source_target_pairs={{0,24},{8,0},{16,8},{24,16},{1,25},{9,1},{17,9},{25,17},{2,26},{10... | collective-permute-start | bytes 356360 | tf_op jit(solution)/shard_map/ppermute | solution.py:56
  12.6 16.1 %copy-start = (bf16[1024,1024]{1,0:T(8,128)(2,1)S(1)}, bf16[1024,1024]{1,0:T(8,128)(2,1)}, u32[]{:S(2)}) copy-start(bf16[1024,1024]{1,0:T(8,128)(2,1)} %traits_ref.3) | copy-start | bytes 6291460
  12.6 7.6 %collective-permute-start.3 = (f32[232,128]{1,0:T(8,128)S(1)}, f32[232,128]{1,0:T(8,128)S(1)}, u32[]{:S(2)}, u32[]{:S(2)}) collective-permute-start(f32[232,128]{1,0:T(8,128)S(1)} %shard_map.61.after_ref.a), channel_id=1, source_target_pairs={{0,64},{64,128},{128,192},{192,0},{1,65},{65,129},{129,193},{193,1... | collective-permute-start | bytes 356360 | tf_op jit(solution)/shard_map/ppermute | solution.py:56
  14.0 6.7 %collective-permute-start.4 = (f32[232,128]{1,0:T(8,128)S(1)}, f32[232,128]{1,0:T(8,128)S(1)}, u32[]{:S(2)}, u32[]{:S(2)}) collective-permute-start(f32[232,128]{1,0:T(8,128)S(1)} %shard_map.61.after_ref.a), channel_id=1, source_target_pairs={{0,128},{64,192},{128,0},{192,64},{1,129},{65,193},{129,1},{193,65... | collective-permute-start | bytes 356360 | tf_op jit(solution)/shard_map/ppermute | solution.py:56
  16.6 4.7 %collective-permute-start.5 = (f32[232,128]{1,0:T(8,128)S(1)}, f32[232,128]{1,0:T(8,128)S(1)}, u32[]{:S(2)}, u32[]{:S(2)}) collective-permute-start(f32[232,128]{1,0:T(8,128)S(1)} %shard_map.61.after_ref.a), channel_id=1, source_target_pairs={{0,192},{64,0},{128,64},{192,128},{1,193},{65,1},{129,65},{193,129... | collective-permute-start | bytes 356360 | tf_op jit(solution)/shard_map/ppermute | solution.py:56
  21.4 9.7 %collective-permute-start.6 = (f32[232,128]{1,0:T(8,128)S(1)}, f32[232,128]{1,0:T(8,128)S(1)}, u32[]{:S(2)}, u32[]{:S(2)}) collective-permute-start(f32[232,128]{1,0:T(8,128)S(1)} %shard_map.63.own_ref.after_ref), channel_id=1, source_target_pairs={{0,32},{32,0},{1,33},{33,1},{2,34},{34,2},{3,35},{35,3},{4,36},{36... | collective-permute-start | bytes 356360 | tf_op jit(solution)/shard_map/ppermute | solution.py:56
  32.8 6.4 %collective-permute-start.7 = (f32[40,512]{1,0:T(8,128)S(1)}, f32[40,512]{1,0:T(8,128)S(1)}, u32[]{:S(2)}, u32[]{:S(2)}) collective-permute-start(f32[40,512]{1,0:T(8,128)S(1)} %slice.4), channel_id=1, source_target_pairs={{0,1},{1,0},{2,3},{3,2},{4,5},{5,4},{6,7},{7,6},{8,9},{9,8},{10,11... | collective-permute-start | bytes 245768 | tf_op jit(solution)/shard_map/ppermute | solution.py:56
  40.9 12.6 %collective-permute-start.12 = (f32[896,128]{1,0:T(8,128)S(1)}, f32[896,128]{1,0:T(8,128)S(1)}, u32[]{:S(2)}, u32[]{:S(2)}) collective-permute-start(f32[896,128]{1,0:T(8,128)S(1)} %get-tuple-element.59.after_ref), channel_id=1, source_target_pairs={{0,24},{8,0},{16,8},{24,16},{1,25},{9,1},{17,9},{25,17},{2,26},{10... | collective-permute-start | bytes 1376264 | tf_op jit(solution)/shard_map/ppermute | solution.py:56
  43.6 14.1 %collective-permute-start.9 = (f32[912,128]{1,0:T(8,128)S(1)}, f32[912,128]{1,0:T(8,128)S(1)}, u32[]{:S(2)}, u32[]{:S(2)}) collective-permute-start(f32[912,128]{1,0:T(8,128)S(1)} %get-tuple-element.68), channel_id=1, source_target_pairs={{0,8},{8,16},{16,24},{24,0},{1,9},{9,17},{17,25},{25,1},{2,10},{10... | collective-permute-start | bytes 1400840 | tf_op jit(solution)/shard_map/ppermute | solution.py:56
  44.3 13.5 %collective-permute-start.22 = (f32[896,128]{1,0:T(8,128)S(1)}, f32[896,128]{1,0:T(8,128)S(1)}, u32[]{:S(2)}, u32[]{:S(2)}) collective-permute-start(f32[896,128]{1,0:T(8,128)S(1)} %get-tuple-element.60.after_ref), channel_id=1, source_target_pairs={{0,192},{64,0},{128,64},{192,128},{1,193},{65,1},{129,65},{193,129... | collective-permute-start | bytes 1376264 | tf_op jit(solution)/shard_map/ppermute | solution.py:56
  46.9 12.7 %collective-permute-start.19 = (f32[896,128]{1,0:T(8,128)S(1)}, f32[896,128]{1,0:T(8,128)S(1)}, u32[]{:S(2)}, u32[]{:S(2)}) collective-permute-start(f32[896,128]{1,0:T(8,128)S(1)} %get-tuple-element.81), channel_id=1, source_target_pairs={{0,64},{64,128},{128,192},{192,0},{1,65},{65,129},{129,193},{193,1... | collective-permute-start | bytes 1376264 | tf_op jit(solution)/shard_map/ppermute | solution.py:56
  47.6 19.0 %collective-permute-start.11 = (f32[896,128]{1,0:T(8,128)S(1)}, f32[896,128]{1,0:T(8,128)S(1)}, u32[]{:S(2)}, u32[]{:S(2)}) collective-permute-start(f32[896,128]{1,0:T(8,128)S(1)} %get-tuple-element.61.after_ref), channel_id=1, source_target_pairs={{0,8},{8,16},{16,24},{24,0},{1,9},{9,17},{17,25},{25,1},{2,10},{10... | collective-permute-start | bytes 1376264 | tf_op jit(solution)/shard_map/ppermute | solution.py:56
  53.4 13.5 %collective-permute-start.8 = (f32[912,128]{1,0:T(8,128)S(1)}, f32[912,128]{1,0:T(8,128)S(1)}, u32[]{:S(2)}, u32[]{:S(2)}) collective-permute-start(f32[912,128]{1,0:T(8,128)S(1)} %get-tuple-element.66), channel_id=1, source_target_pairs={{0,24},{8,0},{16,8},{24,16},{1,25},{9,1},{17,9},{25,17},{2,26},{10... | collective-permute-start | bytes 1400840 | tf_op jit(solution)/shard_map/ppermute | solution.py:56
  57.7 18.2 %collective-permute-start.13 = (f32[896,128]{1,0:T(8,128)S(1)}, f32[896,128]{1,0:T(8,128)S(1)}, u32[]{:S(2)}, u32[]{:S(2)}) collective-permute-start(f32[896,128]{1,0:T(8,128)S(1)} %shard_map.78), channel_id=1, source_target_pairs={{0,24},{8,0},{16,8},{24,16},{1,25},{9,1},{17,9},{25,17},{2,26},{10... | collective-permute-start | bytes 1376264 | tf_op jit(solution)/shard_map/ppermute | solution.py:56
  57.8 18.8 %collective-permute-start.10 = (f32[912,128]{1,0:T(8,128)S(1)}, f32[912,128]{1,0:T(8,128)S(1)}, u32[]{:S(2)}, u32[]{:S(2)}) collective-permute-start(f32[912,128]{1,0:T(8,128)S(1)} %shard_map.77), channel_id=1, source_target_pairs={{0,8},{8,16},{16,24},{24,0},{1,9},{9,17},{17,25},{25,1},{2,10},{10... | collective-permute-start | bytes 1400840 | tf_op jit(solution)/shard_map/ppermute | solution.py:56
  59.6 17.9 %collective-permute-start.18 = (f32[896,128]{1,0:T(8,128)S(1)}, f32[896,128]{1,0:T(8,128)S(1)}, u32[]{:S(2)}, u32[]{:S(2)}) collective-permute-start(f32[896,128]{1,0:T(8,128)S(1)} %get-tuple-element.79), channel_id=1, source_target_pairs={{0,192},{64,0},{128,64},{192,128},{1,193},{65,1},{129,65},{193,129... | collective-permute-start | bytes 1376264 | tf_op jit(solution)/shard_map/ppermute | solution.py:56
  66.6 13.9 %collective-permute-start.21 = (f32[896,128]{1,0:T(8,128)S(1)}, f32[896,128]{1,0:T(8,128)S(1)}, u32[]{:S(2)}, u32[]{:S(2)}) collective-permute-start(f32[896,128]{1,0:T(8,128)S(1)} %get-tuple-element.62.after_ref), channel_id=1, source_target_pairs={{0,64},{64,128},{128,192},{192,0},{1,65},{65,129},{129,193},{193,1... | collective-permute-start | bytes 1376264 | tf_op jit(solution)/shard_map/ppermute | solution.py:56
  67.0 14.9 %collective-permute-start.23 = (f32[896,128]{1,0:T(8,128)S(1)}, f32[896,128]{1,0:T(8,128)S(1)}, u32[]{:S(2)}, u32[]{:S(2)}) collective-permute-start(f32[896,128]{1,0:T(8,128)S(1)} %shard_map.83), channel_id=1, source_target_pairs={{0,192},{64,0},{128,64},{192,128},{1,193},{65,1},{129,65},{193,129... | collective-permute-start | bytes 1376264 | tf_op jit(solution)/shard_map/ppermute | solution.py:56
  75.9 12.6 %collective-permute-start.20 = (f32[896,128]{1,0:T(8,128)S(1)}, f32[896,128]{1,0:T(8,128)S(1)}, u32[]{:S(2)}, u32[]{:S(2)}) collective-permute-start(f32[896,128]{1,0:T(8,128)S(1)} %shard_map.82), channel_id=1, source_target_pairs={{0,64},{64,128},{128,192},{192,0},{1,65},{65,129},{129,193},{193,1... | collective-permute-start | bytes 1376264 | tf_op jit(solution)/shard_map/ppermute | solution.py:56
  76.8 16.8 %collective-permute-start.14 = (f32[464,128]{1,0:T(8,128)S(1)}, f32[464,128]{1,0:T(8,128)S(1)}, u32[]{:S(2)}, u32[]{:S(2)}) collective-permute-start(f32[464,128]{1,0:T(8,128)S(1)} %get-tuple-element.72), channel_id=1, source_target_pairs={{0,64},{64,128},{128,192},{192,0},{1,65},{65,129},{129,193},{193,1... | collective-permute-start | bytes 712712 | tf_op jit(solution)/shard_map/ppermute | solution.py:56
  77.4 22.2 %collective-permute-start.15 = (f32[464,128]{1,0:T(8,128)S(1)}, f32[464,128]{1,0:T(8,128)S(1)}, u32[]{:S(2)}, u32[]{:S(2)}) collective-permute-start(f32[464,128]{1,0:T(8,128)S(1)} %get-tuple-element.73), channel_id=1, source_target_pairs={{0,128},{64,192},{128,0},{192,64},{1,129},{65,193},{129,1},{193,65... | collective-permute-start | bytes 712712 | tf_op jit(solution)/shard_map/ppermute | solution.py:56
  80.5 19.1 %collective-permute-start.16 = (f32[464,128]{1,0:T(8,128)S(1)}, f32[464,128]{1,0:T(8,128)S(1)}, u32[]{:S(2)}, u32[]{:S(2)}) collective-permute-start(f32[464,128]{1,0:T(8,128)S(1)} %get-tuple-element.74), channel_id=1, source_target_pairs={{0,192},{64,0},{128,64},{192,128},{1,193},{65,1},{129,65},{193,129... | collective-permute-start | bytes 712712 | tf_op jit(solution)/shard_map/ppermute | solution.py:56
  88.7 17.2 %collective-permute-start.24 = (f32[448,128]{1,0:T(8,128)S(1)}, f32[448,128]{1,0:T(8,128)S(1)}, u32[]{:S(2)}, u32[]{:S(2)}) collective-permute-start(f32[448,128]{1,0:T(8,128)S(1)} %get-tuple-element.83), channel_id=1, source_target_pairs={{0,8},{8,16},{16,24},{24,0},{1,9},{9,17},{17,25},{25,1},{2,10},{10... | collective-permute-start | bytes 688136 | tf_op jit(solution)/shard_map/ppermute | solution.py:56
  88.8 17.1 %collective-permute-start.25 = (f32[448,128]{1,0:T(8,128)S(1)}, f32[448,128]{1,0:T(8,128)S(1)}, u32[]{:S(2)}, u32[]{:S(2)}) collective-permute-start(f32[448,128]{1,0:T(8,128)S(1)} %get-tuple-element.84), channel_id=1, source_target_pairs={{0,16},{8,24},{16,0},{24,8},{1,17},{9,25},{17,1},{25,9},{2,18},{10... | collective-permute-start | bytes 688136 | tf_op jit(solution)/shard_map/ppermute | solution.py:56
  93.6 12.3 %collective-permute-start.26 = (f32[448,128]{1,0:T(8,128)S(1)}, f32[448,128]{1,0:T(8,128)S(1)}, u32[]{:S(2)}, u32[]{:S(2)}) collective-permute-start(f32[448,128]{1,0:T(8,128)S(1)} %get-tuple-element.85), channel_id=1, source_target_pairs={{0,24},{8,0},{16,8},{24,16},{1,25},{9,1},{17,9},{25,17},{2,26},{10... | collective-permute-start | bytes 688136 | tf_op jit(solution)/shard_map/ppermute | solution.py:56
  99.8 8.5 %collective-permute-start.17 = (f32[240,128]{1,0:T(8,128)S(1)}, f32[240,128]{1,0:T(8,128)S(1)}, u32[]{:S(2)}, u32[]{:S(2)}) collective-permute-start(f32[240,128]{1,0:T(8,128)S(1)} %get-tuple-element.76), channel_id=1, source_target_pairs={{0,32},{32,0},{1,33},{33,1},{2,34},{34,2},{3,35},{35,3},{4,36},{36... | collective-permute-start | bytes 368648 | tf_op jit(solution)/shard_map/ppermute | solution.py:56
  106.0 8.7 %collective-permute-start.27 = (f32[224,128]{1,0:T(8,128)S(1)}, f32[224,128]{1,0:T(8,128)S(1)}, u32[]{:S(2)}, u32[]{:S(2)}) collective-permute-start(f32[224,128]{1,0:T(8,128)S(1)} %get-tuple-element.87), channel_id=1, source_target_pairs={{0,32},{32,0},{1,33},{33,1},{2,34},{34,2},{3,35},{35,3},{4,36},{36... | collective-permute-start | bytes 344072 | tf_op jit(solution)/shard_map/ppermute | solution.py:56
  114.8 5.4 %collective-permute-start.28 = (f32[32,128]{1,0:T(8,128)S(1)}, f32[32,128]{1,0:T(8,128)S(1)}, u32[]{:S(2)}, u32[]{:S(2)}) collective-permute-start(f32[32,128]{1,0:T(8,128)S(1)} %shard_map.86), channel_id=1, source_target_pairs={{0,1},{1,0},{2,3},{3,2},{4,5},{5,4},{6,7},{7,6},{8,9},{9,8},{10,11... | collective-permute-start | bytes 49160 | tf_op jit(solution)/shard_map/ppermute | solution.py:56
  120.2 4.4 %collective-permute-start.29 = (f32[32,128]{1,0:T(8,128)S(1)}, f32[32,128]{1,0:T(8,128)S(1)}, u32[]{:S(2)}, u32[]{:S(2)}) collective-permute-start(f32[32,128]{1,0:T(8,128)S(1)} %max.3.a), channel_id=1, source_target_pairs={{0,2},{2,4},{4,6},{6,0},{1,3},{3,5},{5,7},{7,1},{8,10},{10,12},{12... | collective-permute-start | bytes 49160 | tf_op jit(solution)/shard_map/ppermute | solution.py:56
  120.7 3.9 %collective-permute-start.30 = (f32[32,128]{1,0:T(8,128)S(1)}, f32[32,128]{1,0:T(8,128)S(1)}, u32[]{:S(2)}, u32[]{:S(2)}) collective-permute-start(f32[32,128]{1,0:T(8,128)S(1)} %max.3.a), channel_id=1, source_target_pairs={{0,4},{2,6},{4,0},{6,2},{1,5},{3,7},{5,1},{7,3},{8,12},{10,14},{12... | collective-permute-start | bytes 49160 | tf_op jit(solution)/shard_map/ppermute | solution.py:56
  120.7 4.5 %collective-permute-start.31 = (f32[32,128]{1,0:T(8,128)S(1)}, f32[32,128]{1,0:T(8,128)S(1)}, u32[]{:S(2)}, u32[]{:S(2)}) collective-permute-start(f32[32,128]{1,0:T(8,128)S(1)} %max.3.a), channel_id=1, source_target_pairs={{0,6},{2,0},{4,2},{6,4},{1,7},{3,1},{5,3},{7,5},{8,14},{10,8},{12,... | collective-permute-start | bytes 49160 | tf_op jit(solution)/shard_map/ppermute | solution.py:56

commit v2 on v1

--- a/solution.py
+++ b/solution.py
@@ -111,6 +111,12 @@
     def line_of(part, line):
         return jnp.broadcast_to(part[line : line + 1], wide)
 
+    ones = [jnp.broadcast_to(part[BLOCKS][:, C : C + 1], wide) + zero for part in m]
+    inverse = 1.0 / line_of(ones[-1], 0)
+    for j in range(BLOCKS + 1):
+        row = line_of(m[-1][j], 0) * inverse
+        for g in range(len(m)):
+            m[g][j] = m[g][j] - ones[g] * row if g < C // 8 else row
     for k in range(0, C, 2):
         here, line = k // 8, k % 8
         left = [jnp.broadcast_to(part[BLOCKS][:, k : k + 1], wide) + zero for part in m]
@@ -127,12 +133,6 @@
                 if g == here:
                     rest = jnp.where(row_id == line, top, jnp.where(row_id == line + 1, low, rest))
                 m[g][j] = rest
-    last = [jnp.broadcast_to(part[BLOCKS][:, C : C + 1], wide) + zero for part in m]
-    inverse = 1.0 / line_of(last[-1], 0)
-    for j in range(BLOCKS):
-        row = line_of(m[-1][j], 0) * inverse
-        for g in range(len(m)):
-            m[g][j] = m[g][j] - last[g] * row if g < C // 8 else row
     for g in range(len(m)):
         for j in range(BLOCKS):
             done = m[g][j] if g < C // 8 else jnp.where(row_id == 0, m[g][j], 0.0)
@@ -270,13 +270,12 @@
         if part is not None:
             best = jnp.max(part, axis=1, keepdims=True)
             out = jnp.where(lane == p, jnp.maximum(out, best), out)
-    peak_ref[...] = out
+    peak_ref[...] = jnp.transpose(jnp.concatenate([out, jnp.zeros((96, 128), F32)], axis=0))[:8]
 
 
 def peak_kernel(a, b, c, d, out_ref):
     best = jnp.maximum(jnp.maximum(a[...], b[...]), jnp.maximum(c[...], d[...]))
-    full = jnp.concatenate([best, jnp.zeros((96, 128), F32)], axis=0)
-    out_ref[...] = jnp.transpose(full)[:PERMS, :32]
+    out_ref[...] = best[:PERMS, :32]
 
 
 def scalar_spec(n_in, n_out, grid=(1,)):
@@ -421,7 +420,7 @@
 
     part, got = {}, {}
     after = ss
-    for k in (2, 1, 3, 0):
+    for k in (2, 3, 1, 0):
         for axis in ("x", "y"):
             part[axis, k] = cross(axis, k, after)
             after = part[axis, k][1]
@@ -469,7 +468,7 @@
         score1_kernel, [((32, V), F32), ((32, 128), F32), ((40, 128), F32)], samp, *keeps[0],
         grid_spec=scalar_spec(2, 3), flops=10**6, room=4,
     )
-    peaks = call(score2_kernel, [((32, 128), F32)], *keeps[1], peaks, scales, flops=10**6, room=4)
+    peaks = call(score2_kernel, [((8, 128), F32)], *keeps[1], peaks, scales, flops=10**6, room=4)
     peaks = jnp.maximum(peaks, shift(peaks, "core", 1))
     perm_max = call(
         peak_kernel, [((PERMS, 32), F32)], peaks, *(shift(peaks, "zl", k) for k in (1, 2, 3)),

time: 126 us -> 126 us (level)
  transfers between devices with their start and end apart: 32 -> 32, of which waited for: 17 -> 16; matrix products, arithmetic and copies ran while one was open for 0% -> 0% of each run, Pallas kernels for 13% -> 13%
where the time goes in v2:
time: 126 us; the launch traced here: 125 us
  starting transfers between devices  63.4 us (50%)
  waiting for transfers between devices  37.9 us (30%)
  Pallas kernels  23.1 us (18%)
    ppermute x32, starting transfers between devices, shift(): return lax.ppermute(value, axis, shifts(axis, k))  63.4 us
    ppermute x32, waiting for transfers between devices, shift(): return lax.ppermute(value, axis, shifts(axis, k))  37.9 us
    pallas_call x29, Pallas kernels, call(): pl.pallas_call(kernel, out_shape=shapes[0] if single else shapes, cost_es...  23.1 us
  transfers between devices with their start and end apart: 32, of which 16 were waited for; matrix products, arithmetic and copies ran while one was open for 0% of the time, Pallas kernels for 13%

profile of v2, /device:TPU:1, one launch (start us, length us, event | category | flops | bytes accessed | tf_op | source)
XLA Modules:
  0.0 125.4 jit_solution(3428835954129894125)
XLA Ops:
  0.6 2.2 %shard_map.59 = (f32[232,128]{1,0:T(8,128)S(1)}, bf16[48,1024]{1,0:T(8,128)(2,1)S(1)}, bf16[1024,384]{1,0:T(8,128)(2,1)S(1)}) custom-call(s32[1]{0:T(128)} %bitcast.3.core_ref, bf16[1024,1024]{1,0:T(8,128)(2,1)} %traits_ref.3, bf16[32,1024]{1,0:T(8,128)(2,1)} %bitcast.10, s32[1024,256]{1,0:T(8,128)} %geno_ref.1), custom_call_target="tpu_custom_call" | custom-call | flops 234881024 | bytes 1003520 | tf_op jit(solution)/shard_map/pallas_call | solution.py:40
  2.8 2.1 %collective-permute-start = (f32[232,128]{1,0:T(8,128)S(1)}, f32[232,128]{1,0:T(8,128)S(1)}, u32[]{:S(2)}, u32[]{:S(2)}) collective-permute-start(f32[232,128]{1,0:T(8,128)S(1)} %get-tuple-element.46.after_ref.a), channel_id=1, source_target_pairs={{0,8},{8,16},{16,24},{24,0},{1,9},{9,17},{17,25},{25,1},{2,10},{10... | collective-permute-start | bytes 356360 | tf_op jit(solution)/shard_map/ppermute | solution.py:56
  4.9 2.5 %collective-permute-start.1 = (f32[232,128]{1,0:T(8,128)S(1)}, f32[232,128]{1,0:T(8,128)S(1)}, u32[]{:S(2)}, u32[]{:S(2)}) collective-permute-start(f32[232,128]{1,0:T(8,128)S(1)} %get-tuple-element.46.after_ref.a), channel_id=1, source_target_pairs={{0,16},{8,24},{16,0},{24,8},{1,17},{9,25},{17,1},{25,9},{2,18},{10... | collective-permute-start | bytes 356360 | tf_op jit(solution)/shard_map/ppermute | solution.py:56
  7.4 1.2 collective-permute-start.2
  8.6 3.8 %shard_map.60 = (bf16[3,1024,384]{2,1,0:T(8,128)(2,1)S(1)}, f32[8,128]{1,0:T(8,128)S(1)}) custom-call(s32[1]{0:T(128)S(6)} %mul.13.base_ref, s32[6,1,1024]{2,1,0:T(1,128)S(1)} %reshape.42.order_ref, bf16[1024,384]{1,0:T(8,128)(2,1)S(1)} %get-tuple-element.47.dx_ref, f32[232,128]{1,0:T(8,128)S(1)} %get-tuple-element.46.after_ref.a), custom_call_target="tpu_custom_call" | custom-call | flops 2415919104 | bytes 2363392 | tf_op jit(solution)/shard_map/pallas_call | solution.py:40
  12.4 0.2 collective-permute-done.1.c
  12.6 1.4 %collective-permute-start.3 = (f32[232,128]{1,0:T(8,128)S(1)}, f32[232,128]{1,0:T(8,128)S(1)}, u32[]{:S(2)}, u32[]{:S(2)}) collective-permute-start(f32[232,128]{1,0:T(8,128)S(1)} %shard_map.61.after_ref.a), channel_id=1, source_target_pairs={{0,64},{64,128},{128,192},{192,0},{1,65},{65,129},{129,193},{193,1... | collective-permute-start | bytes 356360 | tf_op jit(solution)/shard_map/ppermute | solution.py:56
  14.0 2.6 %collective-permute-start.4 = (f32[232,128]{1,0:T(8,128)S(1)}, f32[232,128]{1,0:T(8,128)S(1)}, u32[]{:S(2)}, u32[]{:S(2)}) collective-permute-start(f32[232,128]{1,0:T(8,128)S(1)} %shard_map.61.after_ref.a), channel_id=1, source_target_pairs={{0,128},{64,192},{128,0},{192,64},{1,129},{65,193},{129,1},{193,65... | collective-permute-start | bytes 356360 | tf_op jit(solution)/shard_map/ppermute | solution.py:56
  16.6 1.1 collective-permute-start.5
  17.7 2.5 %shard_map.62 = (bf16[2,1024,384]{2,1,0:T(8,128)(2,1)S(1)}, f32[8,128]{1,0:T(8,128)S(1)}) custom-call(s32[1]{0:T(128)S(6)} %mul.13.base_ref, s32[6,1,1024]{2,1,0:T(1,128)S(1)} %reshape.42.order_ref, bf16[1024,384]{1,0:T(8,128)(2,1)S(1)} %get-tuple-element.47.dx_ref, f32[232,128]{1,0:T(8,128)S(1)} %shard_map.61.after_ref.a), custom_call_target="tpu_custom_call" | custom-call | flops 1610612736 | bytes 1576960 | tf_op jit(solution)/shard_map/pallas_call | solution.py:40
  20.2 0.4 collective-permute-done.4.c
  20.6 0.7 collective-permute-done.5.d
  21.4 7.4 %collective-permute-start.6 = (f32[232,128]{1,0:T(8,128)S(1)}, f32[232,128]{1,0:T(8,128)S(1)}, u32[]{:S(2)}, u32[]{:S(2)}) collective-permute-start(f32[232,128]{1,0:T(8,128)S(1)} %shard_map.63.own_ref.after_ref), channel_id=1, source_target_pairs={{0,32},{32,0},{1,33},{33,1},{2,34},{34,2},{3,35},{35,3},{4,36},{36... | collective-permute-start | bytes 356360 | tf_op jit(solution)/shard_map/ppermute | solution.py:56
  28.7 1.1 shard_map.65.yt_ref
  29.9 1.2 collective-permute-done.6.far_ref
  31.1 1.7 %shard_map.64.own_ref = f32[40,768]{1,0:T(8,128)S(1)} custom-call(f32[232,128]{1,0:T(8,128)S(1)} %shard_map.63.own_ref.after_ref, f32[232,128]{1,0:T(8,128)S(1)} %collective-permute-done.6.far_ref), custom_call_target="tpu_custom_call" | custom-call | flops 100000000 | bytes 122880 | tf_op jit(solution)/shard_map/pallas_call | solution.py:40
  32.8 3.5 %collective-permute-start.7 = (f32[40,512]{1,0:T(8,128)S(1)}, f32[40,512]{1,0:T(8,128)S(1)}, u32[]{:S(2)}, u32[]{:S(2)}) collective-permute-start(f32[40,512]{1,0:T(8,128)S(1)} %slice.4), channel_id=1, source_target_pairs={{0,1},{1,0},{2,3},{3,2},{4,5},{5,4},{6,7},{7,6},{8,9},{9,8},{10,11... | collective-permute-start | bytes 245768 | tf_op jit(solution)/shard_map/ppermute | solution.py:56
  36.3 1.8 %shard_map.66 = (bf16[1,1024,384]{2,1,0:T(8,128)(2,1)S(1)}, f32[8,128]{1,0:T(8,128)}) custom-call(s32[1]{0:T(128)S(6)} %mul.13.base_ref, s32[6,1,1024]{2,1,0:T(1,128)S(1)} %reshape.42.order_ref, bf16[1024,384]{1,0:T(8,128)(2,1)S(1)} %get-tuple-element.47.dx_ref, f32[232,128]{1,0:T(8,128)S(1)} %shard_map.63.own_ref.after_ref), custom_call_target="tpu_custom_call" | custom-call | flops 805306368 | bytes 790528 | tf_op jit(solution)/shard_map/pallas_call | solution.py:40
  38.1 1.1 shard_map.67
  39.2 1.0 shard_map.68
  40.2 0.7 shard_map.69
  40.9 2.7 %collective-permute-start.12 = (f32[896,128]{1,0:T(8,128)S(1)}, f32[896,128]{1,0:T(8,128)S(1)}, u32[]{:S(2)}, u32[]{:S(2)}) collective-permute-start(f32[896,128]{1,0:T(8,128)S(1)} %get-tuple-element.59.after_ref), channel_id=1, source_target_pairs={{0,24},{8,0},{16,8},{24,16},{1,25},{9,1},{17,9},{25,17},{2,26},{10... | collective-permute-start | bytes 1376264 | tf_op jit(solution)/shard_map/ppermute | solution.py:56
  43.6 0.7 shard_map.70
  44.4 2.5 %collective-permute-start.22 = (f32[896,128]{1,0:T(8,128)S(1)}, f32[896,128]{1,0:T(8,128)S(1)}, u32[]{:S(2)}, u32[]{:S(2)}) collective-permute-start(f32[896,128]{1,0:T(8,128)S(1)} %get-tuple-element.60.after_ref), channel_id=1, source_target_pairs={{0,192},{64,0},{128,64},{192,128},{1,193},{65,1},{129,65},{193,129... | collective-permute-start | bytes 1376264 | tf_op jit(solution)/shard_map/ppermute | solution.py:56
  46.9 0.7 shard_map.71
  47.6 0.7 shard_map.72
  48.3 0.7 shard_map.73
  49.0 0.1 collective-permute-start.11
  49.1 0.7 shard_map.74
  49.9 0.7 shard_map.75
  50.6 2.9 %collective-permute-done.12.b = f32[896,128]{1,0:T(8,128)S(1)} collective-permute-done((f32[896,128]{1,0:T(8,128)S(1)}, f32[896,128]{1,0:T(8,128)S(1)}, u32[]{:S(2)}, u32[]{:S(2)}) %collective-permute-start.12) | collective-permute-done | bytes 458784 | tf_op jit(solution)/shard_map/ppermute | solution.py:56
  53.5 3.4 %collective-permute-start.8 = (f32[912,128]{1,0:T(8,128)S(1)}, f32[912,128]{1,0:T(8,128)S(1)}, u32[]{:S(2)}, u32[]{:S(2)}) collective-permute-start(f32[912,128]{1,0:T(8,128)S(1)} %get-tuple-element.66), channel_id=1, source_target_pairs={{0,24},{8,0},{16,8},{24,16},{1,25},{9,1},{17,9},{25,17},{2,26},{10... | collective-permute-start | bytes 1400840 | tf_op jit(solution)/shard_map/ppermute | solution.py:56
  56.9 0.7 shard_map.76
  57.7 0.1 collective-permute-start.13
  57.9 1.5 %collective-permute-start.10 = (f32[912,128]{1,0:T(8,128)S(1)}, f32[912,128]{1,0:T(8,128)S(1)}, u32[]{:S(2)}, u32[]{:S(2)}) collective-permute-start(f32[912,128]{1,0:T(8,128)S(1)} %shard_map.77), channel_id=1, source_target_pairs={{0,8},{8,16},{16,24},{24,0},{1,9},{9,17},{17,25},{25,1},{2,10},{10... | collective-permute-start | bytes 1400840 | tf_op jit(solution)/shard_map/ppermute | solution.py:56
  59.4 0.2 collective-permute-done.19.b
  59.7 7.0 %collective-permute-done.11.high_near = f32[896,128]{1,0:T(8,128)S(1)} collective-permute-done((f32[896,128]{1,0:T(8,128)S(1)}, f32[896,128]{1,0:T(8,128)S(1)}, u32[]{:S(2)}, u32[]{:S(2)}) %collective-permute-start.11) | collective-permute-done | bytes 458784 | tf_op jit(solution)/shard_map/ppermute | solution.py:56
  66.6 2.4 %collective-permute-start.18 = (f32[896,128]{1,0:T(8,128)S(1)}, f32[896,128]{1,0:T(8,128)S(1)}, u32[]{:S(2)}, u32[]{:S(2)}) collective-permute-start(f32[896,128]{1,0:T(8,128)S(1)} %get-tuple-element.79), channel_id=1, source_target_pairs={{0,192},{64,0},{128,64},{192,128},{1,193},{65,1},{129,65},{193,129... | collective-permute-start | bytes 1376264 | tf_op jit(solution)/shard_map/ppermute | solution.py:56
  69.3 6.6 %collective-permute-done.13.high_far = f32[896,128]{1,0:T(8,128)S(1)} collective-permute-done((f32[896,128]{1,0:T(8,128)S(1)}, f32[896,128]{1,0:T(8,128)S(1)}, u32[]{:S(2)}, u32[]{:S(2)}) %collective-permute-start.13) | collective-permute-done | bytes 458784 | tf_op jit(solution)/shard_map/ppermute | solution.py:56
  75.9 0.3 collective-permute-start.20
  76.2 0.5 collective-permute-done.10.low_far
  76.6 0.2 shard_map.79
  76.8 0.6 collective-permute-start.14
  77.5 3.1 %collective-permute-start.15 = (f32[464,128]{1,0:T(8,128)S(1)}, f32[464,128]{1,0:T(8,128)S(1)}, u32[]{:S(2)}, u32[]{:S(2)}) collective-permute-start(f32[464,128]{1,0:T(8,128)S(1)} %get-tuple-element.73), channel_id=1, source_target_pairs={{0,128},{64,192},{128,0},{192,64},{1,129},{65,193},{129,1},{193,65... | collective-permute-start | bytes 712712 | tf_op jit(solution)/shard_map/ppermute | solution.py:56
  80.5 1.4 %collective-permute-start.16 = (f32[464,128]{1,0:T(8,128)S(1)}, f32[464,128]{1,0:T(8,128)S(1)}, u32[]{:S(2)}, u32[]{:S(2)}) collective-permute-start(f32[464,128]{1,0:T(8,128)S(1)} %get-tuple-element.74), channel_id=1, source_target_pairs={{0,192},{64,0},{128,64},{192,128},{1,193},{65,1},{129,65},{193,129... | collective-permute-start | bytes 712712 | tf_op jit(solution)/shard_map/ppermute | solution.py:56
  81.9 5.7 %collective-permute-done.23.high_far = f32[896,128]{1,0:T(8,128)S(1)} collective-permute-done((f32[896,128]{1,0:T(8,128)S(1)}, f32[896,128]{1,0:T(8,128)S(1)}, u32[]{:S(2)}, u32[]{:S(2)}) %collective-permute-start.23) | collective-permute-done | bytes 458784 | tf_op jit(solution)/shard_map/ppermute | solution.py:56
  87.6 0.1 shard_map.84
  87.8 4.5 %collective-permute-start.25 = (f32[448,128]{1,0:T(8,128)S(1)}, f32[448,128]{1,0:T(8,128)S(1)}, u32[]{:S(2)}, u32[]{:S(2)}) collective-permute-start(f32[448,128]{1,0:T(8,128)S(1)} %get-tuple-element.84), channel_id=1, source_target_pairs={{0,16},{8,24},{16,0},{24,8},{1,17},{9,25},{17,1},{25,9},{2,18},{10... | collective-permute-start | bytes 688136 | tf_op jit(solution)/shard_map/ppermute | solution.py:56
  92.3 0.3 collective-permute-done.14.b
  92.6 3.4 %collective-permute-start.26 = (f32[448,128]{1,0:T(8,128)S(1)}, f32[448,128]{1,0:T(8,128)S(1)}, u32[]{:S(2)}, u32[]{:S(2)}) collective-permute-start(f32[448,128]{1,0:T(8,128)S(1)} %get-tuple-element.85), channel_id=1, source_target_pairs={{0,24},{8,0},{16,8},{24,16},{1,25},{9,1},{17,9},{25,17},{2,26},{10... | collective-permute-start | bytes 688136 | tf_op jit(solution)/shard_map/ppermute | solution.py:56
  96.0 2.6 %collective-permute-done.15.c = f32[464,128]{1,0:T(8,128)S(1)} collective-permute-done((f32[464,128]{1,0:T(8,128)S(1)}, f32[464,128]{1,0:T(8,128)S(1)}, u32[]{:S(2)}, u32[]{:S(2)}) %collective-permute-start.15) | collective-permute-done | bytes 237600 | tf_op jit(solution)/shard_map/ppermute | solution.py:56
  98.7 6.2 %collective-permute-start.17 = (f32[240,128]{1,0:T(8,128)S(1)}, f32[240,128]{1,0:T(8,128)S(1)}, u32[]{:S(2)}, u32[]{:S(2)}) collective-permute-start(f32[240,128]{1,0:T(8,128)S(1)} %get-tuple-element.76), channel_id=1, source_target_pairs={{0,32},{32,0},{1,33},{33,1},{2,34},{34,2},{3,35},{35,3},{4,36},{36... | collective-permute-start | bytes 368648 | tf_op jit(solution)/shard_map/ppermute | solution.py:56
  104.9 0.3 collective-permute-start.27
  105.2 2.0 %collective-permute-done.17.got = f32[240,128]{1,0:T(8,128)S(1)} collective-permute-done((f32[240,128]{1,0:T(8,128)S(1)}, f32[240,128]{1,0:T(8,128)S(1)}, u32[]{:S(2)}, u32[]{:S(2)}) %collective-permute-start.17) | collective-permute-done | bytes 122912 | tf_op jit(solution)/shard_map/ppermute | solution.py:56
  107.2 0.7 shard_map.81
  107.9 5.7 %collective-permute-done.27.got = f32[224,128]{1,0:T(8,128)S(1)} collective-permute-done((f32[224,128]{1,0:T(8,128)S(1)}, f32[224,128]{1,0:T(8,128)S(1)}, u32[]{:S(2)}, u32[]{:S(2)}) %collective-permute-start.27) | collective-permute-done | bytes 114720 | tf_op jit(solution)/shard_map/ppermute | solution.py:56
  113.7 0.2 shard_map.86
  113.8 4.8 %collective-permute-start.28 = (f32[8,128]{1,0:T(8,128)S(1)}, f32[8,128]{1,0:T(8,128)S(1)}, u32[]{:S(2)}, u32[]{:S(2)}) collective-permute-start(f32[8,128]{1,0:T(8,128)S(1)} %shard_map.86), channel_id=1, source_target_pairs={{0,1},{1,0},{2,3},{3,2},{4,5},{5,4},{6,7},{7,6},{8,9},{9,8},{10,11... | collective-permute-start | bytes 12296 | tf_op jit(solution)/shard_map/ppermute | solution.py:56
  118.7 0.8 collective-permute-done.28
  119.5 0.3 collective-permute-start.29
  119.8 2.2 %collective-permute-start.30 = (f32[8,128]{1,0:T(8,128)S(1)}, f32[8,128]{1,0:T(8,128)S(1)}, u32[]{:S(2)}, u32[]{:S(2)}) collective-permute-start(f32[8,128]{1,0:T(8,128)S(1)} %max.3.a), channel_id=1, source_target_pairs={{0,4},{2,6},{4,0},{6,2},{1,5},{3,7},{5,1},{7,3},{8,12},{10,14},{12... | collective-permute-start | bytes 12296 | tf_op jit(solution)/shard_map/ppermute | solution.py:56
  122.0 1.8 %collective-permute-start.31 = (f32[8,128]{1,0:T(8,128)S(1)}, f32[8,128]{1,0:T(8,128)S(1)}, u32[]{:S(2)}, u32[]{:S(2)}) collective-permute-start(f32[8,128]{1,0:T(8,128)S(1)} %max.3.a), channel_id=1, source_target_pairs={{0,6},{2,0},{4,2},{6,4},{1,7},{3,1},{5,3},{7,5},{8,14},{10,8},{12,... | collective-permute-start | bytes 12296 | tf_op jit(solution)/shard_map/ppermute | solution.py:56
  123.8 1.0 collective-permute-done.31.d
  124.8 0.6 shard_map.87
  (36 shorter events, 0.7 us)
Async XLA Ops:
  0.6 7.9 %copy-start.1 = (s32[6,1024]{1,0:T(8,128)S(1)}, s32[6,1024]{1,0:T(8,128)}, u32[]{:S(2)}) copy-start(s32[6,1024]{1,0:T(8,128)} %param.7) | copy-start | bytes 73732
  2.8 9.5 %collective-permute-start = (f32[232,128]{1,0:T(8,128)S(1)}, f32[232,128]{1,0:T(8,128)S(1)}, u32[]{:S(2)}, u32[]{:S(2)}) collective-permute-start(f32[232,128]{1,0:T(8,128)S(1)} %get-tuple-element.46.after_ref.a), channel_id=1, source_target_pairs={{0,8},{8,16},{16,24},{24,0},{1,9},{9,17},{17,25},{25,1},{2,10},{10... | collective-permute-start | bytes 356360 | tf_op jit(solution)/shard_map/ppermute | solution.py:56
  4.9 7.6 %collective-permute-start.1 = (f32[232,128]{1,0:T(8,128)S(1)}, f32[232,128]{1,0:T(8,128)S(1)}, u32[]{:S(2)}, u32[]{:S(2)}) collective-permute-start(f32[232,128]{1,0:T(8,128)S(1)} %get-tuple-element.46.after_ref.a), channel_id=1, source_target_pairs={{0,16},{8,24},{16,0},{24,8},{1,17},{9,25},{17,1},{25,9},{2,18},{10... | collective-permute-start | bytes 356360 | tf_op jit(solution)/shard_map/ppermute | solution.py:56
  7.4 5.2 %collective-permute-start.2 = (f32[232,128]{1,0:T(8,128)S(1)}, f32[232,128]{1,0:T(8,128)S(1)}, u32[]{:S(2)}, u32[]{:S(2)}) collective-permute-start(f32[232,128]{1,0:T(8,128)S(1)} %get-tuple-element.46.after_ref.a), channel_id=1, source_target_pairs={{0,24},{8,0},{16,8},{24,16},{1,25},{9,1},{17,9},{25,17},{2,26},{10... | collective-permute-start | bytes 356360 | tf_op jit(solution)/shard_map/ppermute | solution.py:56
  12.6 16.1 %copy-start = (bf16[1024,1024]{1,0:T(8,128)(2,1)S(1)}, bf16[1024,1024]{1,0:T(8,128)(2,1)}, u32[]{:S(2)}) copy-start(bf16[1024,1024]{1,0:T(8,128)(2,1)} %traits_ref.3) | copy-start | bytes 6291460
  12.6 7.6 %collective-permute-start.3 = (f32[232,128]{1,0:T(8,128)S(1)}, f32[232,128]{1,0:T(8,128)S(1)}, u32[]{:S(2)}, u32[]{:S(2)}) collective-permute-start(f32[232,128]{1,0:T(8,128)S(1)} %shard_map.61.after_ref.a), channel_id=1, source_target_pairs={{0,64},{64,128},{128,192},{192,0},{1,65},{65,129},{129,193},{193,1... | collective-permute-start | bytes 356360 | tf_op jit(solution)/shard_map/ppermute | solution.py:56
  14.0 6.7 %collective-permute-start.4 = (f32[232,128]{1,0:T(8,128)S(1)}, f32[232,128]{1,0:T(8,128)S(1)}, u32[]{:S(2)}, u32[]{:S(2)}) collective-permute-start(f32[232,128]{1,0:T(8,128)S(1)} %shard_map.61.after_ref.a), channel_id=1, source_target_pairs={{0,128},{64,192},{128,0},{192,64},{1,129},{65,193},{129,1},{193,65... | collective-permute-start | bytes 356360 | tf_op jit(solution)/shard_map/ppermute | solution.py:56
  16.6 4.7 %collective-permute-start.5 = (f32[232,128]{1,0:T(8,128)S(1)}, f32[232,128]{1,0:T(8,128)S(1)}, u32[]{:S(2)}, u32[]{:S(2)}) collective-permute-start(f32[232,128]{1,0:T(8,128)S(1)} %shard_map.61.after_ref.a), channel_id=1, source_target_pairs={{0,192},{64,0},{128,64},{192,128},{1,193},{65,1},{129,65},{193,129... | collective-permute-start | bytes 356360 | tf_op jit(solution)/shard_map/ppermute | solution.py:56
  21.4 9.7 %collective-permute-start.6 = (f32[232,128]{1,0:T(8,128)S(1)}, f32[232,128]{1,0:T(8,128)S(1)}, u32[]{:S(2)}, u32[]{:S(2)}) collective-permute-start(f32[232,128]{1,0:T(8,128)S(1)} %shard_map.63.own_ref.after_ref), channel_id=1, source_target_pairs={{0,32},{32,0},{1,33},{33,1},{2,34},{34,2},{3,35},{35,3},{4,36},{36... | collective-permute-start | bytes 356360 | tf_op jit(solution)/shard_map/ppermute | solution.py:56
  32.8 6.4 %collective-permute-start.7 = (f32[40,512]{1,0:T(8,128)S(1)}, f32[40,512]{1,0:T(8,128)S(1)}, u32[]{:S(2)}, u32[]{:S(2)}) collective-permute-start(f32[40,512]{1,0:T(8,128)S(1)} %slice.4), channel_id=1, source_target_pairs={{0,1},{1,0},{2,3},{3,2},{4,5},{5,4},{6,7},{7,6},{8,9},{9,8},{10,11... | collective-permute-start | bytes 245768 | tf_op jit(solution)/shard_map/ppermute | solution.py:56
  40.9 12.6 %collective-permute-start.12 = (f32[896,128]{1,0:T(8,128)S(1)}, f32[896,128]{1,0:T(8,128)S(1)}, u32[]{:S(2)}, u32[]{:S(2)}) collective-permute-start(f32[896,128]{1,0:T(8,128)S(1)} %get-tuple-element.59.after_ref), channel_id=1, source_target_pairs={{0,24},{8,0},{16,8},{24,16},{1,25},{9,1},{17,9},{25,17},{2,26},{10... | collective-permute-start | bytes 1376264 | tf_op jit(solution)/shard_map/ppermute | solution.py:56
  43.6 14.1 %collective-permute-start.9 = (f32[912,128]{1,0:T(8,128)S(1)}, f32[912,128]{1,0:T(8,128)S(1)}, u32[]{:S(2)}, u32[]{:S(2)}) collective-permute-start(f32[912,128]{1,0:T(8,128)S(1)} %get-tuple-element.68), channel_id=1, source_target_pairs={{0,8},{8,16},{16,24},{24,0},{1,9},{9,17},{17,25},{25,1},{2,10},{10... | collective-permute-start | bytes 1400840 | tf_op jit(solution)/shard_map/ppermute | solution.py:56
  44.4 13.5 %collective-permute-start.22 = (f32[896,128]{1,0:T(8,128)S(1)}, f32[896,128]{1,0:T(8,128)S(1)}, u32[]{:S(2)}, u32[]{:S(2)}) collective-permute-start(f32[896,128]{1,0:T(8,128)S(1)} %get-tuple-element.60.after_ref), channel_id=1, source_target_pairs={{0,192},{64,0},{128,64},{192,128},{1,193},{65,1},{129,65},{193,129... | collective-permute-start | bytes 1376264 | tf_op jit(solution)/shard_map/ppermute | solution.py:56
  46.9 12.7 %collective-permute-start.19 = (f32[896,128]{1,0:T(8,128)S(1)}, f32[896,128]{1,0:T(8,128)S(1)}, u32[]{:S(2)}, u32[]{:S(2)}) collective-permute-start(f32[896,128]{1,0:T(8,128)S(1)} %get-tuple-element.81), channel_id=1, source_target_pairs={{0,64},{64,128},{128,192},{192,0},{1,65},{65,129},{129,193},{193,1... | collective-permute-start | bytes 1376264 | tf_op jit(solution)/shard_map/ppermute | solution.py:56
  49.0 17.6 %collective-permute-start.11 = (f32[896,128]{1,0:T(8,128)S(1)}, f32[896,128]{1,0:T(8,128)S(1)}, u32[]{:S(2)}, u32[]{:S(2)}) collective-permute-start(f32[896,128]{1,0:T(8,128)S(1)} %get-tuple-element.63.after_ref), channel_id=1, source_target_pairs={{0,8},{8,16},{16,24},{24,0},{1,9},{9,17},{17,25},{25,1},{2,10},{10... | collective-permute-start | bytes 1376264 | tf_op jit(solution)/shard_map/ppermute | solution.py:56
  53.5 15.7 %collective-permute-start.8 = (f32[912,128]{1,0:T(8,128)S(1)}, f32[912,128]{1,0:T(8,128)S(1)}, u32[]{:S(2)}, u32[]{:S(2)}) collective-permute-start(f32[912,128]{1,0:T(8,128)S(1)} %get-tuple-element.66), channel_id=1, source_target_pairs={{0,24},{8,0},{16,8},{24,16},{1,25},{9,1},{17,9},{25,17},{2,26},{10... | collective-permute-start | bytes 1400840 | tf_op jit(solution)/shard_map/ppermute | solution.py:56
  57.7 18.2 %collective-permute-start.13 = (f32[896,128]{1,0:T(8,128)S(1)}, f32[896,128]{1,0:T(8,128)S(1)}, u32[]{:S(2)}, u32[]{:S(2)}) collective-permute-start(f32[896,128]{1,0:T(8,128)S(1)} %shard_map.78), channel_id=1, source_target_pairs={{0,24},{8,0},{16,8},{24,16},{1,25},{9,1},{17,9},{25,17},{2,26},{10... | collective-permute-start | bytes 1376264 | tf_op jit(solution)/shard_map/ppermute | solution.py:56
  57.9 18.8 %collective-permute-start.10 = (f32[912,128]{1,0:T(8,128)S(1)}, f32[912,128]{1,0:T(8,128)S(1)}, u32[]{:S(2)}, u32[]{:S(2)}) collective-permute-start(f32[912,128]{1,0:T(8,128)S(1)} %shard_map.77), channel_id=1, source_target_pairs={{0,8},{8,16},{16,24},{24,0},{1,9},{9,17},{17,25},{25,1},{2,10},{10... | collective-permute-start | bytes 1400840 | tf_op jit(solution)/shard_map/ppermute | solution.py:56
  59.6 17.9 %collective-permute-start.21 = (f32[896,128]{1,0:T(8,128)S(1)}, f32[896,128]{1,0:T(8,128)S(1)}, u32[]{:S(2)}, u32[]{:S(2)}) collective-permute-start(f32[896,128]{1,0:T(8,128)S(1)} %get-tuple-element.64.after_ref), channel_id=1, source_target_pairs={{0,64},{64,128},{128,192},{192,0},{1,65},{65,129},{129,193},{193,1... | collective-permute-start | bytes 1376264 | tf_op jit(solution)/shard_map/ppermute | solution.py:56
  66.6 13.9 %collective-permute-start.18 = (f32[896,128]{1,0:T(8,128)S(1)}, f32[896,128]{1,0:T(8,128)S(1)}, u32[]{:S(2)}, u32[]{:S(2)}) collective-permute-start(f32[896,128]{1,0:T(8,128)S(1)} %get-tuple-element.79), channel_id=1, source_target_pairs={{0,192},{64,0},{128,64},{192,128},{1,193},{65,1},{129,65},{193,129... | collective-permute-start | bytes 1376264 | tf_op jit(solution)/shard_map/ppermute | solution.py:56
  69.2 18.4 %collective-permute-start.23 = (f32[896,128]{1,0:T(8,128)S(1)}, f32[896,128]{1,0:T(8,128)S(1)}, u32[]{:S(2)}, u32[]{:S(2)}) collective-permute-start(f32[896,128]{1,0:T(8,128)S(1)} %shard_map.83), channel_id=1, source_target_pairs={{0,192},{64,0},{128,64},{192,128},{1,193},{65,1},{129,65},{193,129... | collective-permute-start | bytes 1376264 | tf_op jit(solution)/shard_map/ppermute | solution.py:56
  75.9 11.7 %collective-permute-start.20 = (f32[896,128]{1,0:T(8,128)S(1)}, f32[896,128]{1,0:T(8,128)S(1)}, u32[]{:S(2)}, u32[]{:S(2)}) collective-permute-start(f32[896,128]{1,0:T(8,128)S(1)} %shard_map.82), channel_id=1, source_target_pairs={{0,64},{64,128},{128,192},{192,0},{1,65},{65,129},{129,193},{193,1... | collective-permute-start | bytes 1376264 | tf_op jit(solution)/shard_map/ppermute | solution.py:56
  76.8 15.7 %collective-permute-start.14 = (f32[464,128]{1,0:T(8,128)S(1)}, f32[464,128]{1,0:T(8,128)S(1)}, u32[]{:S(2)}, u32[]{:S(2)}) collective-permute-start(f32[464,128]{1,0:T(8,128)S(1)} %get-tuple-element.72), channel_id=1, source_target_pairs={{0,64},{64,128},{128,192},{192,0},{1,65},{65,129},{129,193},{193,1... | collective-permute-start | bytes 712712 | tf_op jit(solution)/shard_map/ppermute | solution.py:56
  77.5 21.1 %collective-permute-start.15 = (f32[464,128]{1,0:T(8,128)S(1)}, f32[464,128]{1,0:T(8,128)S(1)}, u32[]{:S(2)}, u32[]{:S(2)}) collective-permute-start(f32[464,128]{1,0:T(8,128)S(1)} %get-tuple-element.73), channel_id=1, source_target_pairs={{0,128},{64,192},{128,0},{192,64},{1,129},{65,193},{129,1},{193,65... | collective-permute-start | bytes 712712 | tf_op jit(solution)/shard_map/ppermute | solution.py:56
  80.5 18.0 %collective-permute-start.16 = (f32[464,128]{1,0:T(8,128)S(1)}, f32[464,128]{1,0:T(8,128)S(1)}, u32[]{:S(2)}, u32[]{:S(2)}) collective-permute-start(f32[464,128]{1,0:T(8,128)S(1)} %get-tuple-element.74), channel_id=1, source_target_pairs={{0,192},{64,0},{128,64},{192,128},{1,193},{65,1},{129,65},{193,129... | collective-permute-start | bytes 712712 | tf_op jit(solution)/shard_map/ppermute | solution.py:56
  87.7 17.1 %collective-permute-start.24 = (f32[448,128]{1,0:T(8,128)S(1)}, f32[448,128]{1,0:T(8,128)S(1)}, u32[]{:S(2)}, u32[]{:S(2)}) collective-permute-start(f32[448,128]{1,0:T(8,128)S(1)} %get-tuple-element.83), channel_id=1, source_target_pairs={{0,8},{8,16},{16,24},{24,0},{1,9},{9,17},{17,25},{25,1},{2,10},{10... | collective-permute-start | bytes 688136 | tf_op jit(solution)/shard_map/ppermute | solution.py:56
  87.8 17.0 %collective-permute-start.25 = (f32[448,128]{1,0:T(8,128)S(1)}, f32[448,128]{1,0:T(8,128)S(1)}, u32[]{:S(2)}, u32[]{:S(2)}) collective-permute-start(f32[448,128]{1,0:T(8,128)S(1)} %get-tuple-element.84), channel_id=1, source_target_pairs={{0,16},{8,24},{16,0},{24,8},{1,17},{9,25},{17,1},{25,9},{2,18},{10... | collective-permute-start | bytes 688136 | tf_op jit(solution)/shard_map/ppermute | solution.py:56
  92.6 12.3 %collective-permute-start.26 = (f32[448,128]{1,0:T(8,128)S(1)}, f32[448,128]{1,0:T(8,128)S(1)}, u32[]{:S(2)}, u32[]{:S(2)}) collective-permute-start(f32[448,128]{1,0:T(8,128)S(1)} %get-tuple-element.85), channel_id=1, source_target_pairs={{0,24},{8,0},{16,8},{24,16},{1,25},{9,1},{17,9},{25,17},{2,26},{10... | collective-permute-start | bytes 688136 | tf_op jit(solution)/shard_map/ppermute | solution.py:56
  98.7 8.6 %collective-permute-start.17 = (f32[240,128]{1,0:T(8,128)S(1)}, f32[240,128]{1,0:T(8,128)S(1)}, u32[]{:S(2)}, u32[]{:S(2)}) collective-permute-start(f32[240,128]{1,0:T(8,128)S(1)} %get-tuple-element.76), channel_id=1, source_target_pairs={{0,32},{32,0},{1,33},{33,1},{2,34},{34,2},{3,35},{35,3},{4,36},{36... | collective-permute-start | bytes 368648 | tf_op jit(solution)/shard_map/ppermute | solution.py:56
  104.9 8.8 %collective-permute-start.27 = (f32[224,128]{1,0:T(8,128)S(1)}, f32[224,128]{1,0:T(8,128)S(1)}, u32[]{:S(2)}, u32[]{:S(2)}) collective-permute-start(f32[224,128]{1,0:T(8,128)S(1)} %get-tuple-element.87), channel_id=1, source_target_pairs={{0,32},{32,0},{1,33},{33,1},{2,34},{34,2},{3,35},{35,3},{4,36},{36... | collective-permute-start | bytes 344072 | tf_op jit(solution)/shard_map/ppermute | solution.py:56
  113.8 5.6 %collective-permute-start.28 = (f32[8,128]{1,0:T(8,128)S(1)}, f32[8,128]{1,0:T(8,128)S(1)}, u32[]{:S(2)}, u32[]{:S(2)}) collective-permute-start(f32[8,128]{1,0:T(8,128)S(1)} %shard_map.86), channel_id=1, source_target_pairs={{0,1},{1,0},{2,3},{3,2},{4,5},{5,4},{6,7},{7,6},{8,9},{9,8},{10,11... | collective-permute-start | bytes 12296 | tf_op jit(solution)/shard_map/ppermute | solution.py:56
  119.5 4.3 %collective-permute-start.29 = (f32[8,128]{1,0:T(8,128)S(1)}, f32[8,128]{1,0:T(8,128)S(1)}, u32[]{:S(2)}, u32[]{:S(2)}) collective-permute-start(f32[8,128]{1,0:T(8,128)S(1)} %max.3.a), channel_id=1, source_target_pairs={{0,2},{2,4},{4,6},{6,0},{1,3},{3,5},{5,7},{7,1},{8,10},{10,12},{12... | collective-permute-start | bytes 12296 | tf_op jit(solution)/shard_map/ppermute | solution.py:56
  119.8 4.0 %collective-permute-start.30 = (f32[8,128]{1,0:T(8,128)S(1)}, f32[8,128]{1,0:T(8,128)S(1)}, u32[]{:S(2)}, u32[]{:S(2)}) collective-permute-start(f32[8,128]{1,0:T(8,128)S(1)} %max.3.a), channel_id=1, source_target_pairs={{0,4},{2,6},{4,0},{6,2},{1,5},{3,7},{5,1},{7,3},{8,12},{10,14},{12... | collective-permute-start | bytes 12296 | tf_op jit(solution)/shard_map/ppermute | solution.py:56
  122.0 2.8 %collective-permute-start.31 = (f32[8,128]{1,0:T(8,128)S(1)}, f32[8,128]{1,0:T(8,128)S(1)}, u32[]{:S(2)}, u32[]{:S(2)}) collective-permute-start(f32[8,128]{1,0:T(8,128)S(1)} %max.3.a), channel_id=1, source_target_pairs={{0,6},{2,0},{4,2},{6,4},{1,7},{3,1},{5,3},{7,5},{8,14},{10,8},{12,... | collective-permute-start | bytes 12296 | tf_op jit(solution)/shard_map/ppermute | solution.py:56

commit v3 on v2

--- a/solution.py
+++ b/solution.py
@@ -18,6 +18,7 @@
 HALF = E // 2
 COLS = V + HALF + 128
 BLOCKS = (V + HALF) // 128
+STEP = 256
 SPLIT = (3, 2, 1)
 SQUARES = 16
 CHUNK = (PERMS + 1) * V // 2
@@ -56,24 +57,43 @@
     return lax.ppermute(value, axis, shifts(axis, k))
 
 
-def front_kernel(core_ref, traits_ref, cov_ref, geno_ref, pay_ref, xt_ref, dx_ref):
-    del core_ref
+def front_kernel(core_ref, traits_hbm, cov_hbm, geno_hbm, pay_ref, xt_ref, dx_ref, traits, cov, geno, sems):
+    half = pl.ds(pl.multiple_of(core_ref[0] * HALF, HALF), HALF)
+    first = pltpu.make_async_copy(cov_hbm, cov, sems.at[0])
+    second = pltpu.make_async_copy(geno_hbm, geno, sems.at[1])
+    blocks = []
+    for i in range(ROWS // STEP):
+        rows = pl.ds(i * STEP, STEP)
+        blocks.append(pltpu.make_async_copy(traits_hbm.at[rows, half], traits.at[rows, :], sems.at[2 + i]))
+    for copy in (first, second, *blocks):
+        copy.start()
+    first.wait()
     row = lax.broadcasted_iota(jnp.int32, (128 - C, ROWS), 0)
     tail = jnp.where(row == 0, 1.0, 0.0).astype(F32)
-    design_t = jnp.concatenate([cov_ref[...].astype(F32), tail], axis=0)
-    dosage = geno_ref[...].astype(F32).astype(BF16)
+    design_t = jnp.concatenate([cov[...].astype(F32), tail], axis=0)
     design_b = jnp.transpose(design_t).astype(BF16)
-    dx_ref[:, :V] = dosage
     dx_ref[:, V:] = design_b
     xt = design_t[:48].astype(BF16)
     xt_ref[...] = xt
     pay_ref[BLOCKS * C :, :] = dot(xt, design_b)[:40]
-    for at, part in ((0, dot(xt, dosage)), (V // 128, dot(xt, traits_ref[...]))):
+
+    def place(at, part):
         for j in range(part.shape[1] // 128):
             block = part[:, j * 128 : (j + 1) * 128]
             pay_ref[(at + j) * C : (at + j + 1) * C, :] = block[:C]
             ones = BLOCKS * C + C + 1 + at + j
             pay_ref[ones : ones + 1, :] = block[C : C + 1]
+
+    second.wait()
+    dosage = geno[...].astype(F32).astype(BF16)
+    dx_ref[:, :V] = dosage
+    place(0, dot(xt, dosage))
+    total = None
+    for i, copy in enumerate(blocks):
+        copy.wait()
+        part = dot(xt[:, i * STEP : (i + 1) * STEP], traits[i * STEP : (i + 1) * STEP, :])
+        total = part if total is None else total + part
+    place(V // 128, total)
 
 
 def turn_kernel(traits_ref, out_ref):
@@ -308,15 +328,13 @@
         grid_spec=pltpu.PrefetchScalarGridSpec(
             num_scalar_prefetch=1,
             grid=(1,),
-            in_specs=[
-                pl.BlockSpec((ROWS, HALF), lambda i, c: (0, c[0])),
-                pl.BlockSpec((C, ROWS), lambda i, c: (0, 0)),
-                pl.BlockSpec((ROWS, V), lambda i, c: (0, 0)),
-            ],
-            out_specs=[
-                pl.BlockSpec((BLOCKS * C + 40, 128), lambda i, c: (0, 0)),
-                pl.BlockSpec((48, ROWS), lambda i, c: (0, 0)),
-                pl.BlockSpec((ROWS, V + 128), lambda i, c: (0, 0)),
+            in_specs=[anywhere] * 3,
+            out_specs=[pl.BlockSpec(memory_space=pltpu.VMEM)] * 3,
+            scratch_shapes=[
+                pltpu.VMEM((ROWS, HALF), BF16),
+                pltpu.VMEM((C, ROWS), BF16),
+                pltpu.VMEM((ROWS, V), jnp.int32),
+                pltpu.SemaphoreType.DMA((2 + ROWS // STEP,)),
             ],
         ),
         flops=2 * 128 * ROWS * COLS,

time: 126 us -> 126 us (level)
  no operation moved by 1% of the time
where the time goes in v3:
time: 126 us; the launch traced here: 125 us
  starting transfers between devices  63.3 us (50%)
  waiting for transfers between devices  38.1 us (30%)
  Pallas kernels  23 us (18%)
    ppermute x32, starting transfers between devices, shift(): return lax.ppermute(value, axis, shifts(axis, k))  63.3 us
    ppermute x32, waiting for transfers between devices, shift(): return lax.ppermute(value, axis, shifts(axis, k))  38.1 us
    pallas_call x29, Pallas kernels, call(): pl.pallas_call(kernel, out_shape=shapes[0] if single else shapes, cost_es...  23 us
  transfers between devices with their start and end apart: 32, of which 16 were waited for; matrix products, arithmetic and copies ran while one was open for 0% of the time, Pallas kernels for 13%

profile of v3, /device:TPU:1, one launch (start us, length us, event | category | flops | bytes accessed | tf_op | source)
XLA Modules:
  0.0 125.3 jit_solution(4297425216179126708)
XLA Ops:
  0.6 2.1 %shard_map.59 = (f32[232,128]{1,0:T(8,128)S(1)}, bf16[48,1024]{1,0:T(8,128)(2,1)S(1)}, bf16[1024,384]{1,0:T(8,128)(2,1)S(1)}) custom-call(s32[1]{0:T(128)} %bitcast.3.core_ref, bf16[1024,1024]{1,0:T(8,128)(2,1)} %traits_ref.1, bf16[32,1024]{1,0:T(8,128)(2,1)} %bitcast.10, s32[1024,256]{1,0:T(8,128)} %geno_hbm.1), custom_call_target="tpu_custom_call" | custom-call | flops 234881024 | bytes 1003520 | tf_op jit(solution)/shard_map/pallas_call | solution.py:41
  2.7 2.1 %collective-permute-start = (f32[232,128]{1,0:T(8,128)S(1)}, f32[232,128]{1,0:T(8,128)S(1)}, u32[]{:S(2)}, u32[]{:S(2)}) collective-permute-start(f32[232,128]{1,0:T(8,128)S(1)} %get-tuple-element.46.after_ref.a), channel_id=1, source_target_pairs={{0,8},{8,16},{16,24},{24,0},{1,9},{9,17},{17,25},{25,1},{2,10},{10... | collective-permute-start | bytes 356360 | tf_op jit(solution)/shard_map/ppermute | solution.py:57
  4.8 2.5 %collective-permute-start.1 = (f32[232,128]{1,0:T(8,128)S(1)}, f32[232,128]{1,0:T(8,128)S(1)}, u32[]{:S(2)}, u32[]{:S(2)}) collective-permute-start(f32[232,128]{1,0:T(8,128)S(1)} %get-tuple-element.46.after_ref.a), channel_id=1, source_target_pairs={{0,16},{8,24},{16,0},{24,8},{1,17},{9,25},{17,1},{25,9},{2,18},{10... | collective-permute-start | bytes 356360 | tf_op jit(solution)/shard_map/ppermute | solution.py:57
  7.3 1.2 collective-permute-start.2
  8.5 3.8 %shard_map.60 = (bf16[3,1024,384]{2,1,0:T(8,128)(2,1)S(1)}, f32[8,128]{1,0:T(8,128)S(1)}) custom-call(s32[1]{0:T(128)S(6)} %mul.13.base_ref, s32[6,1,1024]{2,1,0:T(1,128)S(1)} %reshape.42.order_ref, bf16[1024,384]{1,0:T(8,128)(2,1)S(1)} %get-tuple-element.47.dx_ref, f32[232,128]{1,0:T(8,128)S(1)} %get-tuple-element.46.after_ref.a), custom_call_target="tpu_custom_call" | custom-call | flops 2415919104 | bytes 2363392 | tf_op jit(solution)/shard_map/pallas_call | solution.py:41
  12.3 0.2 collective-permute-done.1.c
  12.5 1.4 %collective-permute-start.3 = (f32[232,128]{1,0:T(8,128)S(1)}, f32[232,128]{1,0:T(8,128)S(1)}, u32[]{:S(2)}, u32[]{:S(2)}) collective-permute-start(f32[232,128]{1,0:T(8,128)S(1)} %shard_map.61.after_ref.a), channel_id=1, source_target_pairs={{0,64},{64,128},{128,192},{192,0},{1,65},{65,129},{129,193},{193,1... | collective-permute-start | bytes 356360 | tf_op jit(solution)/shard_map/ppermute | solution.py:57
  13.9 2.6 %collective-permute-start.4 = (f32[232,128]{1,0:T(8,128)S(1)}, f32[232,128]{1,0:T(8,128)S(1)}, u32[]{:S(2)}, u32[]{:S(2)}) collective-permute-start(f32[232,128]{1,0:T(8,128)S(1)} %shard_map.61.after_ref.a), channel_id=1, source_target_pairs={{0,128},{64,192},{128,0},{192,64},{1,129},{65,193},{129,1},{193,65... | collective-permute-start | bytes 356360 | tf_op jit(solution)/shard_map/ppermute | solution.py:57
  16.5 1.1 collective-permute-start.5
  17.6 2.5 %shard_map.62 = (bf16[2,1024,384]{2,1,0:T(8,128)(2,1)S(1)}, f32[8,128]{1,0:T(8,128)S(1)}) custom-call(s32[1]{0:T(128)S(6)} %mul.13.base_ref, s32[6,1,1024]{2,1,0:T(1,128)S(1)} %reshape.42.order_ref, bf16[1024,384]{1,0:T(8,128)(2,1)S(1)} %get-tuple-element.47.dx_ref, f32[232,128]{1,0:T(8,128)S(1)} %shard_map.61.after_ref.a), custom_call_target="tpu_custom_call" | custom-call | flops 1610612736 | bytes 1576960 | tf_op jit(solution)/shard_map/pallas_call | solution.py:41
  20.1 0.4 collective-permute-done.4.c
  20.6 0.7 collective-permute-done.5.d
  21.3 7.4 %collective-permute-start.6 = (f32[232,128]{1,0:T(8,128)S(1)}, f32[232,128]{1,0:T(8,128)S(1)}, u32[]{:S(2)}, u32[]{:S(2)}) collective-permute-start(f32[232,128]{1,0:T(8,128)S(1)} %shard_map.63.own_ref.after_ref), channel_id=1, source_target_pairs={{0,32},{32,0},{1,33},{33,1},{2,34},{34,2},{3,35},{35,3},{4,36},{36... | collective-permute-start | bytes 356360 | tf_op jit(solution)/shard_map/ppermute | solution.py:57
  28.7 1.1 shard_map.65.yt_ref
  29.8 1.2 collective-permute-done.6.far_ref
  31.0 1.7 %shard_map.64.own_ref = f32[40,768]{1,0:T(8,128)S(1)} custom-call(f32[232,128]{1,0:T(8,128)S(1)} %shard_map.63.own_ref.after_ref, f32[232,128]{1,0:T(8,128)S(1)} %collective-permute-done.6.far_ref), custom_call_target="tpu_custom_call" | custom-call | flops 100000000 | bytes 122880 | tf_op jit(solution)/shard_map/pallas_call | solution.py:41
  32.7 3.5 %collective-permute-start.7 = (f32[40,512]{1,0:T(8,128)S(1)}, f32[40,512]{1,0:T(8,128)S(1)}, u32[]{:S(2)}, u32[]{:S(2)}) collective-permute-start(f32[40,512]{1,0:T(8,128)S(1)} %slice.4), channel_id=1, source_target_pairs={{0,1},{1,0},{2,3},{3,2},{4,5},{5,4},{6,7},{7,6},{8,9},{9,8},{10,11... | collective-permute-start | bytes 245768 | tf_op jit(solution)/shard_map/ppermute | solution.py:57
  36.2 1.8 %shard_map.66 = (bf16[1,1024,384]{2,1,0:T(8,128)(2,1)S(1)}, f32[8,128]{1,0:T(8,128)}) custom-call(s32[1]{0:T(128)S(6)} %mul.13.base_ref, s32[6,1,1024]{2,1,0:T(1,128)S(1)} %reshape.42.order_ref, bf16[1024,384]{1,0:T(8,128)(2,1)S(1)} %get-tuple-element.47.dx_ref, f32[232,128]{1,0:T(8,128)S(1)} %shard_map.63.own_ref.after_ref), custom_call_target="tpu_custom_call" | custom-call | flops 805306368 | bytes 790528 | tf_op jit(solution)/shard_map/pallas_call | solution.py:41
  38.0 1.1 shard_map.67
  39.1 1.0 shard_map.68
  40.1 0.7 shard_map.69
  40.8 2.7 %collective-permute-start.12 = (f32[896,128]{1,0:T(8,128)S(1)}, f32[896,128]{1,0:T(8,128)S(1)}, u32[]{:S(2)}, u32[]{:S(2)}) collective-permute-start(f32[896,128]{1,0:T(8,128)S(1)} %get-tuple-element.59.after_ref), channel_id=1, source_target_pairs={{0,24},{8,0},{16,8},{24,16},{1,25},{9,1},{17,9},{25,17},{2,26},{10... | collective-permute-start | bytes 1376264 | tf_op jit(solution)/shard_map/ppermute | solution.py:57
  43.5 0.7 shard_map.70
  44.3 2.5 %collective-permute-start.22 = (f32[896,128]{1,0:T(8,128)S(1)}, f32[896,128]{1,0:T(8,128)S(1)}, u32[]{:S(2)}, u32[]{:S(2)}) collective-permute-start(f32[896,128]{1,0:T(8,128)S(1)} %get-tuple-element.60.after_ref), channel_id=1, source_target_pairs={{0,192},{64,0},{128,64},{192,128},{1,193},{65,1},{129,65},{193,129... | collective-permute-start | bytes 1376264 | tf_op jit(solution)/shard_map/ppermute | solution.py:57
  46.8 0.7 shard_map.71
  47.5 0.7 shard_map.72
  48.2 0.7 shard_map.73
  49.0 0.1 collective-permute-start.11
  49.1 0.7 shard_map.74
  49.8 0.7 shard_map.75
  50.5 2.9 %collective-permute-done.12.b = f32[896,128]{1,0:T(8,128)S(1)} collective-permute-done((f32[896,128]{1,0:T(8,128)S(1)}, f32[896,128]{1,0:T(8,128)S(1)}, u32[]{:S(2)}, u32[]{:S(2)}) %collective-permute-start.12) | collective-permute-done | bytes 458784 | tf_op jit(solution)/shard_map/ppermute | solution.py:57
  53.4 3.4 %collective-permute-start.8 = (f32[912,128]{1,0:T(8,128)S(1)}, f32[912,128]{1,0:T(8,128)S(1)}, u32[]{:S(2)}, u32[]{:S(2)}) collective-permute-start(f32[912,128]{1,0:T(8,128)S(1)} %get-tuple-element.66), channel_id=1, source_target_pairs={{0,24},{8,0},{16,8},{24,16},{1,25},{9,1},{17,9},{25,17},{2,26},{10... | collective-permute-start | bytes 1400840 | tf_op jit(solution)/shard_map/ppermute | solution.py:57
  56.8 0.7 shard_map.76
  57.6 0.1 collective-permute-start.13
  57.8 1.5 %collective-permute-start.10 = (f32[912,128]{1,0:T(8,128)S(1)}, f32[912,128]{1,0:T(8,128)S(1)}, u32[]{:S(2)}, u32[]{:S(2)}) collective-permute-start(f32[912,128]{1,0:T(8,128)S(1)} %shard_map.77), channel_id=1, source_target_pairs={{0,8},{8,16},{16,24},{24,0},{1,9},{9,17},{17,25},{25,1},{2,10},{10... | collective-permute-start | bytes 1400840 | tf_op jit(solution)/shard_map/ppermute | solution.py:57
  59.3 0.2 collective-permute-done.19.b
  59.5 7.0 %collective-permute-done.11.high_near = f32[896,128]{1,0:T(8,128)S(1)} collective-permute-done((f32[896,128]{1,0:T(8,128)S(1)}, f32[896,128]{1,0:T(8,128)S(1)}, u32[]{:S(2)}, u32[]{:S(2)}) %collective-permute-start.11) | collective-permute-done | bytes 458784 | tf_op jit(solution)/shard_map/ppermute | solution.py:57
  66.5 2.4 %collective-permute-start.18 = (f32[896,128]{1,0:T(8,128)S(1)}, f32[896,128]{1,0:T(8,128)S(1)}, u32[]{:S(2)}, u32[]{:S(2)}) collective-permute-start(f32[896,128]{1,0:T(8,128)S(1)} %get-tuple-element.79), channel_id=1, source_target_pairs={{0,192},{64,0},{128,64},{192,128},{1,193},{65,1},{129,65},{193,129... | collective-permute-start | bytes 1376264 | tf_op jit(solution)/shard_map/ppermute | solution.py:57
  69.2 6.6 %collective-permute-done.13.high_far = f32[896,128]{1,0:T(8,128)S(1)} collective-permute-done((f32[896,128]{1,0:T(8,128)S(1)}, f32[896,128]{1,0:T(8,128)S(1)}, u32[]{:S(2)}, u32[]{:S(2)}) %collective-permute-start.13) | collective-permute-done | bytes 458784 | tf_op jit(solution)/shard_map/ppermute | solution.py:57
  75.8 0.2 collective-permute-start.20
  76.1 0.5 collective-permute-done.10.low_far
  76.5 0.2 shard_map.79
  76.7 0.6 collective-permute-start.14
  77.4 3.1 %collective-permute-start.15 = (f32[464,128]{1,0:T(8,128)S(1)}, f32[464,128]{1,0:T(8,128)S(1)}, u32[]{:S(2)}, u32[]{:S(2)}) collective-permute-start(f32[464,128]{1,0:T(8,128)S(1)} %get-tuple-element.73), channel_id=1, source_target_pairs={{0,128},{64,192},{128,0},{192,64},{1,129},{65,193},{129,1},{193,65... | collective-permute-start | bytes 712712 | tf_op jit(solution)/shard_map/ppermute | solution.py:57
  80.5 1.4 %collective-permute-start.16 = (f32[464,128]{1,0:T(8,128)S(1)}, f32[464,128]{1,0:T(8,128)S(1)}, u32[]{:S(2)}, u32[]{:S(2)}) collective-permute-start(f32[464,128]{1,0:T(8,128)S(1)} %get-tuple-element.74), channel_id=1, source_target_pairs={{0,192},{64,0},{128,64},{192,128},{1,193},{65,1},{129,65},{193,129... | collective-permute-start | bytes 712712 | tf_op jit(solution)/shard_map/ppermute | solution.py:57
  81.8 5.7 %collective-permute-done.23.high_far = f32[896,128]{1,0:T(8,128)S(1)} collective-permute-done((f32[896,128]{1,0:T(8,128)S(1)}, f32[896,128]{1,0:T(8,128)S(1)}, u32[]{:S(2)}, u32[]{:S(2)}) %collective-permute-start.23) | collective-permute-done | bytes 458784 | tf_op jit(solution)/shard_map/ppermute | solution.py:57
  87.5 0.1 shard_map.84
  87.7 4.5 %collective-permute-start.25 = (f32[448,128]{1,0:T(8,128)S(1)}, f32[448,128]{1,0:T(8,128)S(1)}, u32[]{:S(2)}, u32[]{:S(2)}) collective-permute-start(f32[448,128]{1,0:T(8,128)S(1)} %get-tuple-element.84), channel_id=1, source_target_pairs={{0,16},{8,24},{16,0},{24,8},{1,17},{9,25},{17,1},{25,9},{2,18},{10... | collective-permute-start | bytes 688136 | tf_op jit(solution)/shard_map/ppermute | solution.py:57
  92.2 0.3 collective-permute-done.14.b
  92.5 3.4 %collective-permute-start.26 = (f32[448,128]{1,0:T(8,128)S(1)}, f32[448,128]{1,0:T(8,128)S(1)}, u32[]{:S(2)}, u32[]{:S(2)}) collective-permute-start(f32[448,128]{1,0:T(8,128)S(1)} %get-tuple-element.85), channel_id=1, source_target_pairs={{0,24},{8,0},{16,8},{24,16},{1,25},{9,1},{17,9},{25,17},{2,26},{10... | collective-permute-start | bytes 688136 | tf_op jit(solution)/shard_map/ppermute | solution.py:57
  95.9 2.6 %collective-permute-done.15.c = f32[464,128]{1,0:T(8,128)S(1)} collective-permute-done((f32[464,128]{1,0:T(8,128)S(1)}, f32[464,128]{1,0:T(8,128)S(1)}, u32[]{:S(2)}, u32[]{:S(2)}) %collective-permute-start.15) | collective-permute-done | bytes 237600 | tf_op jit(solution)/shard_map/ppermute | solution.py:57
  98.6 6.2 %collective-permute-start.17 = (f32[240,128]{1,0:T(8,128)S(1)}, f32[240,128]{1,0:T(8,128)S(1)}, u32[]{:S(2)}, u32[]{:S(2)}) collective-permute-start(f32[240,128]{1,0:T(8,128)S(1)} %get-tuple-element.76), channel_id=1, source_target_pairs={{0,32},{32,0},{1,33},{33,1},{2,34},{34,2},{3,35},{35,3},{4,36},{36... | collective-permute-start | bytes 368648 | tf_op jit(solution)/shard_map/ppermute | solution.py:57
  104.8 0.2 collective-permute-start.27
  105.0 2.1 %collective-permute-done.17.got = f32[240,128]{1,0:T(8,128)S(1)} collective-permute-done((f32[240,128]{1,0:T(8,128)S(1)}, f32[240,128]{1,0:T(8,128)S(1)}, u32[]{:S(2)}, u32[]{:S(2)}) %collective-permute-start.17) | collective-permute-done | bytes 122912 | tf_op jit(solution)/shard_map/ppermute | solution.py:57
  107.1 0.7 shard_map.81
  107.9 5.7 %collective-permute-done.27.got = f32[224,128]{1,0:T(8,128)S(1)} collective-permute-done((f32[224,128]{1,0:T(8,128)S(1)}, f32[224,128]{1,0:T(8,128)S(1)}, u32[]{:S(2)}, u32[]{:S(2)}) %collective-permute-start.27) | collective-permute-done | bytes 114720 | tf_op jit(solution)/shard_map/ppermute | solution.py:57
  113.6 0.2 shard_map.86
  113.8 4.8 %collective-permute-start.28 = (f32[8,128]{1,0:T(8,128)S(1)}, f32[8,128]{1,0:T(8,128)S(1)}, u32[]{:S(2)}, u32[]{:S(2)}) collective-permute-start(f32[8,128]{1,0:T(8,128)S(1)} %shard_map.86), channel_id=1, source_target_pairs={{0,1},{1,0},{2,3},{3,2},{4,5},{5,4},{6,7},{7,6},{8,9},{9,8},{10,11... | collective-permute-start | bytes 12296 | tf_op jit(solution)/shard_map/ppermute | solution.py:57
  118.6 0.8 collective-permute-done.28
  119.4 0.3 collective-permute-start.29
  119.7 2.2 %collective-permute-start.30 = (f32[8,128]{1,0:T(8,128)S(1)}, f32[8,128]{1,0:T(8,128)S(1)}, u32[]{:S(2)}, u32[]{:S(2)}) collective-permute-start(f32[8,128]{1,0:T(8,128)S(1)} %max.3.a), channel_id=1, source_target_pairs={{0,4},{2,6},{4,0},{6,2},{1,5},{3,7},{5,1},{7,3},{8,12},{10,14},{12... | collective-permute-start | bytes 12296 | tf_op jit(solution)/shard_map/ppermute | solution.py:57
  122.0 1.7 %collective-permute-start.31 = (f32[8,128]{1,0:T(8,128)S(1)}, f32[8,128]{1,0:T(8,128)S(1)}, u32[]{:S(2)}, u32[]{:S(2)}) collective-permute-start(f32[8,128]{1,0:T(8,128)S(1)} %max.3.a), channel_id=1, source_target_pairs={{0,6},{2,0},{4,2},{6,4},{1,7},{3,1},{5,3},{7,5},{8,14},{10,8},{12,... | collective-permute-start | bytes 12296 | tf_op jit(solution)/shard_map/ppermute | solution.py:57
  123.7 1.0 collective-permute-done.31.d
  124.7 0.6 shard_map.87
  (36 shorter events, 0.7 us)
Async XLA Ops:
  0.6 7.8 %copy-start.1 = (s32[6,1024]{1,0:T(8,128)S(1)}, s32[6,1024]{1,0:T(8,128)}, u32[]{:S(2)}) copy-start(s32[6,1024]{1,0:T(8,128)} %param.7) | copy-start | bytes 73732
  2.7 9.5 %collective-permute-start = (f32[232,128]{1,0:T(8,128)S(1)}, f32[232,128]{1,0:T(8,128)S(1)}, u32[]{:S(2)}, u32[]{:S(2)}) collective-permute-start(f32[232,128]{1,0:T(8,128)S(1)} %get-tuple-element.46.after_ref.a), channel_id=1, source_target_pairs={{0,8},{8,16},{16,24},{24,0},{1,9},{9,17},{17,25},{25,1},{2,10},{10... | collective-permute-start | bytes 356360 | tf_op jit(solution)/shard_map/ppermute | solution.py:57
  4.8 7.6 %collective-permute-start.1 = (f32[232,128]{1,0:T(8,128)S(1)}, f32[232,128]{1,0:T(8,128)S(1)}, u32[]{:S(2)}, u32[]{:S(2)}) collective-permute-start(f32[232,128]{1,0:T(8,128)S(1)} %get-tuple-element.46.after_ref.a), channel_id=1, source_target_pairs={{0,16},{8,24},{16,0},{24,8},{1,17},{9,25},{17,1},{25,9},{2,18},{10... | collective-permute-start | bytes 356360 | tf_op jit(solution)/shard_map/ppermute | solution.py:57
  7.3 5.2 %collective-permute-start.2 = (f32[232,128]{1,0:T(8,128)S(1)}, f32[232,128]{1,0:T(8,128)S(1)}, u32[]{:S(2)}, u32[]{:S(2)}) collective-permute-start(f32[232,128]{1,0:T(8,128)S(1)} %get-tuple-element.46.after_ref.a), channel_id=1, source_target_pairs={{0,24},{8,0},{16,8},{24,16},{1,25},{9,1},{17,9},{25,17},{2,26},{10... | collective-permute-start | bytes 356360 | tf_op jit(solution)/shard_map/ppermute | solution.py:57
  12.5 16.2 %copy-start = (bf16[1024,1024]{1,0:T(8,128)(2,1)S(1)}, bf16[1024,1024]{1,0:T(8,128)(2,1)}, u32[]{:S(2)}) copy-start(bf16[1024,1024]{1,0:T(8,128)(2,1)} %traits_ref.1) | copy-start | bytes 6291460
  12.5 7.6 %collective-permute-start.3 = (f32[232,128]{1,0:T(8,128)S(1)}, f32[232,128]{1,0:T(8,128)S(1)}, u32[]{:S(2)}, u32[]{:S(2)}) collective-permute-start(f32[232,128]{1,0:T(8,128)S(1)} %shard_map.61.after_ref.a), channel_id=1, source_target_pairs={{0,64},{64,128},{128,192},{192,0},{1,65},{65,129},{129,193},{193,1... | collective-permute-start | bytes 356360 | tf_op jit(solution)/shard_map/ppermute | solution.py:57
  13.9 6.7 %collective-permute-start.4 = (f32[232,128]{1,0:T(8,128)S(1)}, f32[232,128]{1,0:T(8,128)S(1)}, u32[]{:S(2)}, u32[]{:S(2)}) collective-permute-start(f32[232,128]{1,0:T(8,128)S(1)} %shard_map.61.after_ref.a), channel_id=1, source_target_pairs={{0,128},{64,192},{128,0},{192,64},{1,129},{65,193},{129,1},{193,65... | collective-permute-start | bytes 356360 | tf_op jit(solution)/shard_map/ppermute | solution.py:57
  16.5 4.7 %collective-permute-start.5 = (f32[232,128]{1,0:T(8,128)S(1)}, f32[232,128]{1,0:T(8,128)S(1)}, u32[]{:S(2)}, u32[]{:S(2)}) collective-permute-start(f32[232,128]{1,0:T(8,128)S(1)} %shard_map.61.after_ref.a), channel_id=1, source_target_pairs={{0,192},{64,0},{128,64},{192,128},{1,193},{65,1},{129,65},{193,129... | collective-permute-start | bytes 356360 | tf_op jit(solution)/shard_map/ppermute | solution.py:57
  21.3 9.7 %collective-permute-start.6 = (f32[232,128]{1,0:T(8,128)S(1)}, f32[232,128]{1,0:T(8,128)S(1)}, u32[]{:S(2)}, u32[]{:S(2)}) collective-permute-start(f32[232,128]{1,0:T(8,128)S(1)} %shard_map.63.own_ref.after_ref), channel_id=1, source_target_pairs={{0,32},{32,0},{1,33},{33,1},{2,34},{34,2},{3,35},{35,3},{4,36},{36... | collective-permute-start | bytes 356360 | tf_op jit(solution)/shard_map/ppermute | solution.py:57
  32.7 6.4 %collective-permute-start.7 = (f32[40,512]{1,0:T(8,128)S(1)}, f32[40,512]{1,0:T(8,128)S(1)}, u32[]{:S(2)}, u32[]{:S(2)}) collective-permute-start(f32[40,512]{1,0:T(8,128)S(1)} %slice.4), channel_id=1, source_target_pairs={{0,1},{1,0},{2,3},{3,2},{4,5},{5,4},{6,7},{7,6},{8,9},{9,8},{10,11... | collective-permute-start | bytes 245768 | tf_op jit(solution)/shard_map/ppermute | solution.py:57
  40.8 12.6 %collective-permute-start.12 = (f32[896,128]{1,0:T(8,128)S(1)}, f32[896,128]{1,0:T(8,128)S(1)}, u32[]{:S(2)}, u32[]{:S(2)}) collective-permute-start(f32[896,128]{1,0:T(8,128)S(1)} %get-tuple-element.59.after_ref), channel_id=1, source_target_pairs={{0,24},{8,0},{16,8},{24,16},{1,25},{9,1},{17,9},{25,17},{2,26},{10... | collective-permute-start | bytes 1376264 | tf_op jit(solution)/shard_map/ppermute | solution.py:57
  43.5 14.1 %collective-permute-start.9 = (f32[912,128]{1,0:T(8,128)S(1)}, f32[912,128]{1,0:T(8,128)S(1)}, u32[]{:S(2)}, u32[]{:S(2)}) collective-permute-start(f32[912,128]{1,0:T(8,128)S(1)} %get-tuple-element.68), channel_id=1, source_target_pairs={{0,8},{8,16},{16,24},{24,0},{1,9},{9,17},{17,25},{25,1},{2,10},{10... | collective-permute-start | bytes 1400840 | tf_op jit(solution)/shard_map/ppermute | solution.py:57
  44.3 13.5 %collective-permute-start.22 = (f32[896,128]{1,0:T(8,128)S(1)}, f32[896,128]{1,0:T(8,128)S(1)}, u32[]{:S(2)}, u32[]{:S(2)}) collective-permute-start(f32[896,128]{1,0:T(8,128)S(1)} %get-tuple-element.60.after_ref), channel_id=1, source_target_pairs={{0,192},{64,0},{128,64},{192,128},{1,193},{65,1},{129,65},{193,129... | collective-permute-start | bytes 1376264 | tf_op jit(solution)/shard_map/ppermute | solution.py:57
  46.8 12.7 %collective-permute-start.19 = (f32[896,128]{1,0:T(8,128)S(1)}, f32[896,128]{1,0:T(8,128)S(1)}, u32[]{:S(2)}, u32[]{:S(2)}) collective-permute-start(f32[896,128]{1,0:T(8,128)S(1)} %get-tuple-element.81), channel_id=1, source_target_pairs={{0,64},{64,128},{128,192},{192,0},{1,65},{65,129},{129,193},{193,1... | collective-permute-start | bytes 1376264 | tf_op jit(solution)/shard_map/ppermute | solution.py:57
  49.0 17.6 %collective-permute-start.11 = (f32[896,128]{1,0:T(8,128)S(1)}, f32[896,128]{1,0:T(8,128)S(1)}, u32[]{:S(2)}, u32[]{:S(2)}) collective-permute-start(f32[896,128]{1,0:T(8,128)S(1)} %get-tuple-element.63.after_ref), channel_id=1, source_target_pairs={{0,8},{8,16},{16,24},{24,0},{1,9},{9,17},{17,25},{25,1},{2,10},{10... | collective-permute-start | bytes 1376264 | tf_op jit(solution)/shard_map/ppermute | solution.py:57
  53.4 15.7 %collective-permute-start.8 = (f32[912,128]{1,0:T(8,128)S(1)}, f32[912,128]{1,0:T(8,128)S(1)}, u32[]{:S(2)}, u32[]{:S(2)}) collective-permute-start(f32[912,128]{1,0:T(8,128)S(1)} %get-tuple-element.66), channel_id=1, source_target_pairs={{0,24},{8,0},{16,8},{24,16},{1,25},{9,1},{17,9},{25,17},{2,26},{10... | collective-permute-start | bytes 1400840 | tf_op jit(solution)/shard_map/ppermute | solution.py:57
  57.6 18.2 %collective-permute-start.13 = (f32[896,128]{1,0:T(8,128)S(1)}, f32[896,128]{1,0:T(8,128)S(1)}, u32[]{:S(2)}, u32[]{:S(2)}) collective-permute-start(f32[896,128]{1,0:T(8,128)S(1)} %shard_map.78), channel_id=1, source_target_pairs={{0,24},{8,0},{16,8},{24,16},{1,25},{9,1},{17,9},{25,17},{2,26},{10... | collective-permute-start | bytes 1376264 | tf_op jit(solution)/shard_map/ppermute | solution.py:57
  57.8 18.8 %collective-permute-start.10 = (f32[912,128]{1,0:T(8,128)S(1)}, f32[912,128]{1,0:T(8,128)S(1)}, u32[]{:S(2)}, u32[]{:S(2)}) collective-permute-start(f32[912,128]{1,0:T(8,128)S(1)} %shard_map.77), channel_id=1, source_target_pairs={{0,8},{8,16},{16,24},{24,0},{1,9},{9,17},{17,25},{25,1},{2,10},{10... | collective-permute-start | bytes 1400840 | tf_op jit(solution)/shard_map/ppermute | solution.py:57
  59.5 17.9 %collective-permute-start.21 = (f32[896,128]{1,0:T(8,128)S(1)}, f32[896,128]{1,0:T(8,128)S(1)}, u32[]{:S(2)}, u32[]{:S(2)}) collective-permute-start(f32[896,128]{1,0:T(8,128)S(1)} %get-tuple-element.64.after_ref), channel_id=1, source_target_pairs={{0,64},{64,128},{128,192},{192,0},{1,65},{65,129},{129,193},{193,1... | collective-permute-start | bytes 1376264 | tf_op jit(solution)/shard_map/ppermute | solution.py:57
  66.5 13.9 %collective-permute-start.18 = (f32[896,128]{1,0:T(8,128)S(1)}, f32[896,128]{1,0:T(8,128)S(1)}, u32[]{:S(2)}, u32[]{:S(2)}) collective-permute-start(f32[896,128]{1,0:T(8,128)S(1)} %get-tuple-element.79), channel_id=1, source_target_pairs={{0,192},{64,0},{128,64},{192,128},{1,193},{65,1},{129,65},{193,129... | collective-permute-start | bytes 1376264 | tf_op jit(solution)/shard_map/ppermute | solution.py:57
  69.1 18.4 %collective-permute-start.23 = (f32[896,128]{1,0:T(8,128)S(1)}, f32[896,128]{1,0:T(8,128)S(1)}, u32[]{:S(2)}, u32[]{:S(2)}) collective-permute-start(f32[896,128]{1,0:T(8,128)S(1)} %shard_map.83), channel_id=1, source_target_pairs={{0,192},{64,0},{128,64},{192,128},{1,193},{65,1},{129,65},{193,129... | collective-permute-start | bytes 1376264 | tf_op jit(solution)/shard_map/ppermute | solution.py:57
  75.8 11.7 %collective-permute-start.20 = (f32[896,128]{1,0:T(8,128)S(1)}, f32[896,128]{1,0:T(8,128)S(1)}, u32[]{:S(2)}, u32[]{:S(2)}) collective-permute-start(f32[896,128]{1,0:T(8,128)S(1)} %shard_map.82), channel_id=1, source_target_pairs={{0,64},{64,128},{128,192},{192,0},{1,65},{65,129},{129,193},{193,1... | collective-permute-start | bytes 1376264 | tf_op jit(solution)/shard_map/ppermute | solution.py:57
  76.7 15.7 %collective-permute-start.14 = (f32[464,128]{1,0:T(8,128)S(1)}, f32[464,128]{1,0:T(8,128)S(1)}, u32[]{:S(2)}, u32[]{:S(2)}) collective-permute-start(f32[464,128]{1,0:T(8,128)S(1)} %get-tuple-element.72), channel_id=1, source_target_pairs={{0,64},{64,128},{128,192},{192,0},{1,65},{65,129},{129,193},{193,1... | collective-permute-start | bytes 712712 | tf_op jit(solution)/shard_map/ppermute | solution.py:57
  77.4 21.1 %collective-permute-start.15 = (f32[464,128]{1,0:T(8,128)S(1)}, f32[464,128]{1,0:T(8,128)S(1)}, u32[]{:S(2)}, u32[]{:S(2)}) collective-permute-start(f32[464,128]{1,0:T(8,128)S(1)} %get-tuple-element.73), channel_id=1, source_target_pairs={{0,128},{64,192},{128,0},{192,64},{1,129},{65,193},{129,1},{193,65... | collective-permute-start | bytes 712712 | tf_op jit(solution)/shard_map/ppermute | solution.py:57
  80.5 18.0 %collective-permute-start.16 = (f32[464,128]{1,0:T(8,128)S(1)}, f32[464,128]{1,0:T(8,128)S(1)}, u32[]{:S(2)}, u32[]{:S(2)}) collective-permute-start(f32[464,128]{1,0:T(8,128)S(1)} %get-tuple-element.74), channel_id=1, source_target_pairs={{0,192},{64,0},{128,64},{192,128},{1,193},{65,1},{129,65},{193,129... | collective-permute-start | bytes 712712 | tf_op jit(solution)/shard_map/ppermute | solution.py:57
  87.6 17.1 %collective-permute-start.24 = (f32[448,128]{1,0:T(8,128)S(1)}, f32[448,128]{1,0:T(8,128)S(1)}, u32[]{:S(2)}, u32[]{:S(2)}) collective-permute-start(f32[448,128]{1,0:T(8,128)S(1)} %get-tuple-element.83), channel_id=1, source_target_pairs={{0,8},{8,16},{16,24},{24,0},{1,9},{9,17},{17,25},{25,1},{2,10},{10... | collective-permute-start | bytes 688136 | tf_op jit(solution)/shard_map/ppermute | solution.py:57
  87.7 17.0 %collective-permute-start.25 = (f32[448,128]{1,0:T(8,128)S(1)}, f32[448,128]{1,0:T(8,128)S(1)}, u32[]{:S(2)}, u32[]{:S(2)}) collective-permute-start(f32[448,128]{1,0:T(8,128)S(1)} %get-tuple-element.84), channel_id=1, source_target_pairs={{0,16},{8,24},{16,0},{24,8},{1,17},{9,25},{17,1},{25,9},{2,18},{10... | collective-permute-start | bytes 688136 | tf_op jit(solution)/shard_map/ppermute | solution.py:57
  92.5 12.3 %collective-permute-start.26 = (f32[448,128]{1,0:T(8,128)S(1)}, f32[448,128]{1,0:T(8,128)S(1)}, u32[]{:S(2)}, u32[]{:S(2)}) collective-permute-start(f32[448,128]{1,0:T(8,128)S(1)} %get-tuple-element.85), channel_id=1, source_target_pairs={{0,24},{8,0},{16,8},{24,16},{1,25},{9,1},{17,9},{25,17},{2,26},{10... | collective-permute-start | bytes 688136 | tf_op jit(solution)/shard_map/ppermute | solution.py:57
  98.6 8.6 %collective-permute-start.17 = (f32[240,128]{1,0:T(8,128)S(1)}, f32[240,128]{1,0:T(8,128)S(1)}, u32[]{:S(2)}, u32[]{:S(2)}) collective-permute-start(f32[240,128]{1,0:T(8,128)S(1)} %get-tuple-element.76), channel_id=1, source_target_pairs={{0,32},{32,0},{1,33},{33,1},{2,34},{34,2},{3,35},{35,3},{4,36},{36... | collective-permute-start | bytes 368648 | tf_op jit(solution)/shard_map/ppermute | solution.py:57
  104.8 8.8 %collective-permute-start.27 = (f32[224,128]{1,0:T(8,128)S(1)}, f32[224,128]{1,0:T(8,128)S(1)}, u32[]{:S(2)}, u32[]{:S(2)}) collective-permute-start(f32[224,128]{1,0:T(8,128)S(1)} %get-tuple-element.87), channel_id=1, source_target_pairs={{0,32},{32,0},{1,33},{33,1},{2,34},{34,2},{3,35},{35,3},{4,36},{36... | collective-permute-start | bytes 344072 | tf_op jit(solution)/shard_map/ppermute | solution.py:57
  113.8 5.6 %collective-permute-start.28 = (f32[8,128]{1,0:T(8,128)S(1)}, f32[8,128]{1,0:T(8,128)S(1)}, u32[]{:S(2)}, u32[]{:S(2)}) collective-permute-start(f32[8,128]{1,0:T(8,128)S(1)} %shard_map.86), channel_id=1, source_target_pairs={{0,1},{1,0},{2,3},{3,2},{4,5},{5,4},{6,7},{7,6},{8,9},{9,8},{10,11... | collective-permute-start | bytes 12296 | tf_op jit(solution)/shard_map/ppermute | solution.py:57
  119.4 4.3 %collective-permute-start.29 = (f32[8,128]{1,0:T(8,128)S(1)}, f32[8,128]{1,0:T(8,128)S(1)}, u32[]{:S(2)}, u32[]{:S(2)}) collective-permute-start(f32[8,128]{1,0:T(8,128)S(1)} %max.3.a), channel_id=1, source_target_pairs={{0,2},{2,4},{4,6},{6,0},{1,3},{3,5},{5,7},{7,1},{8,10},{10,12},{12... | collective-permute-start | bytes 12296 | tf_op jit(solution)/shard_map/ppermute | solution.py:57
  119.7 4.0 %collective-permute-start.30 = (f32[8,128]{1,0:T(8,128)S(1)}, f32[8,128]{1,0:T(8,128)S(1)}, u32[]{:S(2)}, u32[]{:S(2)}) collective-permute-start(f32[8,128]{1,0:T(8,128)S(1)} %max.3.a), channel_id=1, source_target_pairs={{0,4},{2,6},{4,0},{6,2},{1,5},{3,7},{5,1},{7,3},{8,12},{10,14},{12... | collective-permute-start | bytes 12296 | tf_op jit(solution)/shard_map/ppermute | solution.py:57
  122.0 2.8 %collective-permute-start.31 = (f32[8,128]{1,0:T(8,128)S(1)}, f32[8,128]{1,0:T(8,128)S(1)}, u32[]{:S(2)}, u32[]{:S(2)}) collective-permute-start(f32[8,128]{1,0:T(8,128)S(1)} %max.3.a), channel_id=1, source_target_pairs={{0,6},{2,0},{4,2},{6,4},{1,7},{3,1},{5,3},{7,5},{8,14},{10,8},{12,... | collective-permute-start | bytes 12296 | tf_op jit(solution)/shard_map/ppermute | solution.py:57

commit v4 on v3

--- a/solution.py
+++ b/solution.py
@@ -60,12 +60,12 @@
 def front_kernel(core_ref, traits_hbm, cov_hbm, geno_hbm, pay_ref, xt_ref, dx_ref, traits, cov, geno, sems):
     half = pl.ds(pl.multiple_of(core_ref[0] * HALF, HALF), HALF)
     first = pltpu.make_async_copy(cov_hbm, cov, sems.at[0])
-    second = pltpu.make_async_copy(geno_hbm, geno, sems.at[1])
-    blocks = []
+    dosages, blocks = [], []
     for i in range(ROWS // STEP):
         rows = pl.ds(i * STEP, STEP)
-        blocks.append(pltpu.make_async_copy(traits_hbm.at[rows, half], traits.at[rows, :], sems.at[2 + i]))
-    for copy in (first, second, *blocks):
+        dosages.append(pltpu.make_async_copy(geno_hbm.at[rows, :], geno.at[rows, :], sems.at[1 + i]))
+        blocks.append(pltpu.make_async_copy(traits_hbm.at[rows, half], traits.at[rows, :], sems.at[1 + ROWS // STEP + i]))
+    for copy in (first, *dosages, *blocks):
         copy.start()
     first.wait()
     row = lax.broadcasted_iota(jnp.int32, (128 - C, ROWS), 0)
@@ -84,7 +84,8 @@
             ones = BLOCKS * C + C + 1 + at + j
             pay_ref[ones : ones + 1, :] = block[C : C + 1]
 
-    second.wait()
+    for copy in dosages:
+        copy.wait()
     dosage = geno[...].astype(F32).astype(BF16)
     dx_ref[:, :V] = dosage
     place(0, dot(xt, dosage))
@@ -334,7 +335,7 @@
                 pltpu.VMEM((ROWS, HALF), BF16),
                 pltpu.VMEM((C, ROWS), BF16),
                 pltpu.VMEM((ROWS, V), jnp.int32),
-                pltpu.SemaphoreType.DMA((2 + ROWS // STEP,)),
+                pltpu.SemaphoreType.DMA((1 + 2 * (ROWS // STEP),)),
             ],
         ),
         flops=2 * 128 * ROWS * COLS,

time: 126 us -> 126 us (level)
  no operation moved by 1% of the time
where the time goes in v4:
time: 126 us; the launch traced here: 125 us
  starting transfers between devices  63.3 us (50%)
  waiting for transfers between devices  38.1 us (30%)
  Pallas kernels  22.9 us (18%)
    ppermute x32, starting transfers between devices, shift(): return lax.ppermute(value, axis, shifts(axis, k))  63.3 us
    ppermute x32, waiting for transfers between devices, shift(): return lax.ppermute(value, axis, shifts(axis, k))  38.1 us
    pallas_call x29, Pallas kernels, call(): pl.pallas_call(kernel, out_shape=shapes[0] if single else shapes, cost_es...  22.9 us
  transfers between devices with their start and end apart: 32, of which 16 were waited for; matrix products, arithmetic and copies ran while one was open for 0% of the time, Pallas kernels for 13%

profile of v4, /device:TPU:1, one launch (start us, length us, event | category | flops | bytes accessed | tf_op | source)
XLA Modules:
  0.0 125.3 jit_solution(4923722938214995091)
XLA Ops:
  0.6 2.0 %shard_map.59 = (f32[232,128]{1,0:T(8,128)S(1)}, bf16[48,1024]{1,0:T(8,128)(2,1)S(1)}, bf16[1024,384]{1,0:T(8,128)(2,1)S(1)}) custom-call(s32[1]{0:T(128)} %bitcast.3.core_ref, bf16[1024,1024]{1,0:T(8,128)(2,1)} %traits_ref.1, bf16[32,1024]{1,0:T(8,128)(2,1)} %bitcast.10, s32[1024,256]{1,0:T(8,128)} %geno_hbm.1), custom_call_target="tpu_custom_call" | custom-call | flops 234881024 | bytes 1003520 | tf_op jit(solution)/shard_map/pallas_call | solution.py:41
  2.7 2.1 %collective-permute-start = (f32[232,128]{1,0:T(8,128)S(1)}, f32[232,128]{1,0:T(8,128)S(1)}, u32[]{:S(2)}, u32[]{:S(2)}) collective-permute-start(f32[232,128]{1,0:T(8,128)S(1)} %get-tuple-element.46.after_ref.a), channel_id=1, source_target_pairs={{0,8},{8,16},{16,24},{24,0},{1,9},{9,17},{17,25},{25,1},{2,10},{10... | collective-permute-start | bytes 356360 | tf_op jit(solution)/shard_map/ppermute | solution.py:57
  4.8 2.5 %collective-permute-start.1 = (f32[232,128]{1,0:T(8,128)S(1)}, f32[232,128]{1,0:T(8,128)S(1)}, u32[]{:S(2)}, u32[]{:S(2)}) collective-permute-start(f32[232,128]{1,0:T(8,128)S(1)} %get-tuple-element.46.after_ref.a), channel_id=1, source_target_pairs={{0,16},{8,24},{16,0},{24,8},{1,17},{9,25},{17,1},{25,9},{2,18},{10... | collective-permute-start | bytes 356360 | tf_op jit(solution)/shard_map/ppermute | solution.py:57
  7.3 1.2 collective-permute-start.2
  8.4 3.8 %shard_map.60 = (bf16[3,1024,384]{2,1,0:T(8,128)(2,1)S(1)}, f32[8,128]{1,0:T(8,128)S(1)}) custom-call(s32[1]{0:T(128)S(6)} %mul.13.base_ref, s32[6,1,1024]{2,1,0:T(1,128)S(1)} %reshape.42.order_ref, bf16[1024,384]{1,0:T(8,128)(2,1)S(1)} %get-tuple-element.47.dx_ref, f32[232,128]{1,0:T(8,128)S(1)} %get-tuple-element.46.after_ref.a), custom_call_target="tpu_custom_call" | custom-call | flops 2415919104 | bytes 2363392 | tf_op jit(solution)/shard_map/pallas_call | solution.py:41
  12.2 0.2 collective-permute-done.1.c
  12.5 1.4 %collective-permute-start.3 = (f32[232,128]{1,0:T(8,128)S(1)}, f32[232,128]{1,0:T(8,128)S(1)}, u32[]{:S(2)}, u32[]{:S(2)}) collective-permute-start(f32[232,128]{1,0:T(8,128)S(1)} %shard_map.61.after_ref.a), channel_id=1, source_target_pairs={{0,64},{64,128},{128,192},{192,0},{1,65},{65,129},{129,193},{193,1... | collective-permute-start | bytes 356360 | tf_op jit(solution)/shard_map/ppermute | solution.py:57
  13.9 2.6 %collective-permute-start.4 = (f32[232,128]{1,0:T(8,128)S(1)}, f32[232,128]{1,0:T(8,128)S(1)}, u32[]{:S(2)}, u32[]{:S(2)}) collective-permute-start(f32[232,128]{1,0:T(8,128)S(1)} %shard_map.61.after_ref.a), channel_id=1, source_target_pairs={{0,128},{64,192},{128,0},{192,64},{1,129},{65,193},{129,1},{193,65... | collective-permute-start | bytes 356360 | tf_op jit(solution)/shard_map/ppermute | solution.py:57
  16.5 1.1 collective-permute-start.5
  17.6 2.5 %shard_map.62 = (bf16[2,1024,384]{2,1,0:T(8,128)(2,1)S(1)}, f32[8,128]{1,0:T(8,128)S(1)}) custom-call(s32[1]{0:T(128)S(6)} %mul.13.base_ref, s32[6,1,1024]{2,1,0:T(1,128)S(1)} %reshape.42.order_ref, bf16[1024,384]{1,0:T(8,128)(2,1)S(1)} %get-tuple-element.47.dx_ref, f32[232,128]{1,0:T(8,128)S(1)} %shard_map.61.after_ref.a), custom_call_target="tpu_custom_call" | custom-call | flops 1610612736 | bytes 1576960 | tf_op jit(solution)/shard_map/pallas_call | solution.py:41
  20.1 0.4 collective-permute-done.4.c
  20.5 0.7 collective-permute-done.5.d
  21.3 7.4 %collective-permute-start.6 = (f32[232,128]{1,0:T(8,128)S(1)}, f32[232,128]{1,0:T(8,128)S(1)}, u32[]{:S(2)}, u32[]{:S(2)}) collective-permute-start(f32[232,128]{1,0:T(8,128)S(1)} %shard_map.63.own_ref.after_ref), channel_id=1, source_target_pairs={{0,32},{32,0},{1,33},{33,1},{2,34},{34,2},{3,35},{35,3},{4,36},{36... | collective-permute-start | bytes 356360 | tf_op jit(solution)/shard_map/ppermute | solution.py:57
  28.6 1.1 shard_map.65.yt_ref
  29.8 1.2 collective-permute-done.6.far_ref
  31.0 1.7 %shard_map.64.own_ref = f32[40,768]{1,0:T(8,128)S(1)} custom-call(f32[232,128]{1,0:T(8,128)S(1)} %shard_map.63.own_ref.after_ref, f32[232,128]{1,0:T(8,128)S(1)} %collective-permute-done.6.far_ref), custom_call_target="tpu_custom_call" | custom-call | flops 100000000 | bytes 122880 | tf_op jit(solution)/shard_map/pallas_call | solution.py:41
  32.7 3.5 %collective-permute-start.7 = (f32[40,512]{1,0:T(8,128)S(1)}, f32[40,512]{1,0:T(8,128)S(1)}, u32[]{:S(2)}, u32[]{:S(2)}) collective-permute-start(f32[40,512]{1,0:T(8,128)S(1)} %slice.4), channel_id=1, source_target_pairs={{0,1},{1,0},{2,3},{3,2},{4,5},{5,4},{6,7},{7,6},{8,9},{9,8},{10,11... | collective-permute-start | bytes 245768 | tf_op jit(solution)/shard_map/ppermute | solution.py:57
  36.2 1.8 %shard_map.66 = (bf16[1,1024,384]{2,1,0:T(8,128)(2,1)S(1)}, f32[8,128]{1,0:T(8,128)}) custom-call(s32[1]{0:T(128)S(6)} %mul.13.base_ref, s32[6,1,1024]{2,1,0:T(1,128)S(1)} %reshape.42.order_ref, bf16[1024,384]{1,0:T(8,128)(2,1)S(1)} %get-tuple-element.47.dx_ref, f32[232,128]{1,0:T(8,128)S(1)} %shard_map.63.own_ref.after_ref), custom_call_target="tpu_custom_call" | custom-call | flops 805306368 | bytes 790528 | tf_op jit(solution)/shard_map/pallas_call | solution.py:41
  38.0 1.1 shard_map.67
  39.1 1.0 shard_map.68
  40.1 0.7 shard_map.69
  40.8 2.7 %collective-permute-start.12 = (f32[896,128]{1,0:T(8,128)S(1)}, f32[896,128]{1,0:T(8,128)S(1)}, u32[]{:S(2)}, u32[]{:S(2)}) collective-permute-start(f32[896,128]{1,0:T(8,128)S(1)} %get-tuple-element.59.after_ref), channel_id=1, source_target_pairs={{0,24},{8,0},{16,8},{24,16},{1,25},{9,1},{17,9},{25,17},{2,26},{10... | collective-permute-start | bytes 1376264 | tf_op jit(solution)/shard_map/ppermute | solution.py:57
  43.5 0.7 shard_map.70
  44.2 2.5 %collective-permute-start.22 = (f32[896,128]{1,0:T(8,128)S(1)}, f32[896,128]{1,0:T(8,128)S(1)}, u32[]{:S(2)}, u32[]{:S(2)}) collective-permute-start(f32[896,128]{1,0:T(8,128)S(1)} %get-tuple-element.60.after_ref), channel_id=1, source_target_pairs={{0,192},{64,0},{128,64},{192,128},{1,193},{65,1},{129,65},{193,129... | collective-permute-start | bytes 1376264 | tf_op jit(solution)/shard_map/ppermute | solution.py:57
  46.8 0.7 shard_map.71
  47.5 0.7 shard_map.72
  48.2 0.7 shard_map.73
  48.9 0.1 collective-permute-start.11
  49.0 0.7 shard_map.74
  49.8 0.7 shard_map.75
  50.5 2.9 %collective-permute-done.12.b = f32[896,128]{1,0:T(8,128)S(1)} collective-permute-done((f32[896,128]{1,0:T(8,128)S(1)}, f32[896,128]{1,0:T(8,128)S(1)}, u32[]{:S(2)}, u32[]{:S(2)}) %collective-permute-start.12) | collective-permute-done | bytes 458784 | tf_op jit(solution)/shard_map/ppermute | solution.py:57
  53.4 3.4 %collective-permute-start.8 = (f32[912,128]{1,0:T(8,128)S(1)}, f32[912,128]{1,0:T(8,128)S(1)}, u32[]{:S(2)}, u32[]{:S(2)}) collective-permute-start(f32[912,128]{1,0:T(8,128)S(1)} %get-tuple-element.66), channel_id=1, source_target_pairs={{0,24},{8,0},{16,8},{24,16},{1,25},{9,1},{17,9},{25,17},{2,26},{10... | collective-permute-start | bytes 1400840 | tf_op jit(solution)/shard_map/ppermute | solution.py:57
  56.8 0.7 shard_map.76
  57.6 0.1 collective-permute-start.13
  57.7 1.5 %collective-permute-start.10 = (f32[912,128]{1,0:T(8,128)S(1)}, f32[912,128]{1,0:T(8,128)S(1)}, u32[]{:S(2)}, u32[]{:S(2)}) collective-permute-start(f32[912,128]{1,0:T(8,128)S(1)} %shard_map.77), channel_id=1, source_target_pairs={{0,8},{8,16},{16,24},{24,0},{1,9},{9,17},{17,25},{25,1},{2,10},{10... | collective-permute-start | bytes 1400840 | tf_op jit(solution)/shard_map/ppermute | solution.py:57
  59.3 0.2 collective-permute-done.19.b
  59.5 7.0 %collective-permute-done.11.high_near = f32[896,128]{1,0:T(8,128)S(1)} collective-permute-done((f32[896,128]{1,0:T(8,128)S(1)}, f32[896,128]{1,0:T(8,128)S(1)}, u32[]{:S(2)}, u32[]{:S(2)}) %collective-permute-start.11) | collective-permute-done | bytes 458784 | tf_op jit(solution)/shard_map/ppermute | solution.py:57
  66.5 2.5 %collective-permute-start.18 = (f32[896,128]{1,0:T(8,128)S(1)}, f32[896,128]{1,0:T(8,128)S(1)}, u32[]{:S(2)}, u32[]{:S(2)}) collective-permute-start(f32[896,128]{1,0:T(8,128)S(1)} %get-tuple-element.79), channel_id=1, source_target_pairs={{0,192},{64,0},{128,64},{192,128},{1,193},{65,1},{129,65},{193,129... | collective-permute-start | bytes 1376264 | tf_op jit(solution)/shard_map/ppermute | solution.py:57
  69.2 6.6 %collective-permute-done.13.high_far = f32[896,128]{1,0:T(8,128)S(1)} collective-permute-done((f32[896,128]{1,0:T(8,128)S(1)}, f32[896,128]{1,0:T(8,128)S(1)}, u32[]{:S(2)}, u32[]{:S(2)}) %collective-permute-start.13) | collective-permute-done | bytes 458784 | tf_op jit(solution)/shard_map/ppermute | solution.py:57
  75.8 0.3 collective-permute-start.20
  76.1 0.5 collective-permute-done.10.low_far
  76.5 0.2 shard_map.79
  76.7 0.7 collective-permute-start.14
  77.4 3.1 %collective-permute-start.15 = (f32[464,128]{1,0:T(8,128)S(1)}, f32[464,128]{1,0:T(8,128)S(1)}, u32[]{:S(2)}, u32[]{:S(2)}) collective-permute-start(f32[464,128]{1,0:T(8,128)S(1)} %get-tuple-element.73), channel_id=1, source_target_pairs={{0,128},{64,192},{128,0},{192,64},{1,129},{65,193},{129,1},{193,65... | collective-permute-start | bytes 712712 | tf_op jit(solution)/shard_map/ppermute | solution.py:57
  80.5 1.4 %collective-permute-start.16 = (f32[464,128]{1,0:T(8,128)S(1)}, f32[464,128]{1,0:T(8,128)S(1)}, u32[]{:S(2)}, u32[]{:S(2)}) collective-permute-start(f32[464,128]{1,0:T(8,128)S(1)} %get-tuple-element.74), channel_id=1, source_target_pairs={{0,192},{64,0},{128,64},{192,128},{1,193},{65,1},{129,65},{193,129... | collective-permute-start | bytes 712712 | tf_op jit(solution)/shard_map/ppermute | solution.py:57
  81.8 5.8 %collective-permute-done.23.high_far = f32[896,128]{1,0:T(8,128)S(1)} collective-permute-done((f32[896,128]{1,0:T(8,128)S(1)}, f32[896,128]{1,0:T(8,128)S(1)}, u32[]{:S(2)}, u32[]{:S(2)}) %collective-permute-start.23) | collective-permute-done | bytes 458784 | tf_op jit(solution)/shard_map/ppermute | solution.py:57
  87.6 0.1 shard_map.84
  87.8 4.3 %collective-permute-start.25 = (f32[448,128]{1,0:T(8,128)S(1)}, f32[448,128]{1,0:T(8,128)S(1)}, u32[]{:S(2)}, u32[]{:S(2)}) collective-permute-start(f32[448,128]{1,0:T(8,128)S(1)} %get-tuple-element.84), channel_id=1, source_target_pairs={{0,16},{8,24},{16,0},{24,8},{1,17},{9,25},{17,1},{25,9},{2,18},{10... | collective-permute-start | bytes 688136 | tf_op jit(solution)/shard_map/ppermute | solution.py:57
  92.1 0.3 collective-permute-done.14.b
  92.4 3.4 %collective-permute-start.26 = (f32[448,128]{1,0:T(8,128)S(1)}, f32[448,128]{1,0:T(8,128)S(1)}, u32[]{:S(2)}, u32[]{:S(2)}) collective-permute-start(f32[448,128]{1,0:T(8,128)S(1)} %get-tuple-element.85), channel_id=1, source_target_pairs={{0,24},{8,0},{16,8},{24,16},{1,25},{9,1},{17,9},{25,17},{2,26},{10... | collective-permute-start | bytes 688136 | tf_op jit(solution)/shard_map/ppermute | solution.py:57
  95.8 2.7 %collective-permute-done.15.c = f32[464,128]{1,0:T(8,128)S(1)} collective-permute-done((f32[464,128]{1,0:T(8,128)S(1)}, f32[464,128]{1,0:T(8,128)S(1)}, u32[]{:S(2)}, u32[]{:S(2)}) %collective-permute-start.15) | collective-permute-done | bytes 237600 | tf_op jit(solution)/shard_map/ppermute | solution.py:57
  98.6 6.1 %collective-permute-start.17 = (f32[240,128]{1,0:T(8,128)S(1)}, f32[240,128]{1,0:T(8,128)S(1)}, u32[]{:S(2)}, u32[]{:S(2)}) collective-permute-start(f32[240,128]{1,0:T(8,128)S(1)} %get-tuple-element.76), channel_id=1, source_target_pairs={{0,32},{32,0},{1,33},{33,1},{2,34},{34,2},{3,35},{35,3},{4,36},{36... | collective-permute-start | bytes 368648 | tf_op jit(solution)/shard_map/ppermute | solution.py:57
  104.8 0.2 collective-permute-start.27
  105.1 2.0 %collective-permute-done.17.got = f32[240,128]{1,0:T(8,128)S(1)} collective-permute-done((f32[240,128]{1,0:T(8,128)S(1)}, f32[240,128]{1,0:T(8,128)S(1)}, u32[]{:S(2)}, u32[]{:S(2)}) %collective-permute-start.17) | collective-permute-done | bytes 122912 | tf_op jit(solution)/shard_map/ppermute | solution.py:57
  107.1 0.7 shard_map.81
  107.8 5.7 %collective-permute-done.27.got = f32[224,128]{1,0:T(8,128)S(1)} collective-permute-done((f32[224,128]{1,0:T(8,128)S(1)}, f32[224,128]{1,0:T(8,128)S(1)}, u32[]{:S(2)}, u32[]{:S(2)}) %collective-permute-start.27) | collective-permute-done | bytes 114720 | tf_op jit(solution)/shard_map/ppermute | solution.py:57
  113.6 0.2 shard_map.86
  113.7 4.8 %collective-permute-start.28 = (f32[8,128]{1,0:T(8,128)S(1)}, f32[8,128]{1,0:T(8,128)S(1)}, u32[]{:S(2)}, u32[]{:S(2)}) collective-permute-start(f32[8,128]{1,0:T(8,128)S(1)} %shard_map.86), channel_id=1, source_target_pairs={{0,1},{1,0},{2,3},{3,2},{4,5},{5,4},{6,7},{7,6},{8,9},{9,8},{10,11... | collective-permute-start | bytes 12296 | tf_op jit(solution)/shard_map/ppermute | solution.py:57
  118.5 0.8 collective-permute-done.28
  119.4 0.3 collective-permute-start.29
  119.7 2.3 %collective-permute-start.30 = (f32[8,128]{1,0:T(8,128)S(1)}, f32[8,128]{1,0:T(8,128)S(1)}, u32[]{:S(2)}, u32[]{:S(2)}) collective-permute-start(f32[8,128]{1,0:T(8,128)S(1)} %max.3.a), channel_id=1, source_target_pairs={{0,4},{2,6},{4,0},{6,2},{1,5},{3,7},{5,1},{7,3},{8,12},{10,14},{12... | collective-permute-start | bytes 12296 | tf_op jit(solution)/shard_map/ppermute | solution.py:57
  122.0 1.7 %collective-permute-start.31 = (f32[8,128]{1,0:T(8,128)S(1)}, f32[8,128]{1,0:T(8,128)S(1)}, u32[]{:S(2)}, u32[]{:S(2)}) collective-permute-start(f32[8,128]{1,0:T(8,128)S(1)} %max.3.a), channel_id=1, source_target_pairs={{0,6},{2,0},{4,2},{6,4},{1,7},{3,1},{5,3},{7,5},{8,14},{10,8},{12,... | collective-permute-start | bytes 12296 | tf_op jit(solution)/shard_map/ppermute | solution.py:57
  123.7 1.0 collective-permute-done.31.d
  124.7 0.6 shard_map.87
  (36 shorter events, 0.7 us)
Async XLA Ops:
  0.6 7.8 %copy-start.1 = (s32[6,1024]{1,0:T(8,128)S(1)}, s32[6,1024]{1,0:T(8,128)}, u32[]{:S(2)}) copy-start(s32[6,1024]{1,0:T(8,128)} %param.7) | copy-start | bytes 73732
  2.7 9.5 %collective-permute-start = (f32[232,128]{1,0:T(8,128)S(1)}, f32[232,128]{1,0:T(8,128)S(1)}, u32[]{:S(2)}, u32[]{:S(2)}) collective-permute-start(f32[232,128]{1,0:T(8,128)S(1)} %get-tuple-element.46.after_ref.a), channel_id=1, source_target_pairs={{0,8},{8,16},{16,24},{24,0},{1,9},{9,17},{17,25},{25,1},{2,10},{10... | collective-permute-start | bytes 356360 | tf_op jit(solution)/shard_map/ppermute | solution.py:57
  4.8 7.6 %collective-permute-start.1 = (f32[232,128]{1,0:T(8,128)S(1)}, f32[232,128]{1,0:T(8,128)S(1)}, u32[]{:S(2)}, u32[]{:S(2)}) collective-permute-start(f32[232,128]{1,0:T(8,128)S(1)} %get-tuple-element.46.after_ref.a), channel_id=1, source_target_pairs={{0,16},{8,24},{16,0},{24,8},{1,17},{9,25},{17,1},{25,9},{2,18},{10... | collective-permute-start | bytes 356360 | tf_op jit(solution)/shard_map/ppermute | solution.py:57
  7.3 5.2 %collective-permute-start.2 = (f32[232,128]{1,0:T(8,128)S(1)}, f32[232,128]{1,0:T(8,128)S(1)}, u32[]{:S(2)}, u32[]{:S(2)}) collective-permute-start(f32[232,128]{1,0:T(8,128)S(1)} %get-tuple-element.46.after_ref.a), channel_id=1, source_target_pairs={{0,24},{8,0},{16,8},{24,16},{1,25},{9,1},{17,9},{25,17},{2,26},{10... | collective-permute-start | bytes 356360 | tf_op jit(solution)/shard_map/ppermute | solution.py:57
  12.5 16.2 %copy-start = (bf16[1024,1024]{1,0:T(8,128)(2,1)S(1)}, bf16[1024,1024]{1,0:T(8,128)(2,1)}, u32[]{:S(2)}) copy-start(bf16[1024,1024]{1,0:T(8,128)(2,1)} %traits_ref.1) | copy-start | bytes 6291460
  12.5 7.6 %collective-permute-start.3 = (f32[232,128]{1,0:T(8,128)S(1)}, f32[232,128]{1,0:T(8,128)S(1)}, u32[]{:S(2)}, u32[]{:S(2)}) collective-permute-start(f32[232,128]{1,0:T(8,128)S(1)} %shard_map.61.after_ref.a), channel_id=1, source_target_pairs={{0,64},{64,128},{128,192},{192,0},{1,65},{65,129},{129,193},{193,1... | collective-permute-start | bytes 356360 | tf_op jit(solution)/shard_map/ppermute | solution.py:57
  13.9 6.7 %collective-permute-start.4 = (f32[232,128]{1,0:T(8,128)S(1)}, f32[232,128]{1,0:T(8,128)S(1)}, u32[]{:S(2)}, u32[]{:S(2)}) collective-permute-start(f32[232,128]{1,0:T(8,128)S(1)} %shard_map.61.after_ref.a), channel_id=1, source_target_pairs={{0,128},{64,192},{128,0},{192,64},{1,129},{65,193},{129,1},{193,65... | collective-permute-start | bytes 356360 | tf_op jit(solution)/shard_map/ppermute | solution.py:57
  16.5 4.7 %collective-permute-start.5 = (f32[232,128]{1,0:T(8,128)S(1)}, f32[232,128]{1,0:T(8,128)S(1)}, u32[]{:S(2)}, u32[]{:S(2)}) collective-permute-start(f32[232,128]{1,0:T(8,128)S(1)} %shard_map.61.after_ref.a), channel_id=1, source_target_pairs={{0,192},{64,0},{128,64},{192,128},{1,193},{65,1},{129,65},{193,129... | collective-permute-start | bytes 356360 | tf_op jit(solution)/shard_map/ppermute | solution.py:57
  21.3 9.7 %collective-permute-start.6 = (f32[232,128]{1,0:T(8,128)S(1)}, f32[232,128]{1,0:T(8,128)S(1)}, u32[]{:S(2)}, u32[]{:S(2)}) collective-permute-start(f32[232,128]{1,0:T(8,128)S(1)} %shard_map.63.own_ref.after_ref), channel_id=1, source_target_pairs={{0,32},{32,0},{1,33},{33,1},{2,34},{34,2},{3,35},{35,3},{4,36},{36... | collective-permute-start | bytes 356360 | tf_op jit(solution)/shard_map/ppermute | solution.py:57
  32.7 6.4 %collective-permute-start.7 = (f32[40,512]{1,0:T(8,128)S(1)}, f32[40,512]{1,0:T(8,128)S(1)}, u32[]{:S(2)}, u32[]{:S(2)}) collective-permute-start(f32[40,512]{1,0:T(8,128)S(1)} %slice.4), channel_id=1, source_target_pairs={{0,1},{1,0},{2,3},{3,2},{4,5},{5,4},{6,7},{7,6},{8,9},{9,8},{10,11... | collective-permute-start | bytes 245768 | tf_op jit(solution)/shard_map/ppermute | solution.py:57
  40.8 12.6 %collective-permute-start.12 = (f32[896,128]{1,0:T(8,128)S(1)}, f32[896,128]{1,0:T(8,128)S(1)}, u32[]{:S(2)}, u32[]{:S(2)}) collective-permute-start(f32[896,128]{1,0:T(8,128)S(1)} %get-tuple-element.59.after_ref), channel_id=1, source_target_pairs={{0,24},{8,0},{16,8},{24,16},{1,25},{9,1},{17,9},{25,17},{2,26},{10... | collective-permute-start | bytes 1376264 | tf_op jit(solution)/shard_map/ppermute | solution.py:57
  43.5 14.1 %collective-permute-start.9 = (f32[912,128]{1,0:T(8,128)S(1)}, f32[912,128]{1,0:T(8,128)S(1)}, u32[]{:S(2)}, u32[]{:S(2)}) collective-permute-start(f32[912,128]{1,0:T(8,128)S(1)} %get-tuple-element.68), channel_id=1, source_target_pairs={{0,8},{8,16},{16,24},{24,0},{1,9},{9,17},{17,25},{25,1},{2,10},{10... | collective-permute-start | bytes 1400840 | tf_op jit(solution)/shard_map/ppermute | solution.py:57
  44.2 13.5 %collective-permute-start.22 = (f32[896,128]{1,0:T(8,128)S(1)}, f32[896,128]{1,0:T(8,128)S(1)}, u32[]{:S(2)}, u32[]{:S(2)}) collective-permute-start(f32[896,128]{1,0:T(8,128)S(1)} %get-tuple-element.60.after_ref), channel_id=1, source_target_pairs={{0,192},{64,0},{128,64},{192,128},{1,193},{65,1},{129,65},{193,129... | collective-permute-start | bytes 1376264 | tf_op jit(solution)/shard_map/ppermute | solution.py:57
  46.8 12.7 %collective-permute-start.19 = (f32[896,128]{1,0:T(8,128)S(1)}, f32[896,128]{1,0:T(8,128)S(1)}, u32[]{:S(2)}, u32[]{:S(2)}) collective-permute-start(f32[896,128]{1,0:T(8,128)S(1)} %get-tuple-element.81), channel_id=1, source_target_pairs={{0,64},{64,128},{128,192},{192,0},{1,65},{65,129},{129,193},{193,1... | collective-permute-start | bytes 1376264 | tf_op jit(solution)/shard_map/ppermute | solution.py:57
  48.9 17.6 %collective-permute-start.11 = (f32[896,128]{1,0:T(8,128)S(1)}, f32[896,128]{1,0:T(8,128)S(1)}, u32[]{:S(2)}, u32[]{:S(2)}) collective-permute-start(f32[896,128]{1,0:T(8,128)S(1)} %get-tuple-element.63.after_ref), channel_id=1, source_target_pairs={{0,8},{8,16},{16,24},{24,0},{1,9},{9,17},{17,25},{25,1},{2,10},{10... | collective-permute-start | bytes 1376264 | tf_op jit(solution)/shard_map/ppermute | solution.py:57
  53.4 15.7 %collective-permute-start.8 = (f32[912,128]{1,0:T(8,128)S(1)}, f32[912,128]{1,0:T(8,128)S(1)}, u32[]{:S(2)}, u32[]{:S(2)}) collective-permute-start(f32[912,128]{1,0:T(8,128)S(1)} %get-tuple-element.66), channel_id=1, source_target_pairs={{0,24},{8,0},{16,8},{24,16},{1,25},{9,1},{17,9},{25,17},{2,26},{10... | collective-permute-start | bytes 1400840 | tf_op jit(solution)/shard_map/ppermute | solution.py:57
  57.6 18.2 %collective-permute-start.13 = (f32[896,128]{1,0:T(8,128)S(1)}, f32[896,128]{1,0:T(8,128)S(1)}, u32[]{:S(2)}, u32[]{:S(2)}) collective-permute-start(f32[896,128]{1,0:T(8,128)S(1)} %shard_map.78), channel_id=1, source_target_pairs={{0,24},{8,0},{16,8},{24,16},{1,25},{9,1},{17,9},{25,17},{2,26},{10... | collective-permute-start | bytes 1376264 | tf_op jit(solution)/shard_map/ppermute | solution.py:57
  57.7 18.8 %collective-permute-start.10 = (f32[912,128]{1,0:T(8,128)S(1)}, f32[912,128]{1,0:T(8,128)S(1)}, u32[]{:S(2)}, u32[]{:S(2)}) collective-permute-start(f32[912,128]{1,0:T(8,128)S(1)} %shard_map.77), channel_id=1, source_target_pairs={{0,8},{8,16},{16,24},{24,0},{1,9},{9,17},{17,25},{25,1},{2,10},{10... | collective-permute-start | bytes 1400840 | tf_op jit(solution)/shard_map/ppermute | solution.py:57
  59.5 17.9 %collective-permute-start.21 = (f32[896,128]{1,0:T(8,128)S(1)}, f32[896,128]{1,0:T(8,128)S(1)}, u32[]{:S(2)}, u32[]{:S(2)}) collective-permute-start(f32[896,128]{1,0:T(8,128)S(1)} %get-tuple-element.64.after_ref), channel_id=1, source_target_pairs={{0,64},{64,128},{128,192},{192,0},{1,65},{65,129},{129,193},{193,1... | collective-permute-start | bytes 1376264 | tf_op jit(solution)/shard_map/ppermute | solution.py:57
  66.5 13.9 %collective-permute-start.18 = (f32[896,128]{1,0:T(8,128)S(1)}, f32[896,128]{1,0:T(8,128)S(1)}, u32[]{:S(2)}, u32[]{:S(2)}) collective-permute-start(f32[896,128]{1,0:T(8,128)S(1)} %get-tuple-element.79), channel_id=1, source_target_pairs={{0,192},{64,0},{128,64},{192,128},{1,193},{65,1},{129,65},{193,129... | collective-permute-start | bytes 1376264 | tf_op jit(solution)/shard_map/ppermute | solution.py:57
  69.1 18.5 %collective-permute-start.23 = (f32[896,128]{1,0:T(8,128)S(1)}, f32[896,128]{1,0:T(8,128)S(1)}, u32[]{:S(2)}, u32[]{:S(2)}) collective-permute-start(f32[896,128]{1,0:T(8,128)S(1)} %shard_map.83), channel_id=1, source_target_pairs={{0,192},{64,0},{128,64},{192,128},{1,193},{65,1},{129,65},{193,129... | collective-permute-start | bytes 1376264 | tf_op jit(solution)/shard_map/ppermute | solution.py:57
  75.8 11.8 %collective-permute-start.20 = (f32[896,128]{1,0:T(8,128)S(1)}, f32[896,128]{1,0:T(8,128)S(1)}, u32[]{:S(2)}, u32[]{:S(2)}) collective-permute-start(f32[896,128]{1,0:T(8,128)S(1)} %shard_map.82), channel_id=1, source_target_pairs={{0,64},{64,128},{128,192},{192,0},{1,65},{65,129},{129,193},{193,1... | collective-permute-start | bytes 1376264 | tf_op jit(solution)/shard_map/ppermute | solution.py:57
  76.7 15.7 %collective-permute-start.14 = (f32[464,128]{1,0:T(8,128)S(1)}, f32[464,128]{1,0:T(8,128)S(1)}, u32[]{:S(2)}, u32[]{:S(2)}) collective-permute-start(f32[464,128]{1,0:T(8,128)S(1)} %get-tuple-element.72), channel_id=1, source_target_pairs={{0,64},{64,128},{128,192},{192,0},{1,65},{65,129},{129,193},{193,1... | collective-permute-start | bytes 712712 | tf_op jit(solution)/shard_map/ppermute | solution.py:57
  77.4 21.1 %collective-permute-start.15 = (f32[464,128]{1,0:T(8,128)S(1)}, f32[464,128]{1,0:T(8,128)S(1)}, u32[]{:S(2)}, u32[]{:S(2)}) collective-permute-start(f32[464,128]{1,0:T(8,128)S(1)} %get-tuple-element.73), channel_id=1, source_target_pairs={{0,128},{64,192},{128,0},{192,64},{1,129},{65,193},{129,1},{193,65... | collective-permute-start | bytes 712712 | tf_op jit(solution)/shard_map/ppermute | solution.py:57
  80.5 18.1 %collective-permute-start.16 = (f32[464,128]{1,0:T(8,128)S(1)}, f32[464,128]{1,0:T(8,128)S(1)}, u32[]{:S(2)}, u32[]{:S(2)}) collective-permute-start(f32[464,128]{1,0:T(8,128)S(1)} %get-tuple-element.74), channel_id=1, source_target_pairs={{0,192},{64,0},{128,64},{192,128},{1,193},{65,1},{129,65},{193,129... | collective-permute-start | bytes 712712 | tf_op jit(solution)/shard_map/ppermute | solution.py:57
  87.7 17.0 %collective-permute-start.24 = (f32[448,128]{1,0:T(8,128)S(1)}, f32[448,128]{1,0:T(8,128)S(1)}, u32[]{:S(2)}, u32[]{:S(2)}) collective-permute-start(f32[448,128]{1,0:T(8,128)S(1)} %get-tuple-element.83), channel_id=1, source_target_pairs={{0,8},{8,16},{16,24},{24,0},{1,9},{9,17},{17,25},{25,1},{2,10},{10... | collective-permute-start | bytes 688136 | tf_op jit(solution)/shard_map/ppermute | solution.py:57
  87.8 16.9 %collective-permute-start.25 = (f32[448,128]{1,0:T(8,128)S(1)}, f32[448,128]{1,0:T(8,128)S(1)}, u32[]{:S(2)}, u32[]{:S(2)}) collective-permute-start(f32[448,128]{1,0:T(8,128)S(1)} %get-tuple-element.84), channel_id=1, source_target_pairs={{0,16},{8,24},{16,0},{24,8},{1,17},{9,25},{17,1},{25,9},{2,18},{10... | collective-permute-start | bytes 688136 | tf_op jit(solution)/shard_map/ppermute | solution.py:57
  92.4 12.3 %collective-permute-start.26 = (f32[448,128]{1,0:T(8,128)S(1)}, f32[448,128]{1,0:T(8,128)S(1)}, u32[]{:S(2)}, u32[]{:S(2)}) collective-permute-start(f32[448,128]{1,0:T(8,128)S(1)} %get-tuple-element.85), channel_id=1, source_target_pairs={{0,24},{8,0},{16,8},{24,16},{1,25},{9,1},{17,9},{25,17},{2,26},{10... | collective-permute-start | bytes 688136 | tf_op jit(solution)/shard_map/ppermute | solution.py:57
  98.6 8.5 %collective-permute-start.17 = (f32[240,128]{1,0:T(8,128)S(1)}, f32[240,128]{1,0:T(8,128)S(1)}, u32[]{:S(2)}, u32[]{:S(2)}) collective-permute-start(f32[240,128]{1,0:T(8,128)S(1)} %get-tuple-element.76), channel_id=1, source_target_pairs={{0,32},{32,0},{1,33},{33,1},{2,34},{34,2},{3,35},{35,3},{4,36},{36... | collective-permute-start | bytes 368648 | tf_op jit(solution)/shard_map/ppermute | solution.py:57
  104.8 8.8 %collective-permute-start.27 = (f32[224,128]{1,0:T(8,128)S(1)}, f32[224,128]{1,0:T(8,128)S(1)}, u32[]{:S(2)}, u32[]{:S(2)}) collective-permute-start(f32[224,128]{1,0:T(8,128)S(1)} %get-tuple-element.87), channel_id=1, source_target_pairs={{0,32},{32,0},{1,33},{33,1},{2,34},{34,2},{3,35},{35,3},{4,36},{36... | collective-permute-start | bytes 344072 | tf_op jit(solution)/shard_map/ppermute | solution.py:57
  113.7 5.6 %collective-permute-start.28 = (f32[8,128]{1,0:T(8,128)S(1)}, f32[8,128]{1,0:T(8,128)S(1)}, u32[]{:S(2)}, u32[]{:S(2)}) collective-permute-start(f32[8,128]{1,0:T(8,128)S(1)} %shard_map.86), channel_id=1, source_target_pairs={{0,1},{1,0},{2,3},{3,2},{4,5},{5,4},{6,7},{7,6},{8,9},{9,8},{10,11... | collective-permute-start | bytes 12296 | tf_op jit(solution)/shard_map/ppermute | solution.py:57
  119.4 4.3 %collective-permute-start.29 = (f32[8,128]{1,0:T(8,128)S(1)}, f32[8,128]{1,0:T(8,128)S(1)}, u32[]{:S(2)}, u32[]{:S(2)}) collective-permute-start(f32[8,128]{1,0:T(8,128)S(1)} %max.3.a), channel_id=1, source_target_pairs={{0,2},{2,4},{4,6},{6,0},{1,3},{3,5},{5,7},{7,1},{8,10},{10,12},{12... | collective-permute-start | bytes 12296 | tf_op jit(solution)/shard_map/ppermute | solution.py:57
  119.7 4.0 %collective-permute-start.30 = (f32[8,128]{1,0:T(8,128)S(1)}, f32[8,128]{1,0:T(8,128)S(1)}, u32[]{:S(2)}, u32[]{:S(2)}) collective-permute-start(f32[8,128]{1,0:T(8,128)S(1)} %max.3.a), channel_id=1, source_target_pairs={{0,4},{2,6},{4,0},{6,2},{1,5},{3,7},{5,1},{7,3},{8,12},{10,14},{12... | collective-permute-start | bytes 12296 | tf_op jit(solution)/shard_map/ppermute | solution.py:57
  122.0 2.7 %collective-permute-start.31 = (f32[8,128]{1,0:T(8,128)S(1)}, f32[8,128]{1,0:T(8,128)S(1)}, u32[]{:S(2)}, u32[]{:S(2)}) collective-permute-start(f32[8,128]{1,0:T(8,128)S(1)} %max.3.a), channel_id=1, source_target_pairs={{0,6},{2,0},{4,2},{6,4},{1,7},{3,1},{5,3},{7,5},{8,14},{10,8},{12,... | collective-permute-start | bytes 12296 | tf_op jit(solution)/shard_map/ppermute | solution.py:57
